TPU v7x, 32 devices: a whole 2x2x4 slice. The times are simulated.
32 devices in a mesh: heads: 2 (over x), seq: 16 (over z, y, core).
Axes of the slice: x: 2, y: 2, z: 4, core: 2. Of those that a mesh axis runs over, the one named last changes fastest.
Arguments:
- q_nope: bfloat16 [1152, 64, 128], P('seq', 'heads'), may hold values from -6 to 6
- q_rope: bfloat16 [1152, 64, 64], P('seq', 'heads'), may hold values from -125 to 125
- latent: bfloat16 [1152, 512], P('seq'), may hold values from -6 to 6
- key_rope: bfloat16 [1152, 64], P('seq'), may hold values from -5 to 5
- absorb_key: bfloat16 [64, 128, 512], P('heads'), may hold values from -0.5 to 0.5
- absorb_value: bfloat16 [64, 512, 128], P('heads'), may hold values from -0.25 to 0.25
- w_out: bfloat16 [8192, 3584], P('heads', 'seq'), may hold values from -0.125 to 0.125
- residual: bfloat16 [1152, 3584], P(('seq', 'heads')), may hold values from -2 to 2
- norm_gain: float32 [3584], replicated, may hold values from 0.25 to 1.75
- span_table: int32 [32], replicated, may hold values from 0 to 31, each once
Outputs:
- new_residual: bfloat16 [1152, 3584], P(('seq', 'heads'))
- normed: bfloat16 [1152, 3584], P(('seq', 'heads'))
Inputs may be any that keep to these rules, and one draw needn't show every extreme that they name: `span_table`: A permutation of the span numbers.
All inputs are finite; a program needn't handle non-finite values.
Results may differ from a plain program's by a relative error of at most 0.014.
Values may be sent and summed in bfloat16 or wider, within the bound.
No kernel may reach another device: no remote copies, remote signals or barrier semaphores. Data moves between devices by JAX's collectives and lax.ppermute only.
A program may use at most 128 MiB of HBM per device.

v0:
```python
import functools

import jax
import jax.numpy as jnp
from jax import lax
from jax.experimental import pallas as pl
from jax.experimental.pallas import tpu as pltpu
from jax.sharding import PartitionSpec as P

score_scale = 192.0 ** (-0.5)
LOG2E = 1.4426950408889634


def pack_kernel(lat_ref, rope_ref, out_ref):
    width = lat_ref.shape[1]
    out_ref[:, :width] = lat_ref[...]
    rope = rope_ref[...].astype(jnp.float32).T
    both = jnp.concatenate([rope, rope], axis=1)
    out_ref[:, width:] = both.astype(out_ref.dtype)


def pack(latent, rope_t):
    return pl.pallas_call(
        pack_kernel,
        out_shape=jax.ShapeDtypeStruct(
            (latent.shape[0], latent.shape[1] + 2 * rope_t.shape[0]), latent.dtype
        ),
        compiler_params=pltpu.CompilerParams(vmem_limit_bytes=8 * 1024 * 1024),
        name="pack",
    )(latent, rope_t)


def attend_kernel(
    me_ref,
    table_ref,
    nope0_ref,
    nope1_ref,
    rope0_ref,
    rope1_ref,
    *refs,
):
    parts = refs[:4]
    wk_ref, wv_ref, out_ref, kv_ref, bias_ref, q_ref, s_ref, p_ref, total_ref, sem = refs[4:]
    heads, tok, _ = nope0_ref.shape
    rows, keys = bias_ref.shape
    width = wk_ref.shape[2]
    rope = rope0_ref.shape[0] // heads
    span_len = keys // table_ref.shape[0]
    per = tok // span_len

    length = keys // 4
    copies = [
        pltpu.make_async_copy(part, kv_ref.at[pl.ds(n * length, length)], sem.at[n])
        for n, part in enumerate(parts)
    ]

    @pl.when(pl.program_id(0) == 0)
    def _():
        for copy in copies:
            copy.start()
        me = me_ref[0]
        slabs = length // tok
        lane = lax.broadcasted_iota(jnp.int32, (1, keys), 1)
        kpos = jnp.zeros((1, keys), jnp.int32)
        for n in range(keys // span_len):
            block, inside = n // per, n % per
            part, k = block // slabs, block % slabs
            slab = (me >> 2) ^ k
            source = slab * 4 + ((me & 3) ^ ((part & 1) * 2 + (part >> 1)))
            first = table_ref[source * per + inside] * span_len - n * span_len
            kpos = jnp.where(lane >= n * span_len, first + lane, kpos)
        sub = lax.broadcasted_iota(jnp.int32, (rows, 1), 0)
        qpos = jnp.zeros((rows, 1), jnp.int32)
        for n in range(rows // span_len):
            source = me ^ (n // per)
            first = table_ref[source * per + n % per] * span_len - n * span_len
            qpos = jnp.where(sub >= n * span_len, first + sub, qpos)
        bias_ref[...] = jnp.where(kpos <= qpos, jnp.float32(0.0), jnp.float32(-1e30))

    f32, bf16 = jnp.float32, jnp.bfloat16
    for h in range(heads):
        nope = jnp.concatenate([nope0_ref[h].astype(f32), nope1_ref[h].astype(f32)], axis=0)
        q_lat = jnp.dot(nope.astype(bf16), wk_ref[h], preferred_element_type=f32)
        q_ref[h * rows : (h + 1) * rows, :width] = q_lat.astype(bf16)
    lane = lax.broadcasted_iota(jnp.int32, (rows, 2 * rope), 1)
    for h in range(0, heads, 2):
        pick = slice(h * rope, (h + 2) * rope)
        pair = jnp.concatenate(
            [rope0_ref[pick, :].astype(f32).T, rope1_ref[pick, :].astype(f32).T], axis=0
        )
        q_ref[h * rows : (h + 1) * rows, width:] = jnp.where(lane < rope, pair, 0.0).astype(bf16)
        q_ref[(h + 1) * rows : (h + 2) * rows, width:] = jnp.where(lane < rope, 0.0, pair).astype(
            bf16
        )

    @pl.when(pl.program_id(0) == 0)
    def _():
        for copy in copies:
            copy.wait()

    units, step = 2, 16
    count = heads * rows // units

    def scores(u):
        s_ref[pl.ds(u * count, count), :] = lax.dot_general(
            q_ref[pl.ds(u * count, count), :],
            kv_ref[...],
            (((1,), (1,)), ((), ())),
            preferred_element_type=f32,
        )

    def weights(u):
        for r in range(u * count, (u + 1) * count, step):
            block = s_ref[r : r + step, :] * (score_scale * LOG2E)
            block = block + bias_ref[r % rows : r % rows + step, :]
            weight = jnp.exp2(block - jnp.max(block, axis=1, keepdims=True))
            total_ref[r : r + step, :] = 1.0 / jnp.sum(weight, axis=1, keepdims=True)
            p_ref[r : r + step, :] = weight.astype(bf16)

    def outputs(u):
        context = jnp.dot(
            p_ref[pl.ds(u * count, count), :], kv_ref[:, :width], preferred_element_type=f32
        )
        context = (context * total_ref[pl.ds(u * count, count), :]).astype(bf16)
        for n in range(count // rows):
            h = u * (count // rows) + n
            part = jnp.dot(
                context[n * rows : (n + 1) * rows], wv_ref[h], preferred_element_type=f32
            )
            out_ref[:, h * part.shape[1] : (h + 1) * part.shape[1]] = part.astype(out_ref.dtype)

    for u in range(units + 2):
        if u < units:
            scores(u)
        if 1 <= u <= units:
            weights(u - 1)
        if u >= 2:
            outputs(u - 2)


def attend(me, table, nope, rope, parts, wk, wv, group, groups, heads):
    half, tok, size = nope[0].shape
    steps = half // groups // heads
    rows = 2 * tok
    keys, depth = 4 * parts[0].shape[0], parts[0].shape[1]
    width = wk.shape[2]
    rope_rows = rope[0].shape[0] // half * heads
    first = group * steps

    def mine(i, me_ref, table_ref):
        return (first + i, 0, 0)

    def mine_flat(i, me_ref, table_ref):
        return (first + i, 0)

    return pl.pallas_call(
        attend_kernel,
        grid_spec=pltpu.PrefetchScalarGridSpec(
            num_scalar_prefetch=2,
            grid=(steps,),
            in_specs=[
                pl.BlockSpec((heads, tok, size), mine),
                pl.BlockSpec((heads, tok, size), mine),
                pl.BlockSpec((rope_rows, tok), mine_flat),
                pl.BlockSpec((rope_rows, tok), mine_flat),
                *[pl.BlockSpec(memory_space=pl.ANY)] * 4,
                pl.BlockSpec((heads, size, width), mine),
                pl.BlockSpec((heads, width, size), mine),
            ],
            out_specs=pl.BlockSpec((rows, heads * size), lambda i, me_ref, table_ref: (0, i)),
            scratch_shapes=[
                pltpu.VMEM((keys, depth), jnp.bfloat16),
                pltpu.VMEM((rows, keys), jnp.float32),
                pltpu.VMEM((heads * rows, depth), jnp.bfloat16),
                pltpu.VMEM((heads * rows, keys), jnp.float32),
                pltpu.VMEM((heads * rows, keys), jnp.bfloat16),
                pltpu.VMEM((heads * rows, 1), jnp.float32),
                pltpu.SemaphoreType.DMA((4,)),
            ],
        ),
        out_shape=jax.ShapeDtypeStruct((rows, half // groups * size), jnp.bfloat16),
        compiler_params=pltpu.CompilerParams(vmem_limit_bytes=24 * 1024 * 1024),
        cost_estimate=pl.CostEstimate(
            flops=2 * half // groups * rows * keys * (depth + width),
            bytes_accessed=half // groups * (rows + 2 * width) * size * 2,
            transcendentals=half // groups * rows * keys,
        ),
        name="attend",
    )(me, table, *nope, *rope, *parts, wk, wv)


def project_kernel(plain, choice, skip, prev, me_ref, *refs):
    refs = list(refs)

    def take(count):
        out, refs[:count] = refs[:count], []
        return out

    fixed = [take(2) for _ in range(plain)]
    options = [take(2) for _ in range(choice)]
    weights = take(len(refs) - 2 - (2 if prev else 0))
    before = take(2) if prev else []
    keep_ref, send_ref = refs
    tok = keep_ref.shape[2]
    for old, new in zip(before, refs):
        new[: old.shape[0], : old.shape[1]] = old[...]

    def emit(blocks, at, first):
        for j in range(first, len(weights)):
            total = 0.0
            for g in range(2):
                rows = jnp.concatenate([block[g][...] for block in blocks], axis=0)
                width = rows.shape[1]
                total = total + lax.dot_general(
                    rows,
                    weights[j][:, g * width : (g + 1) * width],
                    (((1,), (1,)), ((), ())),
                    preferred_element_type=jnp.float32,
                )
            for n in range(len(blocks)):
                start = 2 * tok * n
                keep_ref[j, at + n] = total[start : start + tok]
                send_ref[j, at + n] = total[start + tok : start + 2 * tok].astype(send_ref.dtype)

    if fixed:
        emit(fixed, 0, skip)
    slab = me_ref[0] >> 2
    inner = (slab == 1) | (slab == 2)
    for n, option in enumerate(options):

        @pl.when(inner if n == 0 else ~inner)
        def _():
            emit([option], plain, 0)


def project(me, fixed, options, weights, tok, skip=0, before=()):
    count = len(fixed) + bool(options)
    shape = (len(weights), count, tok, weights[0].shape[0])
    operands = [ref for block in [*fixed, *options] for ref in block] + list(weights) + list(before)
    vmem = pl.BlockSpec(memory_space=pltpu.VMEM)
    return pl.pallas_call(
        functools.partial(project_kernel, len(fixed), len(options), skip, bool(before)),
        in_specs=[pl.BlockSpec(memory_space=pltpu.SMEM)] + [vmem] * len(operands),
        out_specs=[vmem, vmem],
        out_shape=[
            jax.ShapeDtypeStruct(shape, jnp.float32),
            jax.ShapeDtypeStruct(shape, jnp.bfloat16),
        ],
        compiler_params=pltpu.CompilerParams(vmem_limit_bytes=16 * 1024 * 1024),
        cost_estimate=pl.CostEstimate(
            flops=4 * tok * count * sum(w.size for w in weights),
            bytes_accessed=0,
            transcendentals=0,
        ),
        name="project",
    )(me, *operands)


def finish_kernel(me_ref, res_ref, gain_ref, *refs):
    pieces = refs[:-3]
    new_ref, normed_ref, hidden_ref = refs[-3:]
    me = me_ref[0]
    cols = pieces[0].shape[2]
    wide = 4 * cols
    for k, piece in enumerate(pieces):
        at = pl.multiple_of(me_ref[1 + k] * wide, wide)
        for case in range(4):

            @pl.when((me & 3) == case)
            def _():
                row = jnp.concatenate([piece[j ^ case] for j in range(4)], axis=1)
                old = res_ref[:, pl.ds(at, wide)].astype(jnp.float32)
                hidden_ref[:, pl.ds(at, wide)] = old + row.astype(jnp.float32)

    hidden = hidden_ref[...]
    new_ref[...] = hidden.astype(new_ref.dtype)
    scale = lax.rsqrt(jnp.mean(hidden * hidden, axis=1, keepdims=True) + 1e-06)
    normed_ref[...] = (hidden * scale * gain_ref[...]).astype(normed_ref.dtype)


def finish(places, residual, gain, pieces):
    vmem = pl.BlockSpec(memory_space=pltpu.VMEM)
    out = jax.ShapeDtypeStruct(residual.shape, jnp.bfloat16)
    return pl.pallas_call(
        finish_kernel,
        in_specs=[pl.BlockSpec(memory_space=pltpu.SMEM)] + [vmem] * (2 + len(pieces)),
        out_specs=[vmem, vmem],
        out_shape=[out, out],
        scratch_shapes=[pltpu.VMEM(residual.shape, jnp.float32)],
        compiler_params=pltpu.CompilerParams(vmem_limit_bytes=8 * 1024 * 1024),
        name="finish",
    )(places, residual, gain, *pieces)


def per_device(
    q_nope, q_rope, latent, key_rope, absorb_key, absorb_value, w_out, residual, norm_gain, span_table
):
    f32, bf16 = jnp.float32, jnp.bfloat16
    tok, heads, size = q_nope.shape
    rope = q_rope.shape[2]
    n_seq, n_heads = lax.axis_size("seq"), lax.axis_size("heads")
    depth_z = n_seq // 4
    me = lax.axis_index("seq").astype(jnp.int32)
    core, slab = me & 1, me >> 2
    half = heads // 2

    line = depth_z == 4

    def swap(x, bit):
        return lax.ppermute(x, "seq", [(i, i ^ bit) for i in range(n_seq)])

    def move(x, pairs):
        return lax.ppermute(x, "seq", [(4 * a + r, 4 * b + r) for a, b in pairs for r in range(4)])

    kv_own = pack(latent, key_rope.T)
    zs, ys = [kv_own], [swap(kv_own, 2)]
    for k in range(1, depth_z):
        k = (k ^ (k >> 1)) if line else k
        zs.append(swap(kv_own, 4 * k))
        ys.append(swap(zs[-1], 2))
    if line:
        zs, ys = [zs[k] for k in (0, 1, 3, 2)], [ys[k] for k in (0, 1, 3, 2)]
    along, across = jnp.concatenate(zs, axis=0), jnp.concatenate(ys, axis=0)

    def split_heads(x, count):
        mine = lax.dynamic_slice_in_dim(x, core * count, count, 0)
        theirs = lax.dynamic_slice_in_dim(x, (1 - core) * count, count, 0)
        return mine, swap(theirs, 1)

    nope = split_heads(jnp.transpose(q_nope, (1, 0, 2)), half)
    rotary = split_heads(jnp.transpose(q_rope, (1, 2, 0)).reshape(heads * rope, tok), half * rope)

    wk = lax.dynamic_slice_in_dim(absorb_key, core * half, half, 0)
    wv = lax.dynamic_slice_in_dim(absorb_value, core * half, half, 0)
    along, wk, wv, *own = lax.optimization_barrier((along, wk, wv, nope[0], rotary[0]))
    nope, rotary = (own[0], nope[1]), (own[1], rotary[1])
    parts = [along, across, swap(along, 1), swap(across, 1)]

    w_t = w_out.T
    cols = w_t.shape[0]
    span = half * size
    w_mine = lax.dynamic_slice_in_dim(w_t, core * span, span, 1)
    w_theirs = lax.dynamic_slice_in_dim(w_t, (1 - core) * span, span, 1)
    w_core = swap(w_theirs, 1)
    weights = [w_mine, w_core, swap(w_mine, 2), swap(w_core, 2)]

    groups = 2
    step_heads = max(
        h for h in (4, 2) if half // groups % h == 0 and h * tok * 8 * tok * depth_z <= 3 << 19
    )
    blocks = []
    for g in range(groups):
        mixed = attend(
            me.reshape(1),
            span_table,
            nope,
            rotary,
            parts,
            wk,
            wv,
            g,
            groups,
            step_heads,
        )
        if line:
            near = move(mixed, [(0, 1), (1, 0), (2, 3), (3, 2)])
            mid = move(mixed, [(1, 2), (2, 1)])
            out2 = move(mid, [(1, 0), (2, 3)])
            far = move(near, [(1, 2), (2, 1)])
            out3 = move(far, [(1, 0), (2, 3)])
            blocks.append([mixed, near, far, out2, mid, out3])
        else:
            blocks.append([mixed] + [swap(mixed, 4 * k) for k in range(1, depth_z)])

    def reduce(keep, send):
        count = keep.shape[1]
        other = swap(send, 1)
        total = keep + jnp.stack([other[j ^ 1] for j in range(4)]).astype(f32)
        if n_heads == 2:
            x = lax.axis_index("heads")
            total = total.reshape(4, count, 2, tok // 2, cols)
            keep = lax.dynamic_index_in_dim(total, x, 2, keepdims=False)
            send = lax.dynamic_index_in_dim(total, 1 - x, 2, keepdims=False)
            got = lax.ppermute(send.astype(bf16), "heads", [(0, 1), (1, 0)])
            total = keep + got.astype(f32)
        else:
            total = lax.psum_scatter(total.astype(bf16), "heads", scatter_dimension=2, tiled=True)
        total = total.astype(bf16)
        return [total[:, n] for n in range(count)]

    if line:
        mixed, near, far, out2, mid, out3 = zip(*blocks)
        me1 = me.reshape(1)
        first = project(me1, [mixed, near], [], weights[:2], tok)
        early = project(me1, [mixed, near], [far, out2], weights, tok, 2, first)
        late = project(me1, [], [mid, out3], weights, tok)
        mine = reduce(*early) + reduce(*late)
    else:
        rows = jnp.stack([jnp.concatenate(parts, axis=1) for parts in zip(*blocks)])
        total = jnp.einsum("zti,joi->jzto", rows, jnp.stack(weights), preferred_element_type=f32)
        mine = reduce(total[:, :, :tok], total[:, :, tok:].astype(bf16))
    pieces = [mine[0]] + [swap(mine[k], 4 * k) for k in range(1, depth_z)]
    places = slab ^ jnp.arange(depth_z, dtype=jnp.int32)
    if 4 * cols % 128 == 0:
        places = jnp.concatenate([me.reshape(1), places])
        return tuple(finish(places, residual, norm_gain[None, :], pieces))
    order = jnp.arange(depth_z, dtype=jnp.int32)
    order = jnp.sum(jnp.where(places[None, :] == order[:, None], order[None, :], 0), axis=1)
    columns = jnp.take(jnp.stack(pieces), order, axis=0)
    columns = jnp.take(columns, jnp.arange(4, dtype=jnp.int32) ^ (me & 3), axis=1)
    hidden = residual.astype(f32) + jnp.moveaxis(columns, 2, 0).reshape(residual.shape).astype(f32)
    scale = lax.rsqrt(jnp.mean(hidden * hidden, axis=1, keepdims=True) + 1e-06)
    return (hidden.astype(bf16), (hidden * scale * norm_gain[None, :]).astype(bf16))


def solution(mesh):
    in_specs = (
        P("seq", "heads", None),
        P("seq", "heads", None),
        P("seq", None),
        P("seq", None),
        P("heads", None, None),
        P("heads", None, None),
        P("heads", "seq"),
        P(("seq", "heads"), None),
        P(),
        P(),
    )
    out_specs = (P(("seq", "heads"), None), P(("seq", "heads"), None))

    return jax.shard_map(
        per_device, mesh=mesh, in_specs=in_specs, out_specs=out_specs, check_vma=False
    )
```

profile of v0, /device:TPU:0, one launch (start us, length us, event | category | flops | bytes accessed | tf_op | source)
XLA Modules:
  0.0 120.1 jit_solution(3478237362225569112)
XLA Ops:
  0.6 0.9 copy-done.9
  2.4 3.1 %collective-permute-start = (bf16[72,640]{1,0:T(8,128)(2,1)S(1)}, bf16[72,640]{1,0:T(8,128)(2,1)}, u32[]{:S(2)}, u32[]{:S(2)}) collective-permute-start(bf16[72,640]{1,0:T(8,128)(2,1)S(1)} %pack.1), channel_id=1, source_target_pairs={{0,4},{1,5},{2,6},{3,7},{4,0},{5,1},{6,2},{7,3},{8,12},{9,13},{10,... | collective-permute-start | bytes 276488 | tf_op jit(solution)/shard_map/ppermute | solution.py:310
  5.5 2.6 %collective-permute-start.1 = (bf16[72,640]{1,0:T(8,128)(2,1)S(1)}, bf16[72,640]{1,0:T(8,128)(2,1)S(1)}, u32[]{:S(2)}, u32[]{:S(2)}) collective-permute-start(bf16[72,640]{1,0:T(8,128)(2,1)S(1)} %pack.1), channel_id=1, source_target_pairs={{0,8},{1,9},{2,10},{3,11},{4,12},{5,13},{6,14},{7,15},{8,0},{9,1},... | collective-permute-start | bytes 276488 | tf_op jit(solution)/shard_map/ppermute | solution.py:310
  8.1 1.7 %collective-permute-start.5 = (bf16[72,640]{1,0:T(8,128)(2,1)S(1)}, bf16[72,640]{1,0:T(8,128)(2,1)}, u32[]{:S(2)}, u32[]{:S(2)}) collective-permute-start(bf16[72,640]{1,0:T(8,128)(2,1)S(1)} %pack.1), channel_id=1, source_target_pairs={{0,2},{1,3},{2,0},{3,1},{4,6},{5,7},{6,4},{7,5},{8,10},{9,11},{10,... | collective-permute-start | bytes 276488 | tf_op jit(solution)/shard_map/ppermute | solution.py:310
  9.8 2.6 %dynamic-slice_bitcast_fusion = (bf16[224,2048]{1,0:T(8,128)(2,1)}, bf16[224,2048]{1,0:T(8,128)(2,1)S(1)}) fusion(bf16[4096,224]{0,1:T(8,128)(2,1)} %param.16, s32[]{:T(128)S(6)} %select_n.35, s32[]{:T(128)S(6)} %select_n.34), kind=kLoop, calls=%fused_computation | loop fusion | bytes 3670024 | tf_op jit(solution)/shard_map/dynamic_slice | solution.py:343
  12.7 3.3 %constant_dynamic-slice_fusion.8.refs_5_ = bf16[16,512,128]{2,1,0:T(8,128)(2,1)} fusion(bf16[32,512,128]{2,1,0:T(8,128)(2,1)} %param.15, s32[]{:T(128)S(6)} %select_n.30), kind=kLoop, calls=%fused_computation.31 | loop fusion | bytes 4194308 | tf_op jit(solution)/shard_map/dynamic_slice | solution.py:334
  16.0 1.5 %constant_dynamic-slice_fusion.9.refs_4_ = bf16[16,128,512]{2,1,0:T(8,128)(2,1)} fusion(bf16[32,128,512]{2,1,0:T(8,128)(2,1)S(1)} %copy-done.12, s32[]{:T(128)S(6)} %select_n.30), kind=kLoop, calls=%fused_computation.32 | loop fusion | bytes 4194308 | tf_op jit(solution)/shard_map/dynamic_slice | solution.py:333
  17.6 1.1 pad_maximum_fusion.refs_0_
  19.5 1.7 %collective-permute-start.7 = (bf16[72,640]{1,0:T(8,128)(2,1)S(1)}, bf16[72,640]{1,0:T(8,128)(2,1)S(1)}, u32[]{:S(2)}, u32[]{:S(2)}) collective-permute-start(bf16[72,640]{1,0:T(8,128)(2,1)S(1)} %collective-permute-done.1), channel_id=1, source_target_pairs={{0,2},{1,3},{2,0},{3,1},{4,6},{5,7},{6,4},{7,5},{8,10},{9,11},{10,... | collective-permute-start | bytes 276488 | tf_op jit(solution)/shard_map/ppermute | solution.py:310
  21.6 0.9 constant_dynamic-update-slice_fusion.3
  22.5 2.5 %collective-permute-done.6 = bf16[72,640]{1,0:T(8,128)(2,1)S(1)} collective-permute-done((bf16[72,640]{1,0:T(8,128)(2,1)}, bf16[72,640]{1,0:T(8,128)(2,1)S(1)}, u32[]{:S(2)}, u32[]{:S(2)}) %collective-permute-start.6) | collective-permute-done | bytes 92192 | tf_op jit(solution)/shard_map/ppermute | solution.py:310
  25.0 2.0 %collective-permute-done.7 = bf16[72,640]{1,0:T(8,128)(2,1)S(1)} collective-permute-done((bf16[72,640]{1,0:T(8,128)(2,1)S(1)}, bf16[72,640]{1,0:T(8,128)(2,1)S(1)}, u32[]{:S(2)}, u32[]{:S(2)}) %collective-permute-start.7) | collective-permute-done | bytes 92192 | tf_op jit(solution)/shard_map/ppermute | solution.py:310
  27.0 1.1 collective-permute-done.8
  28.9 1.7 %collective-permute-done.4.rope1_ref = bf16[1024,72]{1,0:T(8,128)(2,1)S(1)} collective-permute-done((bf16[1024,72]{1,0:T(8,128)(2,1)S(1)}, bf16[1024,72]{1,0:T(8,128)(2,1)S(1)}, u32[]{:S(2)}, u32[]{:S(2)}) %collective-permute-start.4) | collective-permute-done | bytes 147488 | tf_op jit(solution)/shard_map/ppermute | solution.py:310
  31.0 1.6 %copy-done.1 = bf16[16,128,512]{2,1,0:T(8,128)(2,1)S(1)} copy-done((bf16[16,128,512]{2,1,0:T(8,128)(2,1)S(1)}, bf16[16,128,512]{2,1,0:T(8,128)(2,1)}, u32[]{:S(2)}) %copy-start.1) | copy-done | bytes 2097176
  32.6 7.4 %attend.3.refs_1_ = bf16[144,1024]{1,0:T(8,128)(2,1)S(1)} custom-call(s32[1]{0:T(128)} %bitcast.me_ref, s32[32]{0:T(128)S(1)} %copy-done.11, bf16[16,72,128]{2,1,0:T(8,128)(2,1)S(1)} %bitcast.41, bf16[16,72,128]{2,1,0:T(8,128)(2,1)S(1)} %collective-permute-done.3.nope1_ref, bf16[1024,72]{1,0:T(8,128)(2,1)S(1)} %get-tuple-element.14.rope0_ref, ...), custom_call_target="tpu_custom_call" | custom-call | flops 3057647616 | bytes 2392064 | tf_op jit(solution)/shard_map/attend/pallas_call | solution.py:156
  39.9 1.0 collective-permute-start.12
  40.9 1.5 %collective-permute-start.21 = (bf16[224,2048]{1,0:T(8,128)(2,1)S(1)}, bf16[224,2048]{1,0:T(8,128)(2,1)}, u32[]{:S(2)}, u32[]{:S(2)}) collective-permute-start(bf16[224,2048]{1,0:T(8,128)(2,1)S(1)} %collective-permute-done.19.refs_5_.refs_9_), channel_id=1, source_target_pairs={{0,2},{1,3},{2,0},{3,1},{4,6},{5,7},{6,4},{7,5},{8,10},{9,11},{10,... | collective-permute-start | bytes 2752520 | tf_op jit(solution)/shard_map/ppermute | solution.py:310
  42.4 1.0 copy-done.7
  43.4 7.4 %attend.2.refs_0_ = bf16[144,1024]{1,0:T(8,128)(2,1)S(1)} custom-call(s32[1]{0:T(128)} %bitcast.me_ref, s32[32]{0:T(128)S(1)} %copy-done.11, bf16[16,72,128]{2,1,0:T(8,128)(2,1)S(1)} %bitcast.42, bf16[16,72,128]{2,1,0:T(8,128)(2,1)S(1)} %collective-permute-done.3.nope1_ref, bf16[1024,72]{1,0:T(8,128)(2,1)S(1)} %get-tuple-element.14.rope0_ref, ...), custom_call_target="tpu_custom_call" | custom-call | flops 3057647616 | bytes 2392064 | tf_op jit(solution)/shard_map/attend/pallas_call | solution.py:156
  50.8 1.4 %collective-permute-start.11 = (bf16[144,1024]{1,0:T(8,128)(2,1)S(1)}, bf16[144,1024]{1,0:T(8,128)(2,1)S(1)}, u32[]{:S(2)}, u32[]{:S(2)}) collective-permute-start(bf16[144,1024]{1,0:T(8,128)(2,1)S(1)} %attend.2.refs_0_), channel_id=1, source_target_pairs={{0,4},{1,5},{2,6},{3,7},{4,0},{5,1},{6,2},{7,3},{8,12},{9,13},{10,... | collective-permute-start | bytes 884744 | tf_op jit(solution)/shard_map/ppermute | solution.py:313
  52.2 1.4 %collective-permute-start.17 = (bf16[144,1024]{1,0:T(8,128)(2,1)S(1)}, bf16[144,1024]{1,0:T(8,128)(2,1)}, u32[]{:S(2)}, u32[]{:S(2)}) collective-permute-start(bf16[144,1024]{1,0:T(8,128)(2,1)S(1)} %attend.3.refs_1_), channel_id=1, source_target_pairs={{4,8},{5,9},{6,10},{7,11},{8,4},{9,5},{10,6},{11,7},{20,24},{21,25... | collective-permute-start | bytes 884744 | tf_op jit(solution)/shard_map/ppermute | solution.py:313
  53.6 1.4 %collective-permute-start.14 = (bf16[144,1024]{1,0:T(8,128)(2,1)S(1)}, bf16[144,1024]{1,0:T(8,128)(2,1)}, u32[]{:S(2)}, u32[]{:S(2)}) collective-permute-start(bf16[144,1024]{1,0:T(8,128)(2,1)S(1)} %collective-permute-done.12.refs_3_), channel_id=1, source_target_pairs={{4,8},{5,9},{6,10},{7,11},{8,4},{9,5},{10,6},{11,7},{20,24},{21,25... | collective-permute-start | bytes 884744 | tf_op jit(solution)/shard_map/ppermute | solution.py:313
  55.0 4.1 %collective-permute-done.11.refs_2_ = bf16[144,1024]{1,0:T(8,128)(2,1)S(1)} collective-permute-done((bf16[144,1024]{1,0:T(8,128)(2,1)S(1)}, bf16[144,1024]{1,0:T(8,128)(2,1)S(1)}, u32[]{:S(2)}, u32[]{:S(2)}) %collective-permute-start.11) | collective-permute-done | bytes 294944 | tf_op jit(solution)/shard_map/ppermute | solution.py:313
  59.0 1.4 %collective-permute-start.13 = (bf16[144,1024]{1,0:T(8,128)(2,1)S(1)}, bf16[144,1024]{1,0:T(8,128)(2,1)}, u32[]{:S(2)}, u32[]{:S(2)}) collective-permute-start(bf16[144,1024]{1,0:T(8,128)(2,1)S(1)} %collective-permute-done.11.refs_2_), channel_id=1, source_target_pairs={{4,8},{5,9},{6,10},{7,11},{8,4},{9,5},{10,6},{11,7},{20,24},{21,25... | collective-permute-start | bytes 884744 | tf_op jit(solution)/shard_map/ppermute | solution.py:313
  61.1 1.4 %collective-permute-start.15 = (bf16[144,1024]{1,0:T(8,128)(2,1)S(1)}, bf16[144,1024]{1,0:T(8,128)(2,1)}, u32[]{:S(2)}, u32[]{:S(2)}) collective-permute-start(bf16[144,1024]{1,0:T(8,128)(2,1)S(1)} %attend.2.refs_0_), channel_id=1, source_target_pairs={{4,8},{5,9},{6,10},{7,11},{8,4},{9,5},{10,6},{11,7},{20,24},{21,25... | collective-permute-start | bytes 884744 | tf_op jit(solution)/shard_map/ppermute | solution.py:313
  63.2 1.3 %collective-permute-start.27 = (bf16[144,1024]{1,0:T(8,128)(2,1)}, bf16[144,1024]{1,0:T(8,128)(2,1)}, u32[]{:S(2)}, u32[]{:S(2)}) collective-permute-start(bf16[144,1024]{1,0:T(8,128)(2,1)} %collective-permute-done.14.refs_5_), channel_id=1, source_target_pairs={{4,0},{5,1},{6,2},{7,3},{8,12},{9,13},{10,14},{11,15},{20,16},{21,... | collective-permute-start | bytes 884744 | tf_op jit(solution)/shard_map/ppermute | solution.py:313
  64.5 1.3 %collective-permute-start.26 = (bf16[144,1024]{1,0:T(8,128)(2,1)}, bf16[144,1024]{1,0:T(8,128)(2,1)}, u32[]{:S(2)}, u32[]{:S(2)}) collective-permute-start(bf16[144,1024]{1,0:T(8,128)(2,1)} %collective-permute-done.13.refs_4_), channel_id=1, source_target_pairs={{4,0},{5,1},{6,2},{7,3},{8,12},{9,13},{10,14},{11,15},{20,16},{21,... | collective-permute-start | bytes 884744 | tf_op jit(solution)/shard_map/ppermute | solution.py:313
  65.8 1.3 %collective-permute-start.18 = (bf16[144,1024]{1,0:T(8,128)(2,1)}, bf16[144,1024]{1,0:T(8,128)(2,1)}, u32[]{:S(2)}, u32[]{:S(2)}) collective-permute-start(bf16[144,1024]{1,0:T(8,128)(2,1)} %collective-permute-done.17.refs_1_), channel_id=1, source_target_pairs={{4,0},{5,1},{6,2},{7,3},{8,12},{9,13},{10,14},{11,15},{20,16},{21,... | collective-permute-start | bytes 884744 | tf_op jit(solution)/shard_map/ppermute | solution.py:313
  67.2 1.3 %collective-permute-start.16 = (bf16[144,1024]{1,0:T(8,128)(2,1)}, bf16[144,1024]{1,0:T(8,128)(2,1)}, u32[]{:S(2)}, u32[]{:S(2)}) collective-permute-start(bf16[144,1024]{1,0:T(8,128)(2,1)} %collective-permute-done.15.refs_0_), channel_id=1, source_target_pairs={{4,0},{5,1},{6,2},{7,3},{8,12},{9,13},{10,14},{11,15},{20,16},{21,... | collective-permute-start | bytes 884744 | tf_op jit(solution)/shard_map/ppermute | solution.py:313
  68.5 1.0 copy-done.3
  69.5 1.0 copy-done.5
  70.4 0.8 project.3
  71.2 6.3 %collective-permute-done.27.refs_3_ = bf16[144,1024]{1,0:T(8,128)(2,1)} collective-permute-done((bf16[144,1024]{1,0:T(8,128)(2,1)}, bf16[144,1024]{1,0:T(8,128)(2,1)}, u32[]{:S(2)}, u32[]{:S(2)}) %collective-permute-start.27) | collective-permute-done | bytes 294944 | tf_op jit(solution)/shard_map/ppermute | solution.py:313
  77.6 6.3 %collective-permute-done.26.refs_2_ = bf16[144,1024]{1,0:T(8,128)(2,1)} collective-permute-done((bf16[144,1024]{1,0:T(8,128)(2,1)}, bf16[144,1024]{1,0:T(8,128)(2,1)}, u32[]{:S(2)}, u32[]{:S(2)}) %collective-permute-start.26) | collective-permute-done | bytes 294944 | tf_op jit(solution)/shard_map/ppermute | solution.py:313
  83.9 2.9 %project.5 = (f32[4,1,72,224]{3,2,1,0:T(8,128)S(1)}, bf16[4,1,72,224]{3,2,1,0:T(8,128)(2,1)S(1)}) custom-call(s32[1]{0:T(128)} %bitcast.me_ref, bf16[144,1024]{1,0:T(8,128)(2,1)} %collective-permute-done.15.refs_0_, bf16[144,1024]{1,0:T(8,128)(2,1)} %collective-permute-done.17.refs_1_, bf16[144,1024]{1,0:T(8,128)(2,1)} %collective-permute-done.26.refs_2_, ...), custom_call_target="tpu_custom_call" | custom-call | flops 528482304 | tf_op jit(solution)/shard_map/project/pallas_call | solution.py:241
  86.9 4.9 %collective-permute-done.18.refs_7_ = bf16[144,1024]{1,0:T(8,128)(2,1)} collective-permute-done((bf16[144,1024]{1,0:T(8,128)(2,1)}, bf16[144,1024]{1,0:T(8,128)(2,1)}, u32[]{:S(2)}, u32[]{:S(2)}) %collective-permute-start.18) | collective-permute-done | bytes 294944 | tf_op jit(solution)/shard_map/ppermute | solution.py:313
  91.8 4.5 %collective-permute-done.16.refs_6_ = bf16[144,1024]{1,0:T(8,128)(2,1)} collective-permute-done((bf16[144,1024]{1,0:T(8,128)(2,1)}, bf16[144,1024]{1,0:T(8,128)(2,1)}, u32[]{:S(2)}, u32[]{:S(2)}) %collective-permute-start.16) | collective-permute-done | bytes 294944 | tf_op jit(solution)/shard_map/ppermute | solution.py:313
  96.4 3.9 %project.4 = (f32[4,3,72,224]{3,2,1,0:T(8,128)S(1)}, bf16[4,3,72,224]{3,2,1,0:T(8,128)(2,1)S(1)}) custom-call(s32[1]{0:T(128)} %bitcast.me_ref, bf16[144,1024]{1,0:T(8,128)(2,1)S(1)} %copy-done.3, bf16[144,1024]{1,0:T(8,128)(2,1)S(1)} %attend.3.refs_1_, bf16[144,1024]{1,0:T(8,128)(2,1)S(1)} %copy-done.5, ...), custom_call_target="tpu_custom_call" | custom-call | flops 1585446912 | tf_op jit(solution)/shard_map/project/pallas_call | solution.py:241
  100.6 1.6 %collective-permute-start.29 = (bf16[4,1,36,224]{3,2,0,1:T(8,128)(2,1)S(1)}, bf16[4,1,36,224]{3,2,0,1:T(8,128)(2,1)S(1)}, u32[]{:S(2)}, u32[]{:S(2)}) collective-permute-start(bf16[4,1,36,224]{3,2,0,1:T(8,128)(2,1)S(1)} %bitcast.51), channel_id=1, source_target_pairs={{0,16},{16,0},{1,17},{17,1},{2,18},{18,2},{3,19},{19,3},{4,20},{20... | collective-permute-start | bytes 193544 | tf_op jit(solution)/shard_map/ppermute | solution.py:384
  103.0 1.5 %collective-permute-start.23 = (bf16[4,3,36,224]{3,2,0,1:T(8,128)(2,1)S(1)}, bf16[4,3,36,224]{3,2,0,1:T(8,128)(2,1)S(1)}, u32[]{:S(2)}, u32[]{:S(2)}) collective-permute-start(bf16[4,3,36,224]{3,2,0,1:T(8,128)(2,1)S(1)} %bitcast.50), channel_id=1, source_target_pairs={{0,16},{16,0},{1,17},{17,1},{2,18},{18,2},{3,19},{19,3},{4,20},{20... | collective-permute-start | bytes 580616 | tf_op jit(solution)/shard_map/ppermute | solution.py:384
  104.4 1.1 collective-permute-done.29
  105.6 3.0 %collective-permute-start.30 = (bf16[4,36,224]{2,1,0:T(8,128)(2,1)S(1)}, bf16[4,36,224]{2,1,0:T(8,128)(2,1)S(1)}, u32[]{:S(2)}, u32[]{:S(2)}) collective-permute-start(bf16[4,36,224]{2,1,0:T(8,128)(2,1)S(1)} %fusion.3), channel_id=1, source_target_pairs={{0,12},{1,13},{2,14},{3,15},{4,8},{5,9},{6,10},{7,11},{8,4},{9,5},... | collective-permute-start | bytes 193544 | tf_op jit(solution)/shard_map/ppermute | solution.py:310
  108.6 2.5 %collective-permute-done.23 = bf16[4,3,36,224]{3,2,0,1:T(8,128)(2,1)S(1)} collective-permute-done((bf16[4,3,36,224]{3,2,0,1:T(8,128)(2,1)S(1)}, bf16[4,3,36,224]{3,2,0,1:T(8,128)(2,1)S(1)}, u32[]{:S(2)}, u32[]{:S(2)}) %collective-permute-start.23) | collective-permute-done | bytes 193568 | tf_op jit(solution)/shard_map/ppermute | solution.py:384
  111.3 3.5 %collective-permute-start.25 = (bf16[4,36,224]{2,1,0:T(8,128)(2,1)S(1)}, bf16[4,36,224]{2,1,0:T(8,128)(2,1)S(1)}, u32[]{:S(2)}, u32[]{:S(2)}) collective-permute-start(bf16[4,36,224]{2,1,0:T(8,128)(2,1)S(1)} %get-tuple-element.34), channel_id=1, source_target_pairs={{0,8},{1,9},{2,10},{3,11},{4,12},{5,13},{6,14},{7,15},{8,0},{9,1},... | collective-permute-start | bytes 193544 | tf_op jit(solution)/shard_map/ppermute | solution.py:310
  114.8 1.7 %collective-permute-done.24.refs_1_ = bf16[4,36,224]{2,1,0:T(8,128)(2,1)S(1)} collective-permute-done((bf16[4,36,224]{2,1,0:T(8,128)(2,1)S(1)}, bf16[4,36,224]{2,1,0:T(8,128)(2,1)S(1)}, u32[]{:S(2)}, u32[]{:S(2)}) %collective-permute-start.24) | collective-permute-done | bytes 64544 | tf_op jit(solution)/shard_map/ppermute | solution.py:310
  116.6 1.6 %collective-permute-done.25.refs_2_ = bf16[4,36,224]{2,1,0:T(8,128)(2,1)S(1)} collective-permute-done((bf16[4,36,224]{2,1,0:T(8,128)(2,1)S(1)}, bf16[4,36,224]{2,1,0:T(8,128)(2,1)S(1)}, u32[]{:S(2)}, u32[]{:S(2)}) %collective-permute-start.25) | collective-permute-done | bytes 64544 | tf_op jit(solution)/shard_map/ppermute | solution.py:310
  118.2 1.8 %finish.1 = (bf16[36,3584]{1,0:T(8,128)(2,1)}, bf16[36,3584]{1,0:T(8,128)(2,1)}) custom-call(s32[5]{0:T(128)S(1)} %pad_add_fusion.me_ref, bf16[36,3584]{1,0:T(8,128)(2,1)S(1)} %copy-done.8, f32[1,3584]{1,0:T(1,128)S(1)} %broadcast_in_dim.3.gain_ref, bf16[4,36,224]{2,1,0:T(8,128)(2,1)S(1)} %get-tuple-element.36.refs_0_, ...), custom_call_target="tpu_custom_call" | custom-call | tf_op jit(solution)/shard_map/finish/pallas_call | solution.py:284
  (83 shorter events, 6.3 us)
Async XLA Ops:
  0.6 0.9 copy-start.9
  1.5 0.7 copy-start.10
  2.2 10.2 %copy-start.13 = (bf16[72,32,128]{2,1,0:T(8,128)(2,1)S(1)}, bf16[72,32,128]{2,1,0:T(8,128)(2,1)}, u32[]{:S(2)}) copy-start(bf16[72,32,128]{2,1,0:T(8,128)(2,1)} %param.10) | copy-start | bytes 1769476
  2.4 15.2 %collective-permute-start = (bf16[72,640]{1,0:T(8,128)(2,1)S(1)}, bf16[72,640]{1,0:T(8,128)(2,1)}, u32[]{:S(2)}, u32[]{:S(2)}) collective-permute-start(bf16[72,640]{1,0:T(8,128)(2,1)S(1)} %pack.1), channel_id=1, source_target_pairs={{0,4},{1,5},{2,6},{3,7},{4,0},{5,1},{6,2},{7,3},{8,12},{9,13},{10,... | collective-permute-start | bytes 276488 | tf_op jit(solution)/shard_map/ppermute | solution.py:310
  5.5 12.1 %collective-permute-start.1 = (bf16[72,640]{1,0:T(8,128)(2,1)S(1)}, bf16[72,640]{1,0:T(8,128)(2,1)S(1)}, u32[]{:S(2)}, u32[]{:S(2)}) collective-permute-start(bf16[72,640]{1,0:T(8,128)(2,1)S(1)} %pack.1), channel_id=1, source_target_pairs={{0,8},{1,9},{2,10},{3,11},{4,12},{5,13},{6,14},{7,15},{8,0},{9,1},... | collective-permute-start | bytes 276488 | tf_op jit(solution)/shard_map/ppermute | solution.py:310
  8.1 9.5 %collective-permute-start.2 = (bf16[72,640]{1,0:T(8,128)(2,1)S(1)}, bf16[72,640]{1,0:T(8,128)(2,1)S(1)}, u32[]{:S(2)}, u32[]{:S(2)}) collective-permute-start(bf16[72,640]{1,0:T(8,128)(2,1)S(1)} %pack.1), channel_id=1, source_target_pairs={{0,12},{1,13},{2,14},{3,15},{4,8},{5,9},{6,10},{7,11},{8,4},{9,5},... | collective-permute-start | bytes 276488 | tf_op jit(solution)/shard_map/ppermute | solution.py:310
  8.1 13.2 %collective-permute-start.5 = (bf16[72,640]{1,0:T(8,128)(2,1)S(1)}, bf16[72,640]{1,0:T(8,128)(2,1)}, u32[]{:S(2)}, u32[]{:S(2)}) collective-permute-start(bf16[72,640]{1,0:T(8,128)(2,1)S(1)} %pack.1), channel_id=1, source_target_pairs={{0,2},{1,3},{2,0},{3,1},{4,6},{5,7},{6,4},{7,5},{8,10},{9,11},{10,... | collective-permute-start | bytes 276488 | tf_op jit(solution)/shard_map/ppermute | solution.py:310
  12.5 28.4 %collective-permute-start.19 = (bf16[224,2048]{1,0:T(8,128)(2,1)}, bf16[224,2048]{1,0:T(8,128)(2,1)S(1)}, u32[]{:S(2)}, u32[]{:S(2)}) collective-permute-start(bf16[224,2048]{1,0:T(8,128)(2,1)} %get-tuple-element.24), channel_id=1, source_target_pairs={{0,1},{1,0},{2,3},{3,2},{4,5},{5,4},{6,7},{7,6},{8,9},{9,8},{10,11... | collective-permute-start | bytes 2752520 | tf_op jit(solution)/shard_map/ppermute | solution.py:310
  12.7 18.3 %copy-start.6 = (bf16[72,16,128]{2,0,1:T(8,128)(2,1)}, bf16[72,16,128]{2,0,1:T(8,128)(2,1)S(1)}, u32[]{:S(2)}) copy-start(bf16[72,16,128]{2,0,1:T(8,128)(2,1)S(1)} %copy.39) | copy-start | bytes 884740
  12.7 3.3 %copy-start.12 = (bf16[32,128,512]{2,1,0:T(8,128)(2,1)S(1)}, bf16[32,128,512]{2,1,0:T(8,128)(2,1)}, u32[]{:S(2)}) copy-start(bf16[32,128,512]{2,1,0:T(8,128)(2,1)} %param.14) | copy-start | bytes 12582916
  16.0 1.6 %copy-start.14 = (bf16[72,32,64]{0,2,1:T(8,128)(2,1)S(1)}, bf16[72,32,64]{0,2,1:T(8,128)(2,1)}, u32[]{:S(2)}) copy-start(bf16[72,32,64]{0,2,1:T(8,128)(2,1)} %param.11) | copy-start | bytes 884740
  17.5 13.4 %copy-start.11 = (s32[32]{0:T(128)S(1)}, s32[32]{0:T(128)}, u32[]{:S(2)}) copy-start(s32[32]{0:T(128)} %table_ref.3) | copy-start | bytes 388
  17.5 13.4 %copy-start = (bf16[16,512,128]{2,1,0:T(8,128)(2,1)S(1)}, bf16[16,512,128]{2,1,0:T(8,128)(2,1)}, u32[]{:S(2)}) copy-start(bf16[16,512,128]{2,1,0:T(8,128)(2,1)} %constant_dynamic-slice_fusion.8.refs_5_) | copy-start | bytes 6291460
  18.7 12.2 %collective-permute-start.9 = (bf16[288,640]{1,0:T(8,128)(2,1)S(1)}, bf16[288,640]{1,0:T(8,128)(2,1)S(1)}, u32[]{:S(2)}, u32[]{:S(2)}) collective-permute-start(bf16[288,640]{1,0:T(8,128)(2,1)S(1)} %pad_maximum_fusion.refs_0_), channel_id=1, source_target_pairs={{0,1},{1,0},{2,3},{3,2},{4,5},{5,4},{6,7},{7,6},{8,9},{9,8},{10,11... | collective-permute-start | bytes 1105928 | tf_op jit(solution)/shard_map/ppermute | solution.py:310
  19.3 5.7 %collective-permute-start.6 = (bf16[72,640]{1,0:T(8,128)(2,1)}, bf16[72,640]{1,0:T(8,128)(2,1)S(1)}, u32[]{:S(2)}, u32[]{:S(2)}) collective-permute-start(bf16[72,640]{1,0:T(8,128)(2,1)} %collective-permute-done), channel_id=1, source_target_pairs={{0,2},{1,3},{2,0},{3,1},{4,6},{5,7},{6,4},{7,5},{8,10},{9,11},{10,... | collective-permute-start | bytes 276488 | tf_op jit(solution)/shard_map/ppermute | solution.py:310
  19.5 7.4 %collective-permute-start.7 = (bf16[72,640]{1,0:T(8,128)(2,1)S(1)}, bf16[72,640]{1,0:T(8,128)(2,1)S(1)}, u32[]{:S(2)}, u32[]{:S(2)}) collective-permute-start(bf16[72,640]{1,0:T(8,128)(2,1)S(1)} %collective-permute-done.1), channel_id=1, source_target_pairs={{0,2},{1,3},{2,0},{3,1},{4,6},{5,7},{6,4},{7,5},{8,10},{9,11},{10,... | collective-permute-start | bytes 276488 | tf_op jit(solution)/shard_map/ppermute | solution.py:310
  21.3 6.8 %collective-permute-start.8 = (bf16[72,640]{1,0:T(8,128)(2,1)S(1)}, bf16[72,640]{1,0:T(8,128)(2,1)S(1)}, u32[]{:S(2)}, u32[]{:S(2)}) collective-permute-start(bf16[72,640]{1,0:T(8,128)(2,1)S(1)} %collective-permute-done.2), channel_id=1, source_target_pairs={{0,2},{1,3},{2,0},{3,1},{4,6},{5,7},{6,4},{7,5},{8,10},{9,11},{10,... | collective-permute-start | bytes 276488 | tf_op jit(solution)/shard_map/ppermute | solution.py:310
  28.1 2.8 %collective-permute-start.10 = (bf16[288,640]{1,0:T(8,128)(2,1)S(1)}, bf16[288,640]{1,0:T(8,128)(2,1)S(1)}, u32[]{:S(2)}, u32[]{:S(2)}) collective-permute-start(bf16[288,640]{1,0:T(8,128)(2,1)S(1)} %constant_dynamic-update-slice_fusion.refs_1_), channel_id=1, source_target_pairs={{0,1},{1,0},{2,3},{3,2},{4,5},{5,4},{6,7},{7,6},{8,9},{9,8},{10,11... | collective-permute-start | bytes 1105928 | tf_op jit(solution)/shard_map/ppermute | solution.py:310
  28.2 2.7 %collective-permute-start.3 = (bf16[16,72,128]{2,1,0:T(8,128)(2,1)S(1)}, bf16[16,72,128]{2,1,0:T(8,128)(2,1)S(1)}, u32[]{:S(2)}, u32[]{:S(2)}) collective-permute-start(bf16[16,72,128]{2,1,0:T(8,128)(2,1)S(1)} %bitcast.49), channel_id=1, source_target_pairs={{0,1},{1,0},{2,3},{3,2},{4,5},{5,4},{6,7},{7,6},{8,9},{9,8},{10,11... | collective-permute-start | bytes 884744 | tf_op jit(solution)/shard_map/ppermute | solution.py:310
  28.8 1.8 %collective-permute-start.4 = (bf16[1024,72]{1,0:T(8,128)(2,1)S(1)}, bf16[1024,72]{1,0:T(8,128)(2,1)S(1)}, u32[]{:S(2)}, u32[]{:S(2)}) collective-permute-start(bf16[1024,72]{1,0:T(8,128)(2,1)S(1)} %get-tuple-element.28), channel_id=1, source_target_pairs={{0,1},{1,0},{2,3},{3,2},{4,5},{5,4},{6,7},{7,6},{8,9},{9,8},{10,11... | collective-permute-start | bytes 442376 | tf_op jit(solution)/shard_map/ppermute | solution.py:310
  30.6 36.5 %collective-permute-start.20 = (bf16[224,2048]{1,0:T(8,128)(2,1)S(1)}, bf16[224,2048]{1,0:T(8,128)(2,1)S(1)}, u32[]{:S(2)}, u32[]{:S(2)}) collective-permute-start(bf16[224,2048]{1,0:T(8,128)(2,1)S(1)} %get-tuple-element.25.refs_4_.refs_8_), channel_id=1, source_target_pairs={{0,2},{1,3},{2,0},{3,1},{4,6},{5,7},{6,4},{7,5},{8,10},{9,11},{10,... | collective-permute-start | bytes 2752520 | tf_op jit(solution)/shard_map/ppermute | solution.py:310
  31.0 1.6 %copy-start.1 = (bf16[16,128,512]{2,1,0:T(8,128)(2,1)S(1)}, bf16[16,128,512]{2,1,0:T(8,128)(2,1)}, u32[]{:S(2)}) copy-start(bf16[16,128,512]{2,1,0:T(8,128)(2,1)} %constant_dynamic-slice_fusion.9.refs_4_) | copy-start | bytes 6291460
  32.6 35.9 %copy-start.15 = (f32[3584]{0:T(1024)S(1)}, f32[3584]{0:T(1024)}, u32[]{:S(2)}) copy-start(f32[3584]{0:T(1024)} %param.18) | copy-start | bytes 43012
  39.9 13.6 %collective-permute-start.12 = (bf16[144,1024]{1,0:T(8,128)(2,1)S(1)}, bf16[144,1024]{1,0:T(8,128)(2,1)S(1)}, u32[]{:S(2)}, u32[]{:S(2)}) collective-permute-start(bf16[144,1024]{1,0:T(8,128)(2,1)S(1)} %attend.3.refs_1_), channel_id=1, source_target_pairs={{0,4},{1,5},{2,6},{3,7},{4,0},{5,1},{6,2},{7,3},{8,12},{9,13},{10,... | collective-permute-start | bytes 884744 | tf_op jit(solution)/shard_map/ppermute | solution.py:313
  40.9 43.0 %collective-permute-start.21 = (bf16[224,2048]{1,0:T(8,128)(2,1)S(1)}, bf16[224,2048]{1,0:T(8,128)(2,1)}, u32[]{:S(2)}, u32[]{:S(2)}) collective-permute-start(bf16[224,2048]{1,0:T(8,128)(2,1)S(1)} %collective-permute-done.19.refs_5_.refs_9_), channel_id=1, source_target_pairs={{0,2},{1,3},{2,0},{3,1},{4,6},{5,7},{6,4},{7,5},{8,10},{9,11},{10,... | collective-permute-start | bytes 2752520 | tf_op jit(solution)/shard_map/ppermute | solution.py:310
  42.4 1.0 copy-start.7
  50.8 8.3 %collective-permute-start.11 = (bf16[144,1024]{1,0:T(8,128)(2,1)S(1)}, bf16[144,1024]{1,0:T(8,128)(2,1)S(1)}, u32[]{:S(2)}, u32[]{:S(2)}) collective-permute-start(bf16[144,1024]{1,0:T(8,128)(2,1)S(1)} %attend.2.refs_0_), channel_id=1, source_target_pairs={{0,4},{1,5},{2,6},{3,7},{4,0},{5,1},{6,2},{7,3},{8,12},{9,13},{10,... | collective-permute-start | bytes 884744 | tf_op jit(solution)/shard_map/ppermute | solution.py:313
  52.2 8.9 %collective-permute-start.17 = (bf16[144,1024]{1,0:T(8,128)(2,1)S(1)}, bf16[144,1024]{1,0:T(8,128)(2,1)}, u32[]{:S(2)}, u32[]{:S(2)}) collective-permute-start(bf16[144,1024]{1,0:T(8,128)(2,1)S(1)} %attend.3.refs_1_), channel_id=1, source_target_pairs={{4,8},{5,9},{6,10},{7,11},{8,4},{9,5},{10,6},{11,7},{20,24},{21,25... | collective-permute-start | bytes 884744 | tf_op jit(solution)/shard_map/ppermute | solution.py:313
  53.6 9.7 %collective-permute-start.14 = (bf16[144,1024]{1,0:T(8,128)(2,1)S(1)}, bf16[144,1024]{1,0:T(8,128)(2,1)}, u32[]{:S(2)}, u32[]{:S(2)}) collective-permute-start(bf16[144,1024]{1,0:T(8,128)(2,1)S(1)} %collective-permute-done.12.refs_3_), channel_id=1, source_target_pairs={{4,8},{5,9},{6,10},{7,11},{8,4},{9,5},{10,6},{11,7},{20,24},{21,25... | collective-permute-start | bytes 884744 | tf_op jit(solution)/shard_map/ppermute | solution.py:313
  59.0 5.5 %collective-permute-start.13 = (bf16[144,1024]{1,0:T(8,128)(2,1)S(1)}, bf16[144,1024]{1,0:T(8,128)(2,1)}, u32[]{:S(2)}, u32[]{:S(2)}) collective-permute-start(bf16[144,1024]{1,0:T(8,128)(2,1)S(1)} %collective-permute-done.11.refs_2_), channel_id=1, source_target_pairs={{4,8},{5,9},{6,10},{7,11},{8,4},{9,5},{10,6},{11,7},{20,24},{21,25... | collective-permute-start | bytes 884744 | tf_op jit(solution)/shard_map/ppermute | solution.py:313
  60.4 0.7 copy-start.4
  61.1 4.7 %collective-permute-start.15 = (bf16[144,1024]{1,0:T(8,128)(2,1)S(1)}, bf16[144,1024]{1,0:T(8,128)(2,1)}, u32[]{:S(2)}, u32[]{:S(2)}) collective-permute-start(bf16[144,1024]{1,0:T(8,128)(2,1)S(1)} %attend.2.refs_0_), channel_id=1, source_target_pairs={{4,8},{5,9},{6,10},{7,11},{8,4},{9,5},{10,6},{11,7},{20,24},{21,25... | collective-permute-start | bytes 884744 | tf_op jit(solution)/shard_map/ppermute | solution.py:313
  62.5 0.7 copy-start.2
  63.2 14.3 %collective-permute-start.27 = (bf16[144,1024]{1,0:T(8,128)(2,1)}, bf16[144,1024]{1,0:T(8,128)(2,1)}, u32[]{:S(2)}, u32[]{:S(2)}) collective-permute-start(bf16[144,1024]{1,0:T(8,128)(2,1)} %collective-permute-done.14.refs_5_), channel_id=1, source_target_pairs={{4,0},{5,1},{6,2},{7,3},{8,12},{9,13},{10,14},{11,15},{20,16},{21,... | collective-permute-start | bytes 884744 | tf_op jit(solution)/shard_map/ppermute | solution.py:313
  64.5 19.4 %collective-permute-start.26 = (bf16[144,1024]{1,0:T(8,128)(2,1)}, bf16[144,1024]{1,0:T(8,128)(2,1)}, u32[]{:S(2)}, u32[]{:S(2)}) collective-permute-start(bf16[144,1024]{1,0:T(8,128)(2,1)} %collective-permute-done.13.refs_4_), channel_id=1, source_target_pairs={{4,0},{5,1},{6,2},{7,3},{8,12},{9,13},{10,14},{11,15},{20,16},{21,... | collective-permute-start | bytes 884744 | tf_op jit(solution)/shard_map/ppermute | solution.py:313
  65.8 26.0 %collective-permute-start.18 = (bf16[144,1024]{1,0:T(8,128)(2,1)}, bf16[144,1024]{1,0:T(8,128)(2,1)}, u32[]{:S(2)}, u32[]{:S(2)}) collective-permute-start(bf16[144,1024]{1,0:T(8,128)(2,1)} %collective-permute-done.17.refs_1_), channel_id=1, source_target_pairs={{4,0},{5,1},{6,2},{7,3},{8,12},{9,13},{10,14},{11,15},{20,16},{21,... | collective-permute-start | bytes 884744 | tf_op jit(solution)/shard_map/ppermute | solution.py:313
  67.2 29.2 %collective-permute-start.16 = (bf16[144,1024]{1,0:T(8,128)(2,1)}, bf16[144,1024]{1,0:T(8,128)(2,1)}, u32[]{:S(2)}, u32[]{:S(2)}) collective-permute-start(bf16[144,1024]{1,0:T(8,128)(2,1)} %collective-permute-done.15.refs_0_), channel_id=1, source_target_pairs={{4,0},{5,1},{6,2},{7,3},{8,12},{9,13},{10,14},{11,15},{20,16},{21,... | collective-permute-start | bytes 884744 | tf_op jit(solution)/shard_map/ppermute | solution.py:313
  68.5 1.0 copy-start.3
  69.5 1.0 copy-start.5
  86.8 13.5 %collective-permute-start.28 = (bf16[4,1,72,224]{3,2,1,0:T(8,128)(2,1)S(1)}, bf16[4,1,72,224]{3,2,1,0:T(8,128)(2,1)S(1)}, u32[]{:S(2)}, u32[]{:S(2)}) collective-permute-start(bf16[4,1,72,224]{3,2,1,0:T(8,128)(2,1)S(1)} %get-tuple-element.23), channel_id=1, source_target_pairs={{0,1},{1,0},{2,3},{3,2},{4,5},{5,4},{6,7},{7,6},{8,9},{9,8},{10,11... | collective-permute-start | bytes 387080 | tf_op jit(solution)/shard_map/ppermute | solution.py:310
  100.3 2.0 %collective-permute-start.22 = (bf16[4,3,72,224]{3,2,1,0:T(8,128)(2,1)S(1)}, bf16[4,3,72,224]{3,2,1,0:T(8,128)(2,1)S(1)}, u32[]{:S(2)}, u32[]{:S(2)}) collective-permute-start(bf16[4,3,72,224]{3,2,1,0:T(8,128)(2,1)S(1)} %get-tuple-element.21), channel_id=1, source_target_pairs={{0,1},{1,0},{2,3},{3,2},{4,5},{5,4},{6,7},{7,6},{8,9},{9,8},{10,11... | collective-permute-start | bytes 1161224 | tf_op jit(solution)/shard_map/ppermute | solution.py:310
  100.6 4.9 %collective-permute-start.29 = (bf16[4,1,36,224]{3,2,0,1:T(8,128)(2,1)S(1)}, bf16[4,1,36,224]{3,2,0,1:T(8,128)(2,1)S(1)}, u32[]{:S(2)}, u32[]{:S(2)}) collective-permute-start(bf16[4,1,36,224]{3,2,0,1:T(8,128)(2,1)S(1)} %bitcast.51), channel_id=1, source_target_pairs={{0,16},{16,0},{1,17},{17,1},{2,18},{18,2},{3,19},{19,3},{4,20},{20... | collective-permute-start | bytes 193544 | tf_op jit(solution)/shard_map/ppermute | solution.py:384
  102.8 15.4 %copy-start.8 = (bf16[36,3584]{1,0:T(8,128)(2,1)S(1)}, bf16[36,3584]{1,0:T(8,128)(2,1)}, u32[]{:S(2)}) copy-start(bf16[36,3584]{1,0:T(8,128)(2,1)} %res_ref.1) | copy-start | bytes 774148
  103.0 8.1 %collective-permute-start.23 = (bf16[4,3,36,224]{3,2,0,1:T(8,128)(2,1)S(1)}, bf16[4,3,36,224]{3,2,0,1:T(8,128)(2,1)S(1)}, u32[]{:S(2)}, u32[]{:S(2)}) collective-permute-start(bf16[4,3,36,224]{3,2,0,1:T(8,128)(2,1)S(1)} %bitcast.50), channel_id=1, source_target_pairs={{0,16},{16,0},{1,17},{17,1},{2,18},{18,2},{3,19},{19,3},{4,20},{20... | collective-permute-start | bytes 580616 | tf_op jit(solution)/shard_map/ppermute | solution.py:384
  105.6 9.3 %collective-permute-start.30 = (bf16[4,36,224]{2,1,0:T(8,128)(2,1)S(1)}, bf16[4,36,224]{2,1,0:T(8,128)(2,1)S(1)}, u32[]{:S(2)}, u32[]{:S(2)}) collective-permute-start(bf16[4,36,224]{2,1,0:T(8,128)(2,1)S(1)} %fusion.3), channel_id=1, source_target_pairs={{0,12},{1,13},{2,14},{3,15},{4,8},{5,9},{6,10},{7,11},{8,4},{9,5},... | collective-permute-start | bytes 193544 | tf_op jit(solution)/shard_map/ppermute | solution.py:310
  111.2 5.4 %collective-permute-start.24 = (bf16[4,36,224]{2,1,0:T(8,128)(2,1)S(1)}, bf16[4,36,224]{2,1,0:T(8,128)(2,1)S(1)}, u32[]{:S(2)}, u32[]{:S(2)}) collective-permute-start(bf16[4,36,224]{2,1,0:T(8,128)(2,1)S(1)} %get-tuple-element.35), channel_id=1, source_target_pairs={{0,4},{1,5},{2,6},{3,7},{4,0},{5,1},{6,2},{7,3},{8,12},{9,13},{10,... | collective-permute-start | bytes 193544 | tf_op jit(solution)/shard_map/ppermute | solution.py:310
  111.3 6.9 %collective-permute-start.25 = (bf16[4,36,224]{2,1,0:T(8,128)(2,1)S(1)}, bf16[4,36,224]{2,1,0:T(8,128)(2,1)S(1)}, u32[]{:S(2)}, u32[]{:S(2)}) collective-permute-start(bf16[4,36,224]{2,1,0:T(8,128)(2,1)S(1)} %get-tuple-element.34), channel_id=1, source_target_pairs={{0,8},{1,9},{2,10},{3,11},{4,12},{5,13},{6,14},{7,15},{8,0},{9,1},... | collective-permute-start | bytes 193544 | tf_op jit(solution)/shard_map/ppermute | solution.py:310
where the time goes:
time: 121 us; the launch traced here: 120 us
  waiting for transfers between devices  40.5 us (33%)
  starting transfers between devices  35.6 us (29%)
  Pallas kernels  24.4 us (20%)
  local copies, waits for them, and re-layouts  17 us (14%)
  other arithmetic  1.51 us (1%)
    ppermute x10, waiting for transfers between devices, move(): lax.ppermute(x, 'seq', [(4 * a + r, 4 * b + r) for a, b in pairs for r in...  26.2 us
    ppermute x19, starting transfers between devices, swap(): return lax.ppermute(x, 'seq', [(i, i ^ bit) for i in range(n_seq)])  19.5 us
    pallas_call x2, Pallas kernels, attend(): pl.pallas_call(attend_kernel, grid_spec=pltpu.PrefetchScalarGridSpec(num_...  14.8 us
    ppermute x10, starting transfers between devices, move(): lax.ppermute(x, 'seq', [(4 * a + r, 4 * b + r) for a, b in pairs for r in...  13.1 us
    ppermute x19, waiting for transfers between devices, swap(): return lax.ppermute(x, 'seq', [(i, i ^ bit) for i in range(n_seq)])  10.7 us
    unnamed x39, local copies, waits for them, and re-layouts  8.66 us
    pallas_call x3, Pallas kernels, project(): pl.pallas_call(functools.partial(project_kernel, len(fixed), len(options)...  7.62 us
    ppermute x2, waiting for transfers between devices, reduce(): got = lax.ppermute(send.astype(bf16), 'heads', [(0, 1), (1, 0)])  3.62 us
  transfers between devices with their start and end apart: 31, of which 13 were waited for; matrix products, arithmetic and copies ran while one was open for 9% of the time, Pallas kernels for 19%

commit v1 on v0

--- a/solution.py
+++ b/solution.py
@@ -189,7 +189,7 @@
     )(me, table, *nope, *rope, *parts, wk, wv)
 
 
-def project_kernel(plain, choice, skip, prev, me_ref, *refs):
+def project_kernel(plain, choice, prev, me_ref, *refs):
     refs = list(refs)
 
     def take(count):
@@ -197,7 +197,7 @@
         return out
 
     fixed = [take(2) for _ in range(plain)]
-    options = [take(2) for _ in range(choice)]
+    options = [[take(2) for _ in range(choice)] for _ in range(2)]
     weights = take(len(refs) - 2 - (2 if prev else 0))
     before = take(2) if prev else []
     keep_ref, send_ref = refs
@@ -205,8 +205,8 @@
     for old, new in zip(before, refs):
         new[: old.shape[0], : old.shape[1]] = old[...]
 
-    def emit(blocks, at, first):
-        for j in range(first, len(weights)):
+    def emit(blocks, at, pieces):
+        for j in pieces:
             total = 0.0
             for g in range(2):
                 rows = jnp.concatenate([block[g][...] for block in blocks], axis=0)
@@ -222,31 +222,37 @@
                 keep_ref[j, at + n] = total[start : start + tok]
                 send_ref[j, at + n] = total[start + tok : start + 2 * tok].astype(send_ref.dtype)
 
-    if fixed:
-        emit(fixed, 0, skip)
+    pieces = range(len(weights))
+    if prev:
+        done, count = before[0].shape[:2]
+        emit(fixed, 0, pieces[done:])
+        emit(fixed[count:], count, pieces[:done])
+    elif fixed:
+        emit(fixed, 0, pieces)
     slab = me_ref[0] >> 2
     inner = (slab == 1) | (slab == 2)
     for n, option in enumerate(options):
-
-        @pl.when(inner if n == 0 else ~inner)
-        def _():
-            emit([option], plain, 0)
-
-
-def project(me, fixed, options, weights, tok, skip=0, before=()):
-    count = len(fixed) + bool(options)
+        if option:
+
+            @pl.when(inner if n == 0 else ~inner)
+            def _():
+                emit(option, plain, pieces)
+
+
+def project(me, fixed, options, weights, tok, before=()):
+    count = len(fixed) + len(options) // 2
     shape = (len(weights), count, tok, weights[0].shape[0])
     operands = [ref for block in [*fixed, *options] for ref in block] + list(weights) + list(before)
     vmem = pl.BlockSpec(memory_space=pltpu.VMEM)
     return pl.pallas_call(
-        functools.partial(project_kernel, len(fixed), len(options), skip, bool(before)),
+        functools.partial(project_kernel, len(fixed), len(options) // 2, bool(before)),
         in_specs=[pl.BlockSpec(memory_space=pltpu.SMEM)] + [vmem] * len(operands),
         out_specs=[vmem, vmem],
         out_shape=[
             jax.ShapeDtypeStruct(shape, jnp.float32),
             jax.ShapeDtypeStruct(shape, jnp.bfloat16),
         ],
-        compiler_params=pltpu.CompilerParams(vmem_limit_bytes=16 * 1024 * 1024),
+        compiler_params=pltpu.CompilerParams(vmem_limit_bytes=6 * 1024 * 1024),
         cost_estimate=pl.CostEstimate(
             flops=4 * tok * count * sum(w.size for w in weights),
             bytes_accessed=0,
@@ -256,6 +262,60 @@
     )(me, *operands)
 
 
+def halve_kernel(x_ref, keep_ref, other_ref, mine_ref, send_ref):
+    pieces, count, tok, _ = keep_ref.shape
+    for j in range(pieces):
+        for n in range(count):
+            total = keep_ref[j, n] + other_ref[j ^ 1, n].astype(jnp.float32)
+            low, high = total[: tok // 2], total[tok // 2 :]
+
+            @pl.when(x_ref[0] == 0)
+            def _():
+                mine_ref[j, n] = low
+                send_ref[j, n] = high.astype(send_ref.dtype)
+
+            @pl.when(x_ref[0] != 0)
+            def _():
+                mine_ref[j, n] = high
+                send_ref[j, n] = low.astype(send_ref.dtype)
+
+
+def join_kernel(mine_ref, got_ref, *outs):
+    for n, out in enumerate(outs):
+        for j in range(mine_ref.shape[0]):
+            out[j] = (mine_ref[j, n] + got_ref[j, n].astype(jnp.float32)).astype(out.dtype)
+
+
+def halve(x, keep, other):
+    pieces, count, tok, cols = keep.shape
+    vmem = pl.BlockSpec(memory_space=pltpu.VMEM)
+    shape = (pieces, count, tok // 2, cols)
+    return pl.pallas_call(
+        halve_kernel,
+        in_specs=[pl.BlockSpec(memory_space=pltpu.SMEM), vmem, vmem],
+        out_specs=[vmem, vmem],
+        out_shape=[
+            jax.ShapeDtypeStruct(shape, jnp.float32),
+            jax.ShapeDtypeStruct(shape, jnp.bfloat16),
+        ],
+        compiler_params=pltpu.CompilerParams(vmem_limit_bytes=4 * 1024 * 1024),
+        name="halve",
+    )(x, keep, other)
+
+
+def join(mine, got):
+    pieces, count, tok, cols = mine.shape
+    vmem = pl.BlockSpec(memory_space=pltpu.VMEM)
+    return pl.pallas_call(
+        join_kernel,
+        in_specs=[vmem, vmem],
+        out_specs=[vmem] * count,
+        out_shape=[jax.ShapeDtypeStruct((pieces, tok, cols), jnp.bfloat16)] * count,
+        compiler_params=pltpu.CompilerParams(vmem_limit_bytes=4 * 1024 * 1024),
+        name="join",
+    )(mine, got)
+
+
 def finish_kernel(me_ref, res_ref, gain_ref, *refs):
     pieces = refs[:-3]
     new_ref, normed_ref, hidden_ref = refs[-3:]
@@ -263,7 +323,7 @@
     cols = pieces[0].shape[2]
     wide = 4 * cols
     for k, piece in enumerate(pieces):
-        at = pl.multiple_of(me_ref[1 + k] * wide, wide)
+        at = pl.multiple_of(((me >> 2) ^ k) * wide, wide)
         for case in range(4):
 
             @pl.when((me & 3) == case)
@@ -278,7 +338,7 @@
     normed_ref[...] = (hidden * scale * gain_ref[...]).astype(normed_ref.dtype)
 
 
-def finish(places, residual, gain, pieces):
+def finish(me, residual, gain, pieces):
     vmem = pl.BlockSpec(memory_space=pltpu.VMEM)
     out = jax.ShapeDtypeStruct(residual.shape, jnp.bfloat16)
     return pl.pallas_call(
@@ -289,7 +349,7 @@
         scratch_shapes=[pltpu.VMEM(residual.shape, jnp.float32)],
         compiler_params=pltpu.CompilerParams(vmem_limit_bytes=8 * 1024 * 1024),
         name="finish",
-    )(places, residual, gain, *pieces)
+    )(me, residual, gain, *pieces)
 
 
 def per_device(
@@ -332,7 +392,11 @@
 
     wk = lax.dynamic_slice_in_dim(absorb_key, core * half, half, 0)
     wv = lax.dynamic_slice_in_dim(absorb_value, core * half, half, 0)
-    along, wk, wv, *own = lax.optimization_barrier((along, wk, wv, nope[0], rotary[0]))
+    head_group = lax.axis_index("heads").astype(jnp.int32).reshape(1)
+    gain = norm_gain[None, :]
+    along, head_group, gain, *own = lax.optimization_barrier(
+        (along, head_group, gain, nope[0], rotary[0])
+    )
     nope, rotary = (own[0], nope[1]), (own[1], rotary[1])
     parts = [along, across, swap(along, 1), swap(across, 1)]
 
@@ -363,54 +427,47 @@
             step_heads,
         )
         if line:
-            near = move(mixed, [(0, 1), (1, 0), (2, 3), (3, 2)])
-            mid = move(mixed, [(1, 2), (2, 1)])
-            out2 = move(mid, [(1, 0), (2, 3)])
+            near, opposite = swap(mixed, 4), swap(mixed, 12)
             far = move(near, [(1, 2), (2, 1)])
-            out3 = move(far, [(1, 0), (2, 3)])
-            blocks.append([mixed, near, far, out2, mid, out3])
+            out = move(opposite, [(1, 0), (2, 3)])
+            blocks.append([mixed, near, opposite, far, out])
         else:
             blocks.append([mixed] + [swap(mixed, 4 * k) for k in range(1, depth_z)])
 
     def reduce(keep, send):
         count = keep.shape[1]
         other = swap(send, 1)
+        if n_heads == 2:
+            mine, send = halve(head_group, keep, other)
+            got = lax.ppermute(send, "heads", [(0, 1), (1, 0)])
+            return list(join(mine, got))
         total = keep + jnp.stack([other[j ^ 1] for j in range(4)]).astype(f32)
-        if n_heads == 2:
-            x = lax.axis_index("heads")
-            total = total.reshape(4, count, 2, tok // 2, cols)
-            keep = lax.dynamic_index_in_dim(total, x, 2, keepdims=False)
-            send = lax.dynamic_index_in_dim(total, 1 - x, 2, keepdims=False)
-            got = lax.ppermute(send.astype(bf16), "heads", [(0, 1), (1, 0)])
-            total = keep + got.astype(f32)
-        else:
-            total = lax.psum_scatter(total.astype(bf16), "heads", scatter_dimension=2, tiled=True)
-        total = total.astype(bf16)
+        total = lax.psum_scatter(total.astype(bf16), "heads", scatter_dimension=2, tiled=True)
         return [total[:, n] for n in range(count)]
 
     if line:
-        mixed, near, far, out2, mid, out3 = zip(*blocks)
+        mixed, near, opposite, far, out = zip(*blocks)
         me1 = me.reshape(1)
         first = project(me1, [mixed, near], [], weights[:2], tok)
-        early = project(me1, [mixed, near], [far, out2], weights, tok, 2, first)
-        late = project(me1, [], [mid, out3], weights, tok)
+        early = project(me1, [mixed, near, opposite], [], weights, tok, first)
+        late = project(me1, [], [far, out], weights, tok)
         mine = reduce(*early) + reduce(*late)
+        mine[2], mine[3] = mine[3], mine[2]
     else:
         rows = jnp.stack([jnp.concatenate(parts, axis=1) for parts in zip(*blocks)])
         total = jnp.einsum("zti,joi->jzto", rows, jnp.stack(weights), preferred_element_type=f32)
         mine = reduce(total[:, :, :tok], total[:, :, tok:].astype(bf16))
     pieces = [mine[0]] + [swap(mine[k], 4 * k) for k in range(1, depth_z)]
+    if 4 * cols % 128 == 0:
+        return tuple(finish(me.reshape(1), residual, gain, pieces))
     places = slab ^ jnp.arange(depth_z, dtype=jnp.int32)
-    if 4 * cols % 128 == 0:
-        places = jnp.concatenate([me.reshape(1), places])
-        return tuple(finish(places, residual, norm_gain[None, :], pieces))
     order = jnp.arange(depth_z, dtype=jnp.int32)
     order = jnp.sum(jnp.where(places[None, :] == order[:, None], order[None, :], 0), axis=1)
     columns = jnp.take(jnp.stack(pieces), order, axis=0)
     columns = jnp.take(columns, jnp.arange(4, dtype=jnp.int32) ^ (me & 3), axis=1)
     hidden = residual.astype(f32) + jnp.moveaxis(columns, 2, 0).reshape(residual.shape).astype(f32)
     scale = lax.rsqrt(jnp.mean(hidden * hidden, axis=1, keepdims=True) + 1e-06)
-    return (hidden.astype(bf16), (hidden * scale * norm_gain[None, :]).astype(bf16))
+    return (hidden.astype(bf16), (hidden * scale * gain).astype(bf16))
 
 
 def solution(mesh):

time: 121 us -> 121 us (level)
  waiting for transfers between devices: 40.5 us -> 57.6 us
  local copies, waits for them, and re-layouts: 17 us -> 9.48 us
  starting transfers between devices: 35.6 us -> 31.3 us
  Pallas kernels: 24.4 us -> 20.4 us
    ppermute x19 -> x23, waiting for transfers between devices: 10.7 us -> 29.2 us  [swap(): return lax.ppermute(x, 'seq', [(i, i ^ bit) for i in range(n_seq)])]
    ppermute x10 -> x4, starting transfers between devices: 13.1 us -> 3.94 us  [move(): lax.ppermute(x, 'seq', [(4 * a + r, 4 * b + r) for a, b in pairs for r in...]
    ppermute x10 -> x4, waiting for transfers between devices: 26.2 us -> 21 us  [move(): lax.ppermute(x, 'seq', [(4 * a + r, 4 * b + r) for a, b in pairs for r in...]
    unnamed x39 -> x17, local copies, waits for them, and re-layouts: 8.66 us -> 3.49 us
    ppermute x19 -> x23, starting transfers between devices: 19.5 us -> 24.6 us  [swap(): return lax.ppermute(x, 'seq', [(i, i ^ bit) for i in range(n_seq)])]
    ppermute x2, waiting for transfers between devices: 3.62 us -> 7.42 us  [reduce(): got = lax.ppermute(send, 'heads', [(0, 1), (1, 0)])]
    pallas_call x3, Pallas kernels: 7.62 us -> 3.86 us  [project(): pl.pallas_call(functools.partial(project_kernel, len(fixed), len(options)...]
    dynamic_slice x1, local copies, waits for them, and re-layouts: 3.31 us -> 0.19 us  [per_device(): wv = lax.dynamic_slice_in_dim(absorb_value, core * half, half, 0)]
  transfers between devices with their start and end apart: 31 -> 29, of which waited for: 13 -> 14; matrix products, arithmetic and copies ran while one was open for 9% -> 7% of each run, Pallas kernels for 19% -> 14%
where the time goes in v1:
time: 121 us
  waiting for transfers between devices  57.6 us (48%)
  starting transfers between devices  31.3 us (26%)
  Pallas kernels  20.4 us (17%)
  local copies, waits for them, and re-layouts  9.48 us (8%)
    ppermute x23, waiting for transfers between devices, swap(): return lax.ppermute(x, 'seq', [(i, i ^ bit) for i in range(n_seq)])  29.2 us
    ppermute x23, starting transfers between devices, swap(): return lax.ppermute(x, 'seq', [(i, i ^ bit) for i in range(n_seq)])  24.6 us
    ppermute x4, waiting for transfers between devices, move(): lax.ppermute(x, 'seq', [(4 * a + r, 4 * b + r) for a, b in pairs for r in...  21 us
    pallas_call x2, Pallas kernels, attend(): pl.pallas_call(attend_kernel, grid_spec=pltpu.PrefetchScalarGridSpec(num_...  14.8 us
    ppermute x2, waiting for transfers between devices, reduce(): got = lax.ppermute(send, 'heads', [(0, 1), (1, 0)])  7.42 us
    ppermute x4, starting transfers between devices, move(): lax.ppermute(x, 'seq', [(4 * a + r, 4 * b + r) for a, b in pairs for r in...  3.94 us
    pallas_call x3, Pallas kernels, project(): pl.pallas_call(functools.partial(project_kernel, len(fixed), len(options)...  3.86 us
    unnamed x17, local copies, waits for them, and re-layouts  3.49 us
  transfers between devices with their start and end apart: 29, of which 14 were waited for; matrix products, arithmetic and copies ran while one was open for 7% of the time, Pallas kernels for 14%

profile of v1, /device:TPU:0, one launch (start us, length us, event | category | flops | bytes accessed | tf_op | source)
XLA Modules:
  0.0 120.7 jit_solution(1570043430245196777)
XLA Ops:
  0.6 0.9 copy-done.1
  1.5 0.7 copy-done.2
  2.4 5.1 %collective-permute-start.2 = (bf16[72,640]{1,0:T(8,128)(2,1)S(1)}, bf16[72,640]{1,0:T(8,128)(2,1)S(1)}, u32[]{:S(2)}, u32[]{:S(2)}) collective-permute-start(bf16[72,640]{1,0:T(8,128)(2,1)S(1)} %pack.1), channel_id=1, source_target_pairs={{0,12},{1,13},{2,14},{3,15},{4,8},{5,9},{6,10},{7,11},{8,4},{9,5},... | collective-permute-start | bytes 276488 | tf_op jit(solution)/shard_map/ppermute | solution.py:370
  7.5 0.6 collective-permute-start
  8.2 1.7 %collective-permute-start.5 = (bf16[72,640]{1,0:T(8,128)(2,1)S(1)}, bf16[72,640]{1,0:T(8,128)(2,1)}, u32[]{:S(2)}, u32[]{:S(2)}) collective-permute-start(bf16[72,640]{1,0:T(8,128)(2,1)S(1)} %pack.1), channel_id=1, source_target_pairs={{0,2},{1,3},{2,0},{3,1},{4,6},{5,7},{6,4},{7,5},{8,10},{9,11},{10,... | collective-permute-start | bytes 276488 | tf_op jit(solution)/shard_map/ppermute | solution.py:370
  9.8 1.6 %dynamic-slice_bitcast_fusion = (bf16[224,2048]{1,0:T(8,128)(2,1)S(1)}, bf16[224,2048]{1,0:T(8,128)(2,1)S(1)}) fusion(bf16[4096,224]{0,1:T(8,128)(2,1)} %param.16, s32[]{:T(128)S(6)} %select_n.25, s32[]{:T(128)S(6)} %select_n.24), kind=kLoop, calls=%fused_computation | loop fusion | bytes 3670024 | tf_op jit(solution)/shard_map/dynamic_slice | solution.py:407
  11.6 1.2 constant_dynamic-slice_fusion.3
  12.8 1.1 constant_dynamic-slice_fusion.2
  13.9 1.5 %collective-permute-done.1 = bf16[72,640]{1,0:T(8,128)(2,1)} collective-permute-done((bf16[72,640]{1,0:T(8,128)(2,1)S(1)}, bf16[72,640]{1,0:T(8,128)(2,1)}, u32[]{:S(2)}, u32[]{:S(2)}) %collective-permute-start.1) | collective-permute-done | bytes 92192 | tf_op jit(solution)/shard_map/ppermute | solution.py:370
  15.4 1.0 pad_maximum_fusion.refs_0_
  16.4 1.6 %collective-permute-start.6 = (bf16[72,640]{1,0:T(8,128)(2,1)}, bf16[72,640]{1,0:T(8,128)(2,1)S(1)}, u32[]{:S(2)}, u32[]{:S(2)}) collective-permute-start(bf16[72,640]{1,0:T(8,128)(2,1)} %collective-permute-done), channel_id=1, source_target_pairs={{0,2},{1,3},{2,0},{3,1},{4,6},{5,7},{6,4},{7,5},{8,10},{9,11},{10,... | collective-permute-start | bytes 276488 | tf_op jit(solution)/shard_map/ppermute | solution.py:370
  18.5 1.5 %collective-permute-start.8 = (bf16[72,640]{1,0:T(8,128)(2,1)S(1)}, bf16[72,640]{1,0:T(8,128)(2,1)S(1)}, u32[]{:S(2)}, u32[]{:S(2)}) collective-permute-start(bf16[72,640]{1,0:T(8,128)(2,1)S(1)} %collective-permute-done.2), channel_id=1, source_target_pairs={{0,2},{1,3},{2,0},{3,1},{4,6},{5,7},{6,4},{7,5},{8,10},{9,11},{10,... | collective-permute-start | bytes 276488 | tf_op jit(solution)/shard_map/ppermute | solution.py:370
  20.0 0.9 constant_dynamic-update-slice_fusion.3
  20.9 1.3 %collective-permute-done.6 = bf16[72,640]{1,0:T(8,128)(2,1)S(1)} collective-permute-done((bf16[72,640]{1,0:T(8,128)(2,1)}, bf16[72,640]{1,0:T(8,128)(2,1)S(1)}, u32[]{:S(2)}, u32[]{:S(2)}) %collective-permute-start.6) | collective-permute-done | bytes 92192 | tf_op jit(solution)/shard_map/ppermute | solution.py:370
  22.3 2.0 %collective-permute-done.7 = bf16[72,640]{1,0:T(8,128)(2,1)S(1)} collective-permute-done((bf16[72,640]{1,0:T(8,128)(2,1)}, bf16[72,640]{1,0:T(8,128)(2,1)S(1)}, u32[]{:S(2)}, u32[]{:S(2)}) %collective-permute-start.7) | collective-permute-done | bytes 92192 | tf_op jit(solution)/shard_map/ppermute | solution.py:370
  24.2 1.4 %collective-permute-done.8 = bf16[72,640]{1,0:T(8,128)(2,1)S(1)} collective-permute-done((bf16[72,640]{1,0:T(8,128)(2,1)S(1)}, bf16[72,640]{1,0:T(8,128)(2,1)S(1)}, u32[]{:S(2)}, u32[]{:S(2)}) %collective-permute-start.8) | collective-permute-done | bytes 92192 | tf_op jit(solution)/shard_map/ppermute | solution.py:370
  25.8 0.6 collective-permute-start.3
  26.5 1.9 %constant_dynamic-slice_fusion.1.refs_4_ = bf16[16,128,512]{2,1,0:T(8,128)(2,1)S(1)} fusion(bf16[32,128,512]{2,1,0:T(8,128)(2,1)} %param.14, s32[]{:T(128)S(6)} %select_n.20), kind=kLoop, calls=%fused_computation.10 | loop fusion | bytes 4194308 | tf_op jit(solution)/shard_map/dynamic_slice | solution.py:393
  28.4 0.8 copy-done.4
  29.4 1.6 %collective-permute-start.16 = (bf16[224,2048]{1,0:T(8,128)(2,1)S(1)}, bf16[224,2048]{1,0:T(8,128)(2,1)S(1)}, u32[]{:S(2)}, u32[]{:S(2)}) collective-permute-start(bf16[224,2048]{1,0:T(8,128)(2,1)S(1)} %get-tuple-element.39.refs_4_.refs_6_), channel_id=1, source_target_pairs={{0,2},{1,3},{2,0},{3,1},{4,6},{5,7},{6,4},{7,5},{8,10},{9,11},{10,... | collective-permute-start | bytes 2752520 | tf_op jit(solution)/shard_map/ppermute | solution.py:370
  31.5 7.4 %attend.2.refs_0_ = bf16[144,1024]{1,0:T(8,128)(2,1)S(1)} custom-call(s32[1]{0:T(128)} %bitcast.me_ref, s32[32]{0:T(128)S(1)} %copy-done.3, bf16[16,72,128]{2,1,0:T(8,128)(2,1)S(1)} %bitcast.16, bf16[16,72,128]{2,1,0:T(8,128)(2,1)S(1)} %collective-permute-done.3.nope1_ref, bf16[1024,72]{1,0:T(8,128)(2,1)S(1)} %get-tuple-element.23.rope0_ref, ...), custom_call_target="tpu_custom_call" | custom-call | flops 3057647616 | bytes 2392064 | tf_op jit(solution)/shard_map/attend/pallas_call | solution.py:156
  38.9 0.7 collective-permute-start.11
  39.7 7.4 %attend.3.refs_1_ = bf16[144,1024]{1,0:T(8,128)(2,1)S(1)} custom-call(s32[1]{0:T(128)} %bitcast.me_ref, s32[32]{0:T(128)S(1)} %copy-done.3, bf16[16,72,128]{2,1,0:T(8,128)(2,1)S(1)} %bitcast.17, bf16[16,72,128]{2,1,0:T(8,128)(2,1)S(1)} %collective-permute-done.3.nope1_ref, bf16[1024,72]{1,0:T(8,128)(2,1)S(1)} %get-tuple-element.23.rope0_ref, ...), custom_call_target="tpu_custom_call" | custom-call | flops 3057647616 | bytes 2392064 | tf_op jit(solution)/shard_map/attend/pallas_call | solution.py:156
  47.0 1.4 %collective-permute-start.12 = (bf16[144,1024]{1,0:T(8,128)(2,1)S(1)}, bf16[144,1024]{1,0:T(8,128)(2,1)S(1)}, u32[]{:S(2)}, u32[]{:S(2)}) collective-permute-start(bf16[144,1024]{1,0:T(8,128)(2,1)S(1)} %attend.3.refs_1_), channel_id=1, source_target_pairs={{0,4},{1,5},{2,6},{3,7},{4,0},{5,1},{6,2},{7,3},{8,12},{9,13},{10,... | collective-permute-start | bytes 884744 | tf_op jit(solution)/shard_map/ppermute | solution.py:370
  48.5 2.6 %collective-permute-start.13 = (bf16[144,1024]{1,0:T(8,128)(2,1)S(1)}, bf16[144,1024]{1,0:T(8,128)(2,1)S(1)}, u32[]{:S(2)}, u32[]{:S(2)}) collective-permute-start(bf16[144,1024]{1,0:T(8,128)(2,1)S(1)} %attend.2.refs_0_), channel_id=1, source_target_pairs={{0,12},{1,13},{2,14},{3,15},{4,8},{5,9},{6,10},{7,11},{8,4},{9,5},... | collective-permute-start | bytes 884744 | tf_op jit(solution)/shard_map/ppermute | solution.py:370
  51.1 1.2 %collective-permute-start.14 = (bf16[144,1024]{1,0:T(8,128)(2,1)S(1)}, bf16[144,1024]{1,0:T(8,128)(2,1)S(1)}, u32[]{:S(2)}, u32[]{:S(2)}) collective-permute-start(bf16[144,1024]{1,0:T(8,128)(2,1)S(1)} %attend.3.refs_1_), channel_id=1, source_target_pairs={{0,12},{1,13},{2,14},{3,15},{4,8},{5,9},{6,10},{7,11},{8,4},{9,5},... | collective-permute-start | bytes 884744 | tf_op jit(solution)/shard_map/ppermute | solution.py:370
  52.3 3.6 %collective-permute-done.12.refs_3_ = bf16[144,1024]{1,0:T(8,128)(2,1)S(1)} collective-permute-done((bf16[144,1024]{1,0:T(8,128)(2,1)S(1)}, bf16[144,1024]{1,0:T(8,128)(2,1)S(1)}, u32[]{:S(2)}, u32[]{:S(2)}) %collective-permute-start.12) | collective-permute-done | bytes 294944 | tf_op jit(solution)/shard_map/ppermute | solution.py:370
  55.9 0.8 project.3
  56.7 8.7 %collective-permute-done.13.refs_4_ = bf16[144,1024]{1,0:T(8,128)(2,1)S(1)} collective-permute-done((bf16[144,1024]{1,0:T(8,128)(2,1)S(1)}, bf16[144,1024]{1,0:T(8,128)(2,1)S(1)}, u32[]{:S(2)}, u32[]{:S(2)}) %collective-permute-start.13) | collective-permute-done | bytes 294944 | tf_op jit(solution)/shard_map/ppermute | solution.py:370
  65.3 4.5 %collective-permute-done.14.refs_5_ = bf16[144,1024]{1,0:T(8,128)(2,1)S(1)} collective-permute-done((bf16[144,1024]{1,0:T(8,128)(2,1)S(1)}, bf16[144,1024]{1,0:T(8,128)(2,1)S(1)}, u32[]{:S(2)}, u32[]{:S(2)}) %collective-permute-start.14) | collective-permute-done | bytes 294944 | tf_op jit(solution)/shard_map/ppermute | solution.py:370
  69.9 1.6 %collective-permute-done.17.refs_9_.refs_7_ = bf16[224,2048]{1,0:T(8,128)(2,1)S(1)} collective-permute-done((bf16[224,2048]{1,0:T(8,128)(2,1)S(1)}, bf16[224,2048]{1,0:T(8,128)(2,1)S(1)}, u32[]{:S(2)}, u32[]{:S(2)}) %collective-permute-start.17) | collective-permute-done | bytes 917536 | tf_op jit(solution)/shard_map/ppermute | solution.py:370
  71.4 1.7 %project.4 = (f32[4,3,72,224]{3,2,1,0:T(8,128)S(1)}, bf16[4,3,72,224]{3,2,1,0:T(8,128)(2,1)S(1)}) custom-call(s32[1]{0:T(128)} %bitcast.me_ref, bf16[144,1024]{1,0:T(8,128)(2,1)S(1)} %attend.2.refs_0_, bf16[144,1024]{1,0:T(8,128)(2,1)S(1)} %attend.3.refs_1_, bf16[144,1024]{1,0:T(8,128)(2,1)S(1)} %collective-permute-done.11.refs_2_, ...), custom_call_target="tpu_custom_call" | custom-call | flops 1585446912 | tf_op jit(solution)/shard_map/project/pallas_call | solution.py:247
  73.2 0.7 collective-permute-start.21
  73.9 0.7 collective-permute-start.22
  74.6 1.3 %collective-permute-start.23 = (bf16[144,1024]{1,0:T(8,128)(2,1)S(1)}, bf16[144,1024]{1,0:T(8,128)(2,1)S(1)}, u32[]{:S(2)}, u32[]{:S(2)}) collective-permute-start(bf16[144,1024]{1,0:T(8,128)(2,1)S(1)} %collective-permute-done.13.refs_4_), channel_id=1, source_target_pairs={{4,0},{5,1},{6,2},{7,3},{8,12},{9,13},{10,14},{11,15},{20,16},{21,... | collective-permute-start | bytes 884744 | tf_op jit(solution)/shard_map/ppermute | solution.py:373
  75.9 1.3 %collective-permute-start.24 = (bf16[144,1024]{1,0:T(8,128)(2,1)S(1)}, bf16[144,1024]{1,0:T(8,128)(2,1)S(1)}, u32[]{:S(2)}, u32[]{:S(2)}) collective-permute-start(bf16[144,1024]{1,0:T(8,128)(2,1)S(1)} %collective-permute-done.14.refs_5_), channel_id=1, source_target_pairs={{4,0},{5,1},{6,2},{7,3},{8,12},{9,13},{10,14},{11,15},{20,16},{21,... | collective-permute-start | bytes 884744 | tf_op jit(solution)/shard_map/ppermute | solution.py:373
  77.2 15.5 %collective-permute-done.23.refs_2_ = bf16[144,1024]{1,0:T(8,128)(2,1)S(1)} collective-permute-done((bf16[144,1024]{1,0:T(8,128)(2,1)S(1)}, bf16[144,1024]{1,0:T(8,128)(2,1)S(1)}, u32[]{:S(2)}, u32[]{:S(2)}) %collective-permute-start.23) | collective-permute-done | bytes 294944 | tf_op jit(solution)/shard_map/ppermute | solution.py:373
  92.7 5.6 %collective-permute-done.24.refs_3_ = bf16[144,1024]{1,0:T(8,128)(2,1)S(1)} collective-permute-done((bf16[144,1024]{1,0:T(8,128)(2,1)S(1)}, bf16[144,1024]{1,0:T(8,128)(2,1)S(1)}, u32[]{:S(2)}, u32[]{:S(2)}) %collective-permute-start.24) | collective-permute-done | bytes 294944 | tf_op jit(solution)/shard_map/ppermute | solution.py:373
  98.2 1.4 %project.5 = (f32[4,1,72,224]{3,2,1,0:T(8,128)S(1)}, bf16[4,1,72,224]{3,2,1,0:T(8,128)(2,1)S(1)}) custom-call(s32[1]{0:T(128)} %bitcast.me_ref, bf16[144,1024]{1,0:T(8,128)(2,1)S(1)} %collective-permute-done.21.refs_0_, bf16[144,1024]{1,0:T(8,128)(2,1)S(1)} %collective-permute-done.22.refs_1_, bf16[144,1024]{1,0:T(8,128)(2,1)S(1)} %collective-permute-done.23.refs_2_, ...), custom_call_target="tpu_custom_call" | custom-call | flops 528482304 | tf_op jit(solution)/shard_map/project/pallas_call | solution.py:247
  100.0 1.6 %collective-permute-start.19 = (bf16[4,3,36,224]{3,2,1,0:T(8,128)(2,1)S(1)}, bf16[4,3,36,224]{3,2,1,0:T(8,128)(2,1)S(1)}, u32[]{:S(2)}, u32[]{:S(2)}) collective-permute-start(bf16[4,3,36,224]{3,2,1,0:T(8,128)(2,1)S(1)} %get-tuple-element.30), channel_id=1, source_target_pairs={{0,16},{16,0},{1,17},{17,1},{2,18},{18,2},{3,19},{19,3},{4,20},{20... | collective-permute-start | bytes 580616 | tf_op jit(solution)/shard_map/ppermute | solution.py:442
  101.6 1.1 collective-permute-start.26
  102.7 7.4 %collective-permute-done.26.got_ref = bf16[4,1,36,224]{3,2,1,0:T(8,128)(2,1)S(1)} collective-permute-done((bf16[4,1,36,224]{3,2,1,0:T(8,128)(2,1)S(1)}, bf16[4,1,36,224]{3,2,1,0:T(8,128)(2,1)S(1)}, u32[]{:S(2)}, u32[]{:S(2)}) %collective-permute-start.26) | collective-permute-done | bytes 64544 | tf_op jit(solution)/shard_map/ppermute | solution.py:442
  110.6 2.5 %collective-permute-start.20 = (bf16[4,36,224]{2,1,0:T(8,128)(2,1)S(1)}, bf16[4,36,224]{2,1,0:T(8,128)(2,1)S(1)}, u32[]{:S(2)}, u32[]{:S(2)}) collective-permute-start(bf16[4,36,224]{2,1,0:T(8,128)(2,1)S(1)} %get-tuple-element.32), channel_id=1, source_target_pairs={{0,4},{1,5},{2,6},{3,7},{4,0},{5,1},{6,2},{7,3},{8,12},{9,13},{10,... | collective-permute-start | bytes 193544 | tf_op jit(solution)/shard_map/ppermute | solution.py:370
  113.2 1.5 %collective-permute-start.28 = (bf16[4,36,224]{2,1,0:T(8,128)(2,1)S(1)}, bf16[4,36,224]{2,1,0:T(8,128)(2,1)S(1)}, u32[]{:S(2)}, u32[]{:S(2)}) collective-permute-start(bf16[4,36,224]{2,1,0:T(8,128)(2,1)S(1)} %get-tuple-element.37), channel_id=1, source_target_pairs={{0,12},{1,13},{2,14},{3,15},{4,8},{5,9},{6,10},{7,11},{8,4},{9,5},... | collective-permute-start | bytes 193544 | tf_op jit(solution)/shard_map/ppermute | solution.py:370
  114.7 2.1 %collective-permute-done.27.refs_2_ = bf16[4,36,224]{2,1,0:T(8,128)(2,1)S(1)} collective-permute-done((bf16[4,36,224]{2,1,0:T(8,128)(2,1)S(1)}, bf16[4,36,224]{2,1,0:T(8,128)(2,1)S(1)}, u32[]{:S(2)}, u32[]{:S(2)}) %collective-permute-start.27) | collective-permute-done | bytes 64544 | tf_op jit(solution)/shard_map/ppermute | solution.py:370
  116.9 0.7 collective-permute-done.20.refs_1_
  117.6 1.8 %collective-permute-done.28.refs_3_ = bf16[4,36,224]{2,1,0:T(8,128)(2,1)S(1)} collective-permute-done((bf16[4,36,224]{2,1,0:T(8,128)(2,1)S(1)}, bf16[4,36,224]{2,1,0:T(8,128)(2,1)S(1)}, u32[]{:S(2)}, u32[]{:S(2)}) %collective-permute-start.28) | collective-permute-done | bytes 64544 | tf_op jit(solution)/shard_map/ppermute | solution.py:370
  119.4 1.3 %finish.1 = (bf16[36,3584]{1,0:T(8,128)(2,1)}, bf16[36,3584]{1,0:T(8,128)(2,1)}) custom-call(s32[1]{0:T(128)} %bitcast.me_ref, bf16[36,3584]{1,0:T(8,128)(2,1)S(1)} %copy-done, f32[1,3584]{1,0:T(1,128)S(1)} %broadcast_in_dim.3.gain_ref, bf16[4,36,224]{2,1,0:T(8,128)(2,1)S(1)} %get-tuple-element.31.refs_0_, ...), custom_call_target="tpu_custom_call" | custom-call | tf_op jit(solution)/shard_map/finish/pallas_call | solution.py:344
  (46 shorter events, 2.9 us)
Async XLA Ops:
  0.6 0.9 copy-start.1
  1.5 0.7 copy-start.2
  2.2 9.3 %copy-start.5 = (f32[3584]{0:T(1024)S(1)}, f32[3584]{0:T(1024)}, u32[]{:S(2)}) copy-start(f32[3584]{0:T(1024)} %param.18) | copy-start | bytes 43012
  2.4 11.5 %collective-permute-start.2 = (bf16[72,640]{1,0:T(8,128)(2,1)S(1)}, bf16[72,640]{1,0:T(8,128)(2,1)S(1)}, u32[]{:S(2)}, u32[]{:S(2)}) collective-permute-start(bf16[72,640]{1,0:T(8,128)(2,1)S(1)} %pack.1), channel_id=1, source_target_pairs={{0,12},{1,13},{2,14},{3,15},{4,8},{5,9},{6,10},{7,11},{8,4},{9,5},... | collective-permute-start | bytes 276488 | tf_op jit(solution)/shard_map/ppermute | solution.py:370
  7.5 7.8 %collective-permute-start.1 = (bf16[72,640]{1,0:T(8,128)(2,1)S(1)}, bf16[72,640]{1,0:T(8,128)(2,1)}, u32[]{:S(2)}, u32[]{:S(2)}) collective-permute-start(bf16[72,640]{1,0:T(8,128)(2,1)S(1)} %pack.1), channel_id=1, source_target_pairs={{0,8},{1,9},{2,10},{3,11},{4,12},{5,13},{6,14},{7,15},{8,0},{9,1},... | collective-permute-start | bytes 276488 | tf_op jit(solution)/shard_map/ppermute | solution.py:370
  7.5 7.8 %collective-permute-start = (bf16[72,640]{1,0:T(8,128)(2,1)S(1)}, bf16[72,640]{1,0:T(8,128)(2,1)}, u32[]{:S(2)}, u32[]{:S(2)}) collective-permute-start(bf16[72,640]{1,0:T(8,128)(2,1)S(1)} %pack.1), channel_id=1, source_target_pairs={{0,4},{1,5},{2,6},{3,7},{4,0},{5,1},{6,2},{7,3},{8,12},{9,13},{10,... | collective-permute-start | bytes 276488 | tf_op jit(solution)/shard_map/ppermute | solution.py:370
  8.2 10.3 %collective-permute-start.5 = (bf16[72,640]{1,0:T(8,128)(2,1)S(1)}, bf16[72,640]{1,0:T(8,128)(2,1)}, u32[]{:S(2)}, u32[]{:S(2)}) collective-permute-start(bf16[72,640]{1,0:T(8,128)(2,1)S(1)} %pack.1), channel_id=1, source_target_pairs={{0,2},{1,3},{2,0},{3,1},{4,6},{5,7},{6,4},{7,5},{8,10},{9,11},{10,... | collective-permute-start | bytes 276488 | tf_op jit(solution)/shard_map/ppermute | solution.py:370
  11.5 19.5 %collective-permute-start.15 = (bf16[224,2048]{1,0:T(8,128)(2,1)S(1)}, bf16[224,2048]{1,0:T(8,128)(2,1)S(1)}, u32[]{:S(2)}, u32[]{:S(2)}) collective-permute-start(bf16[224,2048]{1,0:T(8,128)(2,1)S(1)} %get-tuple-element.38), channel_id=1, source_target_pairs={{0,1},{1,0},{2,3},{3,2},{4,5},{5,4},{6,7},{7,6},{8,9},{9,8},{10,11... | collective-permute-start | bytes 2752520 | tf_op jit(solution)/shard_map/ppermute | solution.py:370
  16.4 15.2 %collective-permute-start.9 = (bf16[288,640]{1,0:T(8,128)(2,1)S(1)}, bf16[288,640]{1,0:T(8,128)(2,1)S(1)}, u32[]{:S(2)}, u32[]{:S(2)}) collective-permute-start(bf16[288,640]{1,0:T(8,128)(2,1)S(1)} %pad_maximum_fusion.refs_0_), channel_id=1, source_target_pairs={{0,1},{1,0},{2,3},{3,2},{4,5},{5,4},{6,7},{7,6},{8,9},{9,8},{10,11... | collective-permute-start | bytes 1105928 | tf_op jit(solution)/shard_map/ppermute | solution.py:370
  16.4 5.8 %collective-permute-start.6 = (bf16[72,640]{1,0:T(8,128)(2,1)}, bf16[72,640]{1,0:T(8,128)(2,1)S(1)}, u32[]{:S(2)}, u32[]{:S(2)}) collective-permute-start(bf16[72,640]{1,0:T(8,128)(2,1)} %collective-permute-done), channel_id=1, source_target_pairs={{0,2},{1,3},{2,0},{3,1},{4,6},{5,7},{6,4},{7,5},{8,10},{9,11},{10,... | collective-permute-start | bytes 276488 | tf_op jit(solution)/shard_map/ppermute | solution.py:370
  18.0 6.2 %collective-permute-start.7 = (bf16[72,640]{1,0:T(8,128)(2,1)}, bf16[72,640]{1,0:T(8,128)(2,1)S(1)}, u32[]{:S(2)}, u32[]{:S(2)}) collective-permute-start(bf16[72,640]{1,0:T(8,128)(2,1)} %collective-permute-done.1), channel_id=1, source_target_pairs={{0,2},{1,3},{2,0},{3,1},{4,6},{5,7},{6,4},{7,5},{8,10},{9,11},{10,... | collective-permute-start | bytes 276488 | tf_op jit(solution)/shard_map/ppermute | solution.py:370
  18.5 7.1 %collective-permute-start.8 = (bf16[72,640]{1,0:T(8,128)(2,1)S(1)}, bf16[72,640]{1,0:T(8,128)(2,1)S(1)}, u32[]{:S(2)}, u32[]{:S(2)}) collective-permute-start(bf16[72,640]{1,0:T(8,128)(2,1)S(1)} %collective-permute-done.2), channel_id=1, source_target_pairs={{0,2},{1,3},{2,0},{3,1},{4,6},{5,7},{6,4},{7,5},{8,10},{9,11},{10,... | collective-permute-start | bytes 276488 | tf_op jit(solution)/shard_map/ppermute | solution.py:370
  25.7 5.9 %collective-permute-start.10 = (bf16[288,640]{1,0:T(8,128)(2,1)S(1)}, bf16[288,640]{1,0:T(8,128)(2,1)S(1)}, u32[]{:S(2)}, u32[]{:S(2)}) collective-permute-start(bf16[288,640]{1,0:T(8,128)(2,1)S(1)} %constant_dynamic-update-slice_fusion.refs_1_), channel_id=1, source_target_pairs={{0,1},{1,0},{2,3},{3,2},{4,5},{5,4},{6,7},{7,6},{8,9},{9,8},{10,11... | collective-permute-start | bytes 1105928 | tf_op jit(solution)/shard_map/ppermute | solution.py:370
  25.8 5.7 %collective-permute-start.3 = (bf16[16,72,128]{2,1,0:T(8,128)(2,1)S(1)}, bf16[16,72,128]{2,1,0:T(8,128)(2,1)S(1)}, u32[]{:S(2)}, u32[]{:S(2)}) collective-permute-start(bf16[16,72,128]{2,1,0:T(8,128)(2,1)S(1)} %bitcast.20), channel_id=1, source_target_pairs={{0,1},{1,0},{2,3},{3,2},{4,5},{5,4},{6,7},{7,6},{8,9},{9,8},{10,11... | collective-permute-start | bytes 884744 | tf_op jit(solution)/shard_map/ppermute | solution.py:370
  26.4 2.8 %copy-start.4 = (bf16[32,512,128]{2,1,0:T(8,128)(2,1)S(1)}, bf16[32,512,128]{2,1,0:T(8,128)(2,1)}, u32[]{:S(2)}) copy-start(bf16[32,512,128]{2,1,0:T(8,128)(2,1)} %param.15) | copy-start | bytes 12582916
  26.4 3.0 %collective-permute-start.4 = (bf16[1024,72]{1,0:T(8,128)(2,1)S(1)}, bf16[1024,72]{1,0:T(8,128)(2,1)S(1)}, u32[]{:S(2)}, u32[]{:S(2)}) collective-permute-start(bf16[1024,72]{1,0:T(8,128)(2,1)S(1)} %get-tuple-element.42), channel_id=1, source_target_pairs={{0,1},{1,0},{2,3},{3,2},{4,5},{5,4},{6,7},{7,6},{8,9},{9,8},{10,11... | collective-permute-start | bytes 442376 | tf_op jit(solution)/shard_map/ppermute | solution.py:370
  29.2 2.3 %copy-start.3 = (s32[32]{0:T(128)S(1)}, s32[32]{0:T(128)}, u32[]{:S(2)}) copy-start(s32[32]{0:T(128)} %table_ref.3) | copy-start | bytes 388
  29.4 40.4 %collective-permute-start.16 = (bf16[224,2048]{1,0:T(8,128)(2,1)S(1)}, bf16[224,2048]{1,0:T(8,128)(2,1)S(1)}, u32[]{:S(2)}, u32[]{:S(2)}) collective-permute-start(bf16[224,2048]{1,0:T(8,128)(2,1)S(1)} %get-tuple-element.39.refs_4_.refs_6_), channel_id=1, source_target_pairs={{0,2},{1,3},{2,0},{3,1},{4,6},{5,7},{6,4},{7,5},{8,10},{9,11},{10,... | collective-permute-start | bytes 2752520 | tf_op jit(solution)/shard_map/ppermute | solution.py:370
  31.0 40.4 %collective-permute-start.17 = (bf16[224,2048]{1,0:T(8,128)(2,1)S(1)}, bf16[224,2048]{1,0:T(8,128)(2,1)S(1)}, u32[]{:S(2)}, u32[]{:S(2)}) collective-permute-start(bf16[224,2048]{1,0:T(8,128)(2,1)S(1)} %collective-permute-done.15.refs_5_.refs_7_), channel_id=1, source_target_pairs={{0,2},{1,3},{2,0},{3,1},{4,6},{5,7},{6,4},{7,5},{8,10},{9,11},{10,... | collective-permute-start | bytes 2752520 | tf_op jit(solution)/shard_map/ppermute | solution.py:370
  38.9 12.1 %collective-permute-start.11 = (bf16[144,1024]{1,0:T(8,128)(2,1)S(1)}, bf16[144,1024]{1,0:T(8,128)(2,1)S(1)}, u32[]{:S(2)}, u32[]{:S(2)}) collective-permute-start(bf16[144,1024]{1,0:T(8,128)(2,1)S(1)} %attend.2.refs_0_), channel_id=1, source_target_pairs={{0,4},{1,5},{2,6},{3,7},{4,0},{5,1},{6,2},{7,3},{8,12},{9,13},{10,... | collective-permute-start | bytes 884744 | tf_op jit(solution)/shard_map/ppermute | solution.py:370
  47.0 8.8 %collective-permute-start.12 = (bf16[144,1024]{1,0:T(8,128)(2,1)S(1)}, bf16[144,1024]{1,0:T(8,128)(2,1)S(1)}, u32[]{:S(2)}, u32[]{:S(2)}) collective-permute-start(bf16[144,1024]{1,0:T(8,128)(2,1)S(1)} %attend.3.refs_1_), channel_id=1, source_target_pairs={{0,4},{1,5},{2,6},{3,7},{4,0},{5,1},{6,2},{7,3},{8,12},{9,13},{10,... | collective-permute-start | bytes 884744 | tf_op jit(solution)/shard_map/ppermute | solution.py:370
  48.5 16.9 %collective-permute-start.13 = (bf16[144,1024]{1,0:T(8,128)(2,1)S(1)}, bf16[144,1024]{1,0:T(8,128)(2,1)S(1)}, u32[]{:S(2)}, u32[]{:S(2)}) collective-permute-start(bf16[144,1024]{1,0:T(8,128)(2,1)S(1)} %attend.2.refs_0_), channel_id=1, source_target_pairs={{0,12},{1,13},{2,14},{3,15},{4,8},{5,9},{6,10},{7,11},{8,4},{9,5},... | collective-permute-start | bytes 884744 | tf_op jit(solution)/shard_map/ppermute | solution.py:370
  51.1 18.8 %collective-permute-start.14 = (bf16[144,1024]{1,0:T(8,128)(2,1)S(1)}, bf16[144,1024]{1,0:T(8,128)(2,1)S(1)}, u32[]{:S(2)}, u32[]{:S(2)}) collective-permute-start(bf16[144,1024]{1,0:T(8,128)(2,1)S(1)} %attend.3.refs_1_), channel_id=1, source_target_pairs={{0,12},{1,13},{2,14},{3,15},{4,8},{5,9},{6,10},{7,11},{8,4},{9,5},... | collective-permute-start | bytes 884744 | tf_op jit(solution)/shard_map/ppermute | solution.py:370
  73.1 26.6 %collective-permute-start.18 = (bf16[4,3,72,224]{3,2,1,0:T(8,128)(2,1)S(1)}, bf16[4,3,72,224]{3,2,1,0:T(8,128)(2,1)S(1)}, u32[]{:S(2)}, u32[]{:S(2)}) collective-permute-start(bf16[4,3,72,224]{3,2,1,0:T(8,128)(2,1)S(1)} %get-tuple-element.28), channel_id=1, source_target_pairs={{0,1},{1,0},{2,3},{3,2},{4,5},{5,4},{6,7},{7,6},{8,9},{9,8},{10,11... | collective-permute-start | bytes 1161224 | tf_op jit(solution)/shard_map/ppermute | solution.py:370
  73.2 4.0 %collective-permute-start.21 = (bf16[144,1024]{1,0:T(8,128)(2,1)S(1)}, bf16[144,1024]{1,0:T(8,128)(2,1)S(1)}, u32[]{:S(2)}, u32[]{:S(2)}) collective-permute-start(bf16[144,1024]{1,0:T(8,128)(2,1)S(1)} %collective-permute-done.11.refs_2_), channel_id=1, source_target_pairs={{4,8},{5,9},{6,10},{7,11},{8,4},{9,5},{10,6},{11,7},{20,24},{21,25... | collective-permute-start | bytes 884744 | tf_op jit(solution)/shard_map/ppermute | solution.py:373
  73.9 3.3 %collective-permute-start.22 = (bf16[144,1024]{1,0:T(8,128)(2,1)S(1)}, bf16[144,1024]{1,0:T(8,128)(2,1)S(1)}, u32[]{:S(2)}, u32[]{:S(2)}) collective-permute-start(bf16[144,1024]{1,0:T(8,128)(2,1)S(1)} %collective-permute-done.12.refs_3_), channel_id=1, source_target_pairs={{4,8},{5,9},{6,10},{7,11},{8,4},{9,5},{10,6},{11,7},{20,24},{21,25... | collective-permute-start | bytes 884744 | tf_op jit(solution)/shard_map/ppermute | solution.py:373
  74.6 18.1 %collective-permute-start.23 = (bf16[144,1024]{1,0:T(8,128)(2,1)S(1)}, bf16[144,1024]{1,0:T(8,128)(2,1)S(1)}, u32[]{:S(2)}, u32[]{:S(2)}) collective-permute-start(bf16[144,1024]{1,0:T(8,128)(2,1)S(1)} %collective-permute-done.13.refs_4_), channel_id=1, source_target_pairs={{4,0},{5,1},{6,2},{7,3},{8,12},{9,13},{10,14},{11,15},{20,16},{21,... | collective-permute-start | bytes 884744 | tf_op jit(solution)/shard_map/ppermute | solution.py:373
  75.9 22.4 %collective-permute-start.24 = (bf16[144,1024]{1,0:T(8,128)(2,1)S(1)}, bf16[144,1024]{1,0:T(8,128)(2,1)S(1)}, u32[]{:S(2)}, u32[]{:S(2)}) collective-permute-start(bf16[144,1024]{1,0:T(8,128)(2,1)S(1)} %collective-permute-done.14.refs_5_), channel_id=1, source_target_pairs={{4,0},{5,1},{6,2},{7,3},{8,12},{9,13},{10,14},{11,15},{20,16},{21,... | collective-permute-start | bytes 884744 | tf_op jit(solution)/shard_map/ppermute | solution.py:373
  99.6 19.8 %copy-start = (bf16[36,3584]{1,0:T(8,128)(2,1)S(1)}, bf16[36,3584]{1,0:T(8,128)(2,1)}, u32[]{:S(2)}) copy-start(bf16[36,3584]{1,0:T(8,128)(2,1)} %res_ref.1) | copy-start | bytes 774148
  99.6 1.9 %collective-permute-start.25 = (bf16[4,1,72,224]{3,2,1,0:T(8,128)(2,1)S(1)}, bf16[4,1,72,224]{3,2,1,0:T(8,128)(2,1)S(1)}, u32[]{:S(2)}, u32[]{:S(2)}) collective-permute-start(bf16[4,1,72,224]{3,2,1,0:T(8,128)(2,1)S(1)} %get-tuple-element.34), channel_id=1, source_target_pairs={{0,1},{1,0},{2,3},{3,2},{4,5},{5,4},{6,7},{7,6},{8,9},{9,8},{10,11... | collective-permute-start | bytes 387080 | tf_op jit(solution)/shard_map/ppermute | solution.py:370
  100.0 10.6 %collective-permute-start.19 = (bf16[4,3,36,224]{3,2,1,0:T(8,128)(2,1)S(1)}, bf16[4,3,36,224]{3,2,1,0:T(8,128)(2,1)S(1)}, u32[]{:S(2)}, u32[]{:S(2)}) collective-permute-start(bf16[4,3,36,224]{3,2,1,0:T(8,128)(2,1)S(1)} %get-tuple-element.30), channel_id=1, source_target_pairs={{0,16},{16,0},{1,17},{17,1},{2,18},{18,2},{3,19},{19,3},{4,20},{20... | collective-permute-start | bytes 580616 | tf_op jit(solution)/shard_map/ppermute | solution.py:442
  101.6 8.5 %collective-permute-start.26 = (bf16[4,1,36,224]{3,2,1,0:T(8,128)(2,1)S(1)}, bf16[4,1,36,224]{3,2,1,0:T(8,128)(2,1)S(1)}, u32[]{:S(2)}, u32[]{:S(2)}) collective-permute-start(bf16[4,1,36,224]{3,2,1,0:T(8,128)(2,1)S(1)} %get-tuple-element.36), channel_id=1, source_target_pairs={{0,16},{16,0},{1,17},{17,1},{2,18},{18,2},{3,19},{19,3},{4,20},{20... | collective-permute-start | bytes 193544 | tf_op jit(solution)/shard_map/ppermute | solution.py:442
  110.1 6.7 %collective-permute-start.27 = (bf16[4,36,224]{2,1,0:T(8,128)(2,1)S(1)}, bf16[4,36,224]{2,1,0:T(8,128)(2,1)S(1)}, u32[]{:S(2)}, u32[]{:S(2)}) collective-permute-start(bf16[4,36,224]{2,1,0:T(8,128)(2,1)S(1)} %join.3), channel_id=1, source_target_pairs={{0,8},{1,9},{2,10},{3,11},{4,12},{5,13},{6,14},{7,15},{8,0},{9,1},... | collective-permute-start | bytes 193544 | tf_op jit(solution)/shard_map/ppermute | solution.py:370
  110.6 7.0 %collective-permute-start.20 = (bf16[4,36,224]{2,1,0:T(8,128)(2,1)S(1)}, bf16[4,36,224]{2,1,0:T(8,128)(2,1)S(1)}, u32[]{:S(2)}, u32[]{:S(2)}) collective-permute-start(bf16[4,36,224]{2,1,0:T(8,128)(2,1)S(1)} %get-tuple-element.32), channel_id=1, source_target_pairs={{0,4},{1,5},{2,6},{3,7},{4,0},{5,1},{6,2},{7,3},{8,12},{9,13},{10,... | collective-permute-start | bytes 193544 | tf_op jit(solution)/shard_map/ppermute | solution.py:370
  113.2 6.2 %collective-permute-start.28 = (bf16[4,36,224]{2,1,0:T(8,128)(2,1)S(1)}, bf16[4,36,224]{2,1,0:T(8,128)(2,1)S(1)}, u32[]{:S(2)}, u32[]{:S(2)}) collective-permute-start(bf16[4,36,224]{2,1,0:T(8,128)(2,1)S(1)} %get-tuple-element.37), channel_id=1, source_target_pairs={{0,12},{1,13},{2,14},{3,15},{4,8},{5,9},{6,10},{7,11},{8,4},{9,5},... | collective-permute-start | bytes 193544 | tf_op jit(solution)/shard_map/ppermute | solution.py:370

commit v2 on v1

--- a/solution.py
+++ b/solution.py
@@ -11,12 +11,19 @@
 LOG2E = 1.4426950408889634
 
 
-def pack_kernel(lat_ref, rope_ref, out_ref):
+def pack_kernel(lat_ref, rope_ref, out_ref, held_ref, sem):
     width = lat_ref.shape[1]
-    out_ref[:, :width] = lat_ref[...]
-    rope = rope_ref[...].astype(jnp.float32).T
+    copies = [
+        pltpu.make_async_copy(lat_ref, out_ref.at[:, pl.ds(0, width)], sem.at[0]),
+        pltpu.make_async_copy(rope_ref, held_ref, sem.at[1]),
+    ]
+    for copy in copies:
+        copy.start()
+    copies[1].wait()
+    rope = held_ref[...].astype(jnp.float32).T
     both = jnp.concatenate([rope, rope], axis=1)
     out_ref[:, width:] = both.astype(out_ref.dtype)
+    copies[0].wait()
 
 
 def pack(latent, rope_t):
@@ -25,6 +32,9 @@
         out_shape=jax.ShapeDtypeStruct(
             (latent.shape[0], latent.shape[1] + 2 * rope_t.shape[0]), latent.dtype
         ),
+        in_specs=[pl.BlockSpec(memory_space=pltpu.HBM)] * 2,
+        out_specs=pl.BlockSpec(memory_space=pltpu.VMEM),
+        scratch_shapes=[pltpu.VMEM(rope_t.shape, rope_t.dtype), pltpu.SemaphoreType.DMA((2,))],
         compiler_params=pltpu.CompilerParams(vmem_limit_bytes=8 * 1024 * 1024),
         name="pack",
     )(latent, rope_t)
@@ -226,7 +236,8 @@
     if prev:
         done, count = before[0].shape[:2]
         emit(fixed, 0, pieces[done:])
-        emit(fixed[count:], count, pieces[:done])
+        if fixed[count:]:
+            emit(fixed[count:], count, pieces[:done])
     elif fixed:
         emit(fixed, 0, pieces)
     slab = me_ref[0] >> 2
@@ -449,10 +460,10 @@
         mixed, near, opposite, far, out = zip(*blocks)
         me1 = me.reshape(1)
         first = project(me1, [mixed, near], [], weights[:2], tok)
-        early = project(me1, [mixed, near, opposite], [], weights, tok, first)
+        early = project(me1, [mixed, near], [], weights, tok, first)
+        middle = project(me1, [opposite], [], weights, tok)
         late = project(me1, [], [far, out], weights, tok)
-        mine = reduce(*early) + reduce(*late)
-        mine[2], mine[3] = mine[3], mine[2]
+        mine = reduce(*early) + reduce(*late) + reduce(*middle)
     else:
         rows = jnp.stack([jnp.concatenate(parts, axis=1) for parts in zip(*blocks)])
         total = jnp.einsum("zti,joi->jzto", rows, jnp.stack(weights), preferred_element_type=f32)

time: 121 us -> 112 us (0.926)
  waiting for transfers between devices: 57.6 us -> 48.1 us
    ppermute x4, waiting for transfers between devices: 21 us -> 14.8 us  [move(): lax.ppermute(x, 'seq', [(4 * a + r, 4 * b + r) for a, b in pairs for r in...]
    ppermute x2 -> x3, waiting for transfers between devices: 7.42 us -> 5.11 us  [reduce(): got = lax.ppermute(send, 'heads', [(0, 1), (1, 0)])]
    ppermute x2 -> x3, starting transfers between devices: 2.66 us -> 3.69 us  [reduce(): got = lax.ppermute(send, 'heads', [(0, 1), (1, 0)])]
    ppermute x23 -> x24, waiting for transfers between devices: 29.2 us -> 28.2 us  [swap(): return lax.ppermute(x, 'seq', [(i, i ^ bit) for i in range(n_seq)])]
    pallas_call x3 -> x4, Pallas kernels: 3.86 us -> 4.53 us  [project(): pl.pallas_call(functools.partial(project_kernel, len(fixed), len(options)...]
    ppermute x23 -> x24, starting transfers between devices: 24.6 us -> 24.5 us  [swap(): return lax.ppermute(x, 'seq', [(i, i ^ bit) for i in range(n_seq)])]
  transfers between devices with their start and end apart: 29 -> 31, of which waited for: 14 -> 13; matrix products, arithmetic and copies ran while one was open for 7% -> 7% of each run, Pallas kernels for 14% -> 18%
where the time goes in v2:
time: 112 us
  waiting for transfers between devices  48.1 us (43%)
  starting transfers between devices  32.1 us (29%)
  Pallas kernels  21.1 us (19%)
  local copies, waits for them, and re-layouts  8.68 us (8%)
    ppermute x24, waiting for transfers between devices, swap(): return lax.ppermute(x, 'seq', [(i, i ^ bit) for i in range(n_seq)])  28.2 us
    ppermute x24, starting transfers between devices, swap(): return lax.ppermute(x, 'seq', [(i, i ^ bit) for i in range(n_seq)])  24.5 us
    ppermute x4, waiting for transfers between devices, move(): lax.ppermute(x, 'seq', [(4 * a + r, 4 * b + r) for a, b in pairs for r in...  14.8 us
    pallas_call x2, Pallas kernels, attend(): pl.pallas_call(attend_kernel, grid_spec=pltpu.PrefetchScalarGridSpec(num_...  14.8 us
    ppermute x3, waiting for transfers between devices, reduce(): got = lax.ppermute(send, 'heads', [(0, 1), (1, 0)])  5.11 us
    pallas_call x4, Pallas kernels, project(): pl.pallas_call(functools.partial(project_kernel, len(fixed), len(options)...  4.53 us
    ppermute x4, starting transfers between devices, move(): lax.ppermute(x, 'seq', [(4 * a + r, 4 * b + r) for a, b in pairs for r in...  3.91 us
    ppermute x3, starting transfers between devices, reduce(): got = lax.ppermute(send, 'heads', [(0, 1), (1, 0)])  3.69 us
  transfers between devices with their start and end apart: 31, of which 13 were waited for; matrix products, arithmetic and copies ran while one was open for 7% of the time, Pallas kernels for 18%

profile of v2, /device:TPU:0, one launch (start us, length us, event | category | flops | bytes accessed | tf_op | source)
XLA Modules:
  0.0 112.0 jit_solution(7400469489251984537)
XLA Ops:
  0.6 0.9 copy-done.1
  1.5 0.7 copy-done.2
  2.4 5.1 %collective-permute-start.2 = (bf16[72,640]{1,0:T(8,128)(2,1)S(1)}, bf16[72,640]{1,0:T(8,128)(2,1)S(1)}, u32[]{:S(2)}, u32[]{:S(2)}) collective-permute-start(bf16[72,640]{1,0:T(8,128)(2,1)S(1)} %pack.1), channel_id=1, source_target_pairs={{0,12},{1,13},{2,14},{3,15},{4,8},{5,9},{6,10},{7,11},{8,4},{9,5},... | collective-permute-start | bytes 276488 | tf_op jit(solution)/shard_map/ppermute | solution.py:381
  7.6 0.6 collective-permute-start
  8.2 1.7 %collective-permute-start.5 = (bf16[72,640]{1,0:T(8,128)(2,1)S(1)}, bf16[72,640]{1,0:T(8,128)(2,1)}, u32[]{:S(2)}, u32[]{:S(2)}) collective-permute-start(bf16[72,640]{1,0:T(8,128)(2,1)S(1)} %pack.1), channel_id=1, source_target_pairs={{0,2},{1,3},{2,0},{3,1},{4,6},{5,7},{6,4},{7,5},{8,10},{9,11},{10,... | collective-permute-start | bytes 276488 | tf_op jit(solution)/shard_map/ppermute | solution.py:381
  9.9 1.6 %dynamic-slice_bitcast_fusion = (bf16[224,2048]{1,0:T(8,128)(2,1)S(1)}, bf16[224,2048]{1,0:T(8,128)(2,1)S(1)}) fusion(bf16[4096,224]{0,1:T(8,128)(2,1)} %param.16, s32[]{:T(128)S(6)} %select_n.25, s32[]{:T(128)S(6)} %select_n.24), kind=kLoop, calls=%fused_computation | loop fusion | bytes 3670024 | tf_op jit(solution)/shard_map/dynamic_slice | solution.py:418
  11.6 1.2 %constant_dynamic-slice_fusion.3 = (bf16[72,16,128]{2,1,0:T(8,128)(2,1)S(1)}, bf16[72,16,128]{2,1,0:T(8,128)(2,1)S(1)}) fusion(bf16[72,32,128]{2,1,0:T(8,128)(2,1)} %param.10, s32[]{:T(128)S(6)} %select_n.22, s32[]{:T(128)S(6)} %select_n.20), kind=kLoop, calls=%fused_computation.12 | loop fusion | bytes 1179656 | tf_op jit(solution)/shard_map/dynamic-slice.1
  12.9 1.1 constant_dynamic-slice_fusion.2
  14.0 1.5 %collective-permute-done.1 = bf16[72,640]{1,0:T(8,128)(2,1)} collective-permute-done((bf16[72,640]{1,0:T(8,128)(2,1)S(1)}, bf16[72,640]{1,0:T(8,128)(2,1)}, u32[]{:S(2)}, u32[]{:S(2)}) %collective-permute-start.1) | collective-permute-done | bytes 92192 | tf_op jit(solution)/shard_map/ppermute | solution.py:381
  15.4 1.0 pad_maximum_fusion.refs_0_
  16.5 1.6 %collective-permute-start.6 = (bf16[72,640]{1,0:T(8,128)(2,1)}, bf16[72,640]{1,0:T(8,128)(2,1)S(1)}, u32[]{:S(2)}, u32[]{:S(2)}) collective-permute-start(bf16[72,640]{1,0:T(8,128)(2,1)} %collective-permute-done), channel_id=1, source_target_pairs={{0,2},{1,3},{2,0},{3,1},{4,6},{5,7},{6,4},{7,5},{8,10},{9,11},{10,... | collective-permute-start | bytes 276488 | tf_op jit(solution)/shard_map/ppermute | solution.py:381
  18.6 1.5 %collective-permute-start.8 = (bf16[72,640]{1,0:T(8,128)(2,1)S(1)}, bf16[72,640]{1,0:T(8,128)(2,1)S(1)}, u32[]{:S(2)}, u32[]{:S(2)}) collective-permute-start(bf16[72,640]{1,0:T(8,128)(2,1)S(1)} %collective-permute-done.2), channel_id=1, source_target_pairs={{0,2},{1,3},{2,0},{3,1},{4,6},{5,7},{6,4},{7,5},{8,10},{9,11},{10,... | collective-permute-start | bytes 276488 | tf_op jit(solution)/shard_map/ppermute | solution.py:381
  20.1 0.9 constant_dynamic-update-slice_fusion.3
  21.0 1.3 %collective-permute-done.6 = bf16[72,640]{1,0:T(8,128)(2,1)S(1)} collective-permute-done((bf16[72,640]{1,0:T(8,128)(2,1)}, bf16[72,640]{1,0:T(8,128)(2,1)S(1)}, u32[]{:S(2)}, u32[]{:S(2)}) %collective-permute-start.6) | collective-permute-done | bytes 92192 | tf_op jit(solution)/shard_map/ppermute | solution.py:381
  22.3 2.0 %collective-permute-done.7 = bf16[72,640]{1,0:T(8,128)(2,1)S(1)} collective-permute-done((bf16[72,640]{1,0:T(8,128)(2,1)}, bf16[72,640]{1,0:T(8,128)(2,1)S(1)}, u32[]{:S(2)}, u32[]{:S(2)}) %collective-permute-start.7) | collective-permute-done | bytes 92192 | tf_op jit(solution)/shard_map/ppermute | solution.py:381
  24.3 1.4 %collective-permute-done.8 = bf16[72,640]{1,0:T(8,128)(2,1)S(1)} collective-permute-done((bf16[72,640]{1,0:T(8,128)(2,1)S(1)}, bf16[72,640]{1,0:T(8,128)(2,1)S(1)}, u32[]{:S(2)}, u32[]{:S(2)}) %collective-permute-start.8) | collective-permute-done | bytes 92192 | tf_op jit(solution)/shard_map/ppermute | solution.py:381
  26.5 1.9 %constant_dynamic-slice_fusion.1.refs_4_ = bf16[16,128,512]{2,1,0:T(8,128)(2,1)S(1)} fusion(bf16[32,128,512]{2,1,0:T(8,128)(2,1)} %param.14, s32[]{:T(128)S(6)} %select_n.20), kind=kLoop, calls=%fused_computation.10 | loop fusion | bytes 4194308 | tf_op jit(solution)/shard_map/dynamic_slice | solution.py:404
  28.5 1.6 %collective-permute-start.14 = (bf16[224,2048]{1,0:T(8,128)(2,1)S(1)}, bf16[224,2048]{1,0:T(8,128)(2,1)S(1)}, u32[]{:S(2)}, u32[]{:S(2)}) collective-permute-start(bf16[224,2048]{1,0:T(8,128)(2,1)S(1)} %get-tuple-element.45.refs_4_.refs_2_), channel_id=1, source_target_pairs={{0,2},{1,3},{2,0},{3,1},{4,6},{5,7},{6,4},{7,5},{8,10},{9,11},{10,... | collective-permute-start | bytes 2752520 | tf_op jit(solution)/shard_map/ppermute | solution.py:381
  30.3 0.8 collective-permute-start.15
  31.1 7.4 %attend.2.refs_0_ = bf16[144,1024]{1,0:T(8,128)(2,1)S(1)} custom-call(s32[1]{0:T(128)} %bitcast.me_ref, s32[32]{0:T(128)S(1)} %copy-done.3, bf16[16,72,128]{2,1,0:T(8,128)(2,1)S(1)} %bitcast.16, bf16[16,72,128]{2,1,0:T(8,128)(2,1)S(1)} %collective-permute-done.3.nope1_ref, bf16[1024,72]{1,0:T(8,128)(2,1)S(1)} %get-tuple-element.26.rope0_ref, ...), custom_call_target="tpu_custom_call" | custom-call | flops 3057647616 | bytes 2392064 | tf_op jit(solution)/shard_map/attend/pallas_call | solution.py:166
  38.5 0.7 collective-permute-start.11
  39.2 7.4 %attend.3.refs_1_ = bf16[144,1024]{1,0:T(8,128)(2,1)S(1)} custom-call(s32[1]{0:T(128)} %bitcast.me_ref, s32[32]{0:T(128)S(1)} %copy-done.3, bf16[16,72,128]{2,1,0:T(8,128)(2,1)S(1)} %bitcast.17, bf16[16,72,128]{2,1,0:T(8,128)(2,1)S(1)} %collective-permute-done.3.nope1_ref, bf16[1024,72]{1,0:T(8,128)(2,1)S(1)} %get-tuple-element.26.rope0_ref, ...), custom_call_target="tpu_custom_call" | custom-call | flops 3057647616 | bytes 2392064 | tf_op jit(solution)/shard_map/attend/pallas_call | solution.py:166
  46.6 1.4 %collective-permute-start.12 = (bf16[144,1024]{1,0:T(8,128)(2,1)S(1)}, bf16[144,1024]{1,0:T(8,128)(2,1)S(1)}, u32[]{:S(2)}, u32[]{:S(2)}) collective-permute-start(bf16[144,1024]{1,0:T(8,128)(2,1)S(1)} %attend.3.refs_1_), channel_id=1, source_target_pairs={{0,4},{1,5},{2,6},{3,7},{4,0},{5,1},{6,2},{7,3},{8,12},{9,13},{10,... | collective-permute-start | bytes 884744 | tf_op jit(solution)/shard_map/ppermute | solution.py:381
  48.0 2.6 %collective-permute-start.21 = (bf16[144,1024]{1,0:T(8,128)(2,1)S(1)}, bf16[144,1024]{1,0:T(8,128)(2,1)S(1)}, u32[]{:S(2)}, u32[]{:S(2)}) collective-permute-start(bf16[144,1024]{1,0:T(8,128)(2,1)S(1)} %attend.2.refs_0_), channel_id=1, source_target_pairs={{0,12},{1,13},{2,14},{3,15},{4,8},{5,9},{6,10},{7,11},{8,4},{9,5},... | collective-permute-start | bytes 884744 | tf_op jit(solution)/shard_map/ppermute | solution.py:381
  50.6 1.2 %collective-permute-start.23 = (bf16[144,1024]{1,0:T(8,128)(2,1)S(1)}, bf16[144,1024]{1,0:T(8,128)(2,1)S(1)}, u32[]{:S(2)}, u32[]{:S(2)}) collective-permute-start(bf16[144,1024]{1,0:T(8,128)(2,1)S(1)} %attend.3.refs_1_), channel_id=1, source_target_pairs={{0,12},{1,13},{2,14},{3,15},{4,8},{5,9},{6,10},{7,11},{8,4},{9,5},... | collective-permute-start | bytes 884744 | tf_op jit(solution)/shard_map/ppermute | solution.py:381
  51.8 3.6 %collective-permute-done.12.refs_3_ = bf16[144,1024]{1,0:T(8,128)(2,1)S(1)} collective-permute-done((bf16[144,1024]{1,0:T(8,128)(2,1)S(1)}, bf16[144,1024]{1,0:T(8,128)(2,1)S(1)}, u32[]{:S(2)}, u32[]{:S(2)}) %collective-permute-start.12) | collective-permute-done | bytes 294944 | tf_op jit(solution)/shard_map/ppermute | solution.py:381
  55.4 0.7 collective-permute-start.19
  56.1 8.8 %collective-permute-done.21.refs_0_ = bf16[144,1024]{1,0:T(8,128)(2,1)S(1)} collective-permute-done((bf16[144,1024]{1,0:T(8,128)(2,1)S(1)}, bf16[144,1024]{1,0:T(8,128)(2,1)S(1)}, u32[]{:S(2)}, u32[]{:S(2)}) %collective-permute-start.21) | collective-permute-done | bytes 294944 | tf_op jit(solution)/shard_map/ppermute | solution.py:381
  64.9 0.7 collective-permute-start.20
  65.6 4.1 %collective-permute-done.23.refs_1_ = bf16[144,1024]{1,0:T(8,128)(2,1)S(1)} collective-permute-done((bf16[144,1024]{1,0:T(8,128)(2,1)S(1)}, bf16[144,1024]{1,0:T(8,128)(2,1)S(1)}, u32[]{:S(2)}, u32[]{:S(2)}) %collective-permute-start.23) | collective-permute-done | bytes 294944 | tf_op jit(solution)/shard_map/ppermute | solution.py:381
  69.7 1.3 %collective-permute-start.22 = (bf16[144,1024]{1,0:T(8,128)(2,1)S(1)}, bf16[144,1024]{1,0:T(8,128)(2,1)S(1)}, u32[]{:S(2)}, u32[]{:S(2)}) collective-permute-start(bf16[144,1024]{1,0:T(8,128)(2,1)S(1)} %collective-permute-done.21.refs_0_), channel_id=1, source_target_pairs={{4,0},{5,1},{6,2},{7,3},{8,12},{9,13},{10,14},{11,15},{20,16},{21,... | collective-permute-start | bytes 884744 | tf_op jit(solution)/shard_map/ppermute | solution.py:384
  71.0 1.3 %collective-permute-start.24 = (bf16[144,1024]{1,0:T(8,128)(2,1)S(1)}, bf16[144,1024]{1,0:T(8,128)(2,1)S(1)}, u32[]{:S(2)}, u32[]{:S(2)}) collective-permute-start(bf16[144,1024]{1,0:T(8,128)(2,1)S(1)} %collective-permute-done.23.refs_1_), channel_id=1, source_target_pairs={{4,0},{5,1},{6,2},{7,3},{8,12},{9,13},{10,14},{11,15},{20,16},{21,... | collective-permute-start | bytes 884744 | tf_op jit(solution)/shard_map/ppermute | solution.py:384
  72.3 0.8 project.4
  73.1 0.8 project.5
  74.0 11.6 %collective-permute-done.22.refs_2_ = bf16[144,1024]{1,0:T(8,128)(2,1)S(1)} collective-permute-done((bf16[144,1024]{1,0:T(8,128)(2,1)S(1)}, bf16[144,1024]{1,0:T(8,128)(2,1)S(1)}, u32[]{:S(2)}, u32[]{:S(2)}) %collective-permute-start.22) | collective-permute-done | bytes 294944 | tf_op jit(solution)/shard_map/ppermute | solution.py:384
  85.7 3.2 %collective-permute-done.24.refs_3_ = bf16[144,1024]{1,0:T(8,128)(2,1)S(1)} collective-permute-done((bf16[144,1024]{1,0:T(8,128)(2,1)S(1)}, bf16[144,1024]{1,0:T(8,128)(2,1)S(1)}, u32[]{:S(2)}, u32[]{:S(2)}) %collective-permute-start.24) | collective-permute-done | bytes 294944 | tf_op jit(solution)/shard_map/ppermute | solution.py:384
  88.8 1.6 %project.6 = (f32[4,1,72,224]{3,2,1,0:T(8,128)S(1)}, bf16[4,1,72,224]{3,2,1,0:T(8,128)(2,1)S(1)}) custom-call(s32[1]{0:T(128)} %bitcast.me_ref, bf16[144,1024]{1,0:T(8,128)(2,1)S(1)} %collective-permute-done.19.refs_0_, bf16[144,1024]{1,0:T(8,128)(2,1)S(1)} %collective-permute-done.20.refs_1_, bf16[144,1024]{1,0:T(8,128)(2,1)S(1)} %collective-permute-done.22.refs_2_, ...), custom_call_target="tpu_custom_call" | custom-call | flops 528482304 | tf_op jit(solution)/shard_map/project/pallas_call | solution.py:258
  90.5 1.4 %project.7 = (f32[4,1,72,224]{3,2,1,0:T(8,128)S(1)}, bf16[4,1,72,224]{3,2,1,0:T(8,128)(2,1)S(1)}) custom-call(s32[1]{0:T(128)} %bitcast.me_ref, bf16[144,1024]{1,0:T(8,128)(2,1)S(1)} %collective-permute-done.21.refs_0_, bf16[144,1024]{1,0:T(8,128)(2,1)S(1)} %collective-permute-done.23.refs_1_, bf16[224,2048]{1,0:T(8,128)(2,1)S(1)} %get-tuple-element.45.refs_4_.refs_2_, ...), custom_call_target="tpu_custom_call" | custom-call | flops 528482304 | tf_op jit(solution)/shard_map/project/pallas_call | solution.py:258
  91.9 0.6 collective-permute-start.28
  92.6 1.5 %collective-permute-start.17 = (bf16[4,2,36,224]{3,2,1,0:T(8,128)(2,1)S(1)}, bf16[4,2,36,224]{3,2,1,0:T(8,128)(2,1)S(1)}, u32[]{:S(2)}, u32[]{:S(2)}) collective-permute-start(bf16[4,2,36,224]{3,2,1,0:T(8,128)(2,1)S(1)} %get-tuple-element.33), channel_id=1, source_target_pairs={{0,16},{16,0},{1,17},{17,1},{2,18},{18,2},{3,19},{19,3},{4,20},{20... | collective-permute-start | bytes 387080 | tf_op jit(solution)/shard_map/ppermute | solution.py:453
  94.2 0.6 collective-permute-start.26
  94.9 1.5 %collective-permute-start.29 = (bf16[4,1,36,224]{3,2,1,0:T(8,128)(2,1)S(1)}, bf16[4,1,36,224]{3,2,1,0:T(8,128)(2,1)S(1)}, u32[]{:S(2)}, u32[]{:S(2)}) collective-permute-start(bf16[4,1,36,224]{3,2,1,0:T(8,128)(2,1)S(1)} %get-tuple-element.43), channel_id=1, source_target_pairs={{0,16},{16,0},{1,17},{17,1},{2,18},{18,2},{3,19},{19,3},{4,20},{20... | collective-permute-start | bytes 193544 | tf_op jit(solution)/shard_map/ppermute | solution.py:453
  96.5 5.0 %collective-permute-done.26.got_ref = bf16[4,1,36,224]{3,2,1,0:T(8,128)(2,1)S(1)} collective-permute-done((bf16[4,1,36,224]{3,2,1,0:T(8,128)(2,1)S(1)}, bf16[4,1,36,224]{3,2,1,0:T(8,128)(2,1)S(1)}, u32[]{:S(2)}, u32[]{:S(2)}) %collective-permute-start.26) | collective-permute-done | bytes 64544 | tf_op jit(solution)/shard_map/ppermute | solution.py:453
  101.5 0.7 collective-permute-start.27
  102.3 2.6 %collective-permute-start.30 = (bf16[4,36,224]{2,1,0:T(8,128)(2,1)S(1)}, bf16[4,36,224]{2,1,0:T(8,128)(2,1)S(1)}, u32[]{:S(2)}, u32[]{:S(2)}) collective-permute-start(bf16[4,36,224]{2,1,0:T(8,128)(2,1)S(1)} %join.5), channel_id=1, source_target_pairs={{0,12},{1,13},{2,14},{3,15},{4,8},{5,9},{6,10},{7,11},{8,4},{9,5},... | collective-permute-start | bytes 193544 | tf_op jit(solution)/shard_map/ppermute | solution.py:381
  105.2 4.2 %collective-permute-done.27.refs_2_ = bf16[4,36,224]{2,1,0:T(8,128)(2,1)S(1)} collective-permute-done((bf16[4,36,224]{2,1,0:T(8,128)(2,1)S(1)}, bf16[4,36,224]{2,1,0:T(8,128)(2,1)S(1)}, u32[]{:S(2)}, u32[]{:S(2)}) %collective-permute-start.27) | collective-permute-done | bytes 64544 | tf_op jit(solution)/shard_map/ppermute | solution.py:381
  109.4 1.3 %collective-permute-done.18.refs_1_ = bf16[4,36,224]{2,1,0:T(8,128)(2,1)S(1)} collective-permute-done((bf16[4,36,224]{2,1,0:T(8,128)(2,1)S(1)}, bf16[4,36,224]{2,1,0:T(8,128)(2,1)S(1)}, u32[]{:S(2)}, u32[]{:S(2)}) %collective-permute-start.18) | collective-permute-done | bytes 64544 | tf_op jit(solution)/shard_map/ppermute | solution.py:381
  110.7 1.3 %finish.1 = (bf16[36,3584]{1,0:T(8,128)(2,1)}, bf16[36,3584]{1,0:T(8,128)(2,1)}) custom-call(s32[1]{0:T(128)} %bitcast.me_ref, bf16[36,3584]{1,0:T(8,128)(2,1)S(1)} %copy-done, f32[1,3584]{1,0:T(1,128)S(1)} %broadcast_in_dim.3.gain_ref, bf16[4,36,224]{2,1,0:T(8,128)(2,1)S(1)} %get-tuple-element.34.refs_0_, ...), custom_call_target="tpu_custom_call" | custom-call | tf_op jit(solution)/shard_map/finish/pallas_call | solution.py:355
  (53 shorter events, 2.9 us)
Async XLA Ops:
  0.6 0.9 copy-start.1
  1.5 0.7 copy-start.2
  2.2 9.4 %copy-start.5 = (f32[3584]{0:T(1024)S(1)}, f32[3584]{0:T(1024)}, u32[]{:S(2)}) copy-start(f32[3584]{0:T(1024)} %param.18) | copy-start | bytes 43012
  2.4 11.5 %collective-permute-start.2 = (bf16[72,640]{1,0:T(8,128)(2,1)S(1)}, bf16[72,640]{1,0:T(8,128)(2,1)S(1)}, u32[]{:S(2)}, u32[]{:S(2)}) collective-permute-start(bf16[72,640]{1,0:T(8,128)(2,1)S(1)} %pack.1), channel_id=1, source_target_pairs={{0,12},{1,13},{2,14},{3,15},{4,8},{5,9},{6,10},{7,11},{8,4},{9,5},... | collective-permute-start | bytes 276488 | tf_op jit(solution)/shard_map/ppermute | solution.py:381
  7.6 7.8 %collective-permute-start.1 = (bf16[72,640]{1,0:T(8,128)(2,1)S(1)}, bf16[72,640]{1,0:T(8,128)(2,1)}, u32[]{:S(2)}, u32[]{:S(2)}) collective-permute-start(bf16[72,640]{1,0:T(8,128)(2,1)S(1)} %pack.1), channel_id=1, source_target_pairs={{0,8},{1,9},{2,10},{3,11},{4,12},{5,13},{6,14},{7,15},{8,0},{9,1},... | collective-permute-start | bytes 276488 | tf_op jit(solution)/shard_map/ppermute | solution.py:381
  7.6 7.8 %collective-permute-start = (bf16[72,640]{1,0:T(8,128)(2,1)S(1)}, bf16[72,640]{1,0:T(8,128)(2,1)}, u32[]{:S(2)}, u32[]{:S(2)}) collective-permute-start(bf16[72,640]{1,0:T(8,128)(2,1)S(1)} %pack.1), channel_id=1, source_target_pairs={{0,4},{1,5},{2,6},{3,7},{4,0},{5,1},{6,2},{7,3},{8,12},{9,13},{10,... | collective-permute-start | bytes 276488 | tf_op jit(solution)/shard_map/ppermute | solution.py:381
  8.2 10.3 %collective-permute-start.5 = (bf16[72,640]{1,0:T(8,128)(2,1)S(1)}, bf16[72,640]{1,0:T(8,128)(2,1)}, u32[]{:S(2)}, u32[]{:S(2)}) collective-permute-start(bf16[72,640]{1,0:T(8,128)(2,1)S(1)} %pack.1), channel_id=1, source_target_pairs={{0,2},{1,3},{2,0},{3,1},{4,6},{5,7},{6,4},{7,5},{8,10},{9,11},{10,... | collective-permute-start | bytes 276488 | tf_op jit(solution)/shard_map/ppermute | solution.py:381
  11.5 18.8 %collective-permute-start.13 = (bf16[224,2048]{1,0:T(8,128)(2,1)S(1)}, bf16[224,2048]{1,0:T(8,128)(2,1)S(1)}, u32[]{:S(2)}, u32[]{:S(2)}) collective-permute-start(bf16[224,2048]{1,0:T(8,128)(2,1)S(1)} %get-tuple-element.44), channel_id=1, source_target_pairs={{0,1},{1,0},{2,3},{3,2},{4,5},{5,4},{6,7},{7,6},{8,9},{9,8},{10,11... | collective-permute-start | bytes 2752520 | tf_op jit(solution)/shard_map/ppermute | solution.py:381
  16.4 14.7 %collective-permute-start.9 = (bf16[288,640]{1,0:T(8,128)(2,1)S(1)}, bf16[288,640]{1,0:T(8,128)(2,1)S(1)}, u32[]{:S(2)}, u32[]{:S(2)}) collective-permute-start(bf16[288,640]{1,0:T(8,128)(2,1)S(1)} %pad_maximum_fusion.refs_0_), channel_id=1, source_target_pairs={{0,1},{1,0},{2,3},{3,2},{4,5},{5,4},{6,7},{7,6},{8,9},{9,8},{10,11... | collective-permute-start | bytes 1105928 | tf_op jit(solution)/shard_map/ppermute | solution.py:381
  16.5 5.8 %collective-permute-start.6 = (bf16[72,640]{1,0:T(8,128)(2,1)}, bf16[72,640]{1,0:T(8,128)(2,1)S(1)}, u32[]{:S(2)}, u32[]{:S(2)}) collective-permute-start(bf16[72,640]{1,0:T(8,128)(2,1)} %collective-permute-done), channel_id=1, source_target_pairs={{0,2},{1,3},{2,0},{3,1},{4,6},{5,7},{6,4},{7,5},{8,10},{9,11},{10,... | collective-permute-start | bytes 276488 | tf_op jit(solution)/shard_map/ppermute | solution.py:381
  18.1 6.2 %collective-permute-start.7 = (bf16[72,640]{1,0:T(8,128)(2,1)}, bf16[72,640]{1,0:T(8,128)(2,1)S(1)}, u32[]{:S(2)}, u32[]{:S(2)}) collective-permute-start(bf16[72,640]{1,0:T(8,128)(2,1)} %collective-permute-done.1), channel_id=1, source_target_pairs={{0,2},{1,3},{2,0},{3,1},{4,6},{5,7},{6,4},{7,5},{8,10},{9,11},{10,... | collective-permute-start | bytes 276488 | tf_op jit(solution)/shard_map/ppermute | solution.py:381
  18.6 7.1 %collective-permute-start.8 = (bf16[72,640]{1,0:T(8,128)(2,1)S(1)}, bf16[72,640]{1,0:T(8,128)(2,1)S(1)}, u32[]{:S(2)}, u32[]{:S(2)}) collective-permute-start(bf16[72,640]{1,0:T(8,128)(2,1)S(1)} %collective-permute-done.2), channel_id=1, source_target_pairs={{0,2},{1,3},{2,0},{3,1},{4,6},{5,7},{6,4},{7,5},{8,10},{9,11},{10,... | collective-permute-start | bytes 276488 | tf_op jit(solution)/shard_map/ppermute | solution.py:381
  25.7 5.3 %collective-permute-start.10 = (bf16[288,640]{1,0:T(8,128)(2,1)S(1)}, bf16[288,640]{1,0:T(8,128)(2,1)S(1)}, u32[]{:S(2)}, u32[]{:S(2)}) collective-permute-start(bf16[288,640]{1,0:T(8,128)(2,1)S(1)} %constant_dynamic-update-slice_fusion.refs_1_), channel_id=1, source_target_pairs={{0,1},{1,0},{2,3},{3,2},{4,5},{5,4},{6,7},{7,6},{8,9},{9,8},{10,11... | collective-permute-start | bytes 1105928 | tf_op jit(solution)/shard_map/ppermute | solution.py:381
  25.9 5.2 %collective-permute-start.3 = (bf16[16,72,128]{2,1,0:T(8,128)(2,1)S(1)}, bf16[16,72,128]{2,1,0:T(8,128)(2,1)S(1)}, u32[]{:S(2)}, u32[]{:S(2)}) collective-permute-start(bf16[16,72,128]{2,1,0:T(8,128)(2,1)S(1)} %bitcast.20), channel_id=1, source_target_pairs={{0,1},{1,0},{2,3},{3,2},{4,5},{5,4},{6,7},{7,6},{8,9},{9,8},{10,11... | collective-permute-start | bytes 884744 | tf_op jit(solution)/shard_map/ppermute | solution.py:381
  26.4 3.6 %copy-start.4 = (bf16[32,512,128]{2,1,0:T(8,128)(2,1)S(1)}, bf16[32,512,128]{2,1,0:T(8,128)(2,1)}, u32[]{:S(2)}) copy-start(bf16[32,512,128]{2,1,0:T(8,128)(2,1)} %param.15) | copy-start | bytes 12582916
  26.5 2.0 %collective-permute-start.4 = (bf16[1024,72]{1,0:T(8,128)(2,1)S(1)}, bf16[1024,72]{1,0:T(8,128)(2,1)S(1)}, u32[]{:S(2)}, u32[]{:S(2)}) collective-permute-start(bf16[1024,72]{1,0:T(8,128)(2,1)S(1)} %get-tuple-element.48), channel_id=1, source_target_pairs={{0,1},{1,0},{2,3},{3,2},{4,5},{5,4},{6,7},{7,6},{8,9},{9,8},{10,11... | collective-permute-start | bytes 442376 | tf_op jit(solution)/shard_map/ppermute | solution.py:381
  28.5 2.6 %copy-start.3 = (s32[32]{0:T(128)S(1)}, s32[32]{0:T(128)}, u32[]{:S(2)}) copy-start(s32[32]{0:T(128)} %table_ref.3) | copy-start | bytes 388
  28.5 42.5 %collective-permute-start.14 = (bf16[224,2048]{1,0:T(8,128)(2,1)S(1)}, bf16[224,2048]{1,0:T(8,128)(2,1)S(1)}, u32[]{:S(2)}, u32[]{:S(2)}) collective-permute-start(bf16[224,2048]{1,0:T(8,128)(2,1)S(1)} %get-tuple-element.45.refs_4_.refs_2_), channel_id=1, source_target_pairs={{0,2},{1,3},{2,0},{3,1},{4,6},{5,7},{6,4},{7,5},{8,10},{9,11},{10,... | collective-permute-start | bytes 2752520 | tf_op jit(solution)/shard_map/ppermute | solution.py:381
  30.3 42.8 %collective-permute-start.15 = (bf16[224,2048]{1,0:T(8,128)(2,1)S(1)}, bf16[224,2048]{1,0:T(8,128)(2,1)S(1)}, u32[]{:S(2)}, u32[]{:S(2)}) collective-permute-start(bf16[224,2048]{1,0:T(8,128)(2,1)S(1)} %collective-permute-done.13.refs_5_.refs_3_), channel_id=1, source_target_pairs={{0,2},{1,3},{2,0},{3,1},{4,6},{5,7},{6,4},{7,5},{8,10},{9,11},{10,... | collective-permute-start | bytes 2752520 | tf_op jit(solution)/shard_map/ppermute | solution.py:381
  38.5 12.1 %collective-permute-start.11 = (bf16[144,1024]{1,0:T(8,128)(2,1)S(1)}, bf16[144,1024]{1,0:T(8,128)(2,1)S(1)}, u32[]{:S(2)}, u32[]{:S(2)}) collective-permute-start(bf16[144,1024]{1,0:T(8,128)(2,1)S(1)} %attend.2.refs_0_), channel_id=1, source_target_pairs={{0,4},{1,5},{2,6},{3,7},{4,0},{5,1},{6,2},{7,3},{8,12},{9,13},{10,... | collective-permute-start | bytes 884744 | tf_op jit(solution)/shard_map/ppermute | solution.py:381
  46.6 8.8 %collective-permute-start.12 = (bf16[144,1024]{1,0:T(8,128)(2,1)S(1)}, bf16[144,1024]{1,0:T(8,128)(2,1)S(1)}, u32[]{:S(2)}, u32[]{:S(2)}) collective-permute-start(bf16[144,1024]{1,0:T(8,128)(2,1)S(1)} %attend.3.refs_1_), channel_id=1, source_target_pairs={{0,4},{1,5},{2,6},{3,7},{4,0},{5,1},{6,2},{7,3},{8,12},{9,13},{10,... | collective-permute-start | bytes 884744 | tf_op jit(solution)/shard_map/ppermute | solution.py:381
  48.0 16.9 %collective-permute-start.21 = (bf16[144,1024]{1,0:T(8,128)(2,1)S(1)}, bf16[144,1024]{1,0:T(8,128)(2,1)S(1)}, u32[]{:S(2)}, u32[]{:S(2)}) collective-permute-start(bf16[144,1024]{1,0:T(8,128)(2,1)S(1)} %attend.2.refs_0_), channel_id=1, source_target_pairs={{0,12},{1,13},{2,14},{3,15},{4,8},{5,9},{6,10},{7,11},{8,4},{9,5},... | collective-permute-start | bytes 884744 | tf_op jit(solution)/shard_map/ppermute | solution.py:381
  50.6 19.1 %collective-permute-start.23 = (bf16[144,1024]{1,0:T(8,128)(2,1)S(1)}, bf16[144,1024]{1,0:T(8,128)(2,1)S(1)}, u32[]{:S(2)}, u32[]{:S(2)}) collective-permute-start(bf16[144,1024]{1,0:T(8,128)(2,1)S(1)} %attend.3.refs_1_), channel_id=1, source_target_pairs={{0,12},{1,13},{2,14},{3,15},{4,8},{5,9},{6,10},{7,11},{8,4},{9,5},... | collective-permute-start | bytes 884744 | tf_op jit(solution)/shard_map/ppermute | solution.py:381
  55.4 18.6 %collective-permute-start.19 = (bf16[144,1024]{1,0:T(8,128)(2,1)S(1)}, bf16[144,1024]{1,0:T(8,128)(2,1)S(1)}, u32[]{:S(2)}, u32[]{:S(2)}) collective-permute-start(bf16[144,1024]{1,0:T(8,128)(2,1)S(1)} %collective-permute-done.11.refs_2_), channel_id=1, source_target_pairs={{4,8},{5,9},{6,10},{7,11},{8,4},{9,5},{10,6},{11,7},{20,24},{21,25... | collective-permute-start | bytes 884744 | tf_op jit(solution)/shard_map/ppermute | solution.py:384
  64.9 9.1 %collective-permute-start.20 = (bf16[144,1024]{1,0:T(8,128)(2,1)S(1)}, bf16[144,1024]{1,0:T(8,128)(2,1)S(1)}, u32[]{:S(2)}, u32[]{:S(2)}) collective-permute-start(bf16[144,1024]{1,0:T(8,128)(2,1)S(1)} %collective-permute-done.12.refs_3_), channel_id=1, source_target_pairs={{4,8},{5,9},{6,10},{7,11},{8,4},{9,5},{10,6},{11,7},{20,24},{21,25... | collective-permute-start | bytes 884744 | tf_op jit(solution)/shard_map/ppermute | solution.py:384
  69.7 16.0 %collective-permute-start.22 = (bf16[144,1024]{1,0:T(8,128)(2,1)S(1)}, bf16[144,1024]{1,0:T(8,128)(2,1)S(1)}, u32[]{:S(2)}, u32[]{:S(2)}) collective-permute-start(bf16[144,1024]{1,0:T(8,128)(2,1)S(1)} %collective-permute-done.21.refs_0_), channel_id=1, source_target_pairs={{4,0},{5,1},{6,2},{7,3},{8,12},{9,13},{10,14},{11,15},{20,16},{21,... | collective-permute-start | bytes 884744 | tf_op jit(solution)/shard_map/ppermute | solution.py:384
  71.0 17.8 %collective-permute-start.24 = (bf16[144,1024]{1,0:T(8,128)(2,1)S(1)}, bf16[144,1024]{1,0:T(8,128)(2,1)S(1)}, u32[]{:S(2)}, u32[]{:S(2)}) collective-permute-start(bf16[144,1024]{1,0:T(8,128)(2,1)S(1)} %collective-permute-done.23.refs_1_), channel_id=1, source_target_pairs={{4,0},{5,1},{6,2},{7,3},{8,12},{9,13},{10,14},{11,15},{20,16},{21,... | collective-permute-start | bytes 884744 | tf_op jit(solution)/shard_map/ppermute | solution.py:384
  73.9 18.5 %collective-permute-start.16 = (bf16[4,2,72,224]{3,2,1,0:T(8,128)(2,1)S(1)}, bf16[4,2,72,224]{3,2,1,0:T(8,128)(2,1)S(1)}, u32[]{:S(2)}, u32[]{:S(2)}) collective-permute-start(bf16[4,2,72,224]{3,2,1,0:T(8,128)(2,1)S(1)} %get-tuple-element.31), channel_id=1, source_target_pairs={{0,1},{1,0},{2,3},{3,2},{4,5},{5,4},{6,7},{7,6},{8,9},{9,8},{10,11... | collective-permute-start | bytes 774152 | tf_op jit(solution)/shard_map/ppermute | solution.py:381
  90.4 3.7 %collective-permute-start.25 = (bf16[4,1,72,224]{3,2,1,0:T(8,128)(2,1)S(1)}, bf16[4,1,72,224]{3,2,1,0:T(8,128)(2,1)S(1)}, u32[]{:S(2)}, u32[]{:S(2)}) collective-permute-start(bf16[4,1,72,224]{3,2,1,0:T(8,128)(2,1)S(1)} %get-tuple-element.37), channel_id=1, source_target_pairs={{0,1},{1,0},{2,3},{3,2},{4,5},{5,4},{6,7},{7,6},{8,9},{9,8},{10,11... | collective-permute-start | bytes 387080 | tf_op jit(solution)/shard_map/ppermute | solution.py:381
  91.9 18.8 %copy-start = (bf16[36,3584]{1,0:T(8,128)(2,1)S(1)}, bf16[36,3584]{1,0:T(8,128)(2,1)}, u32[]{:S(2)}) copy-start(bf16[36,3584]{1,0:T(8,128)(2,1)} %res_ref.1) | copy-start | bytes 774148
  91.9 3.0 %collective-permute-start.28 = (bf16[4,1,72,224]{3,2,1,0:T(8,128)(2,1)S(1)}, bf16[4,1,72,224]{3,2,1,0:T(8,128)(2,1)S(1)}, u32[]{:S(2)}, u32[]{:S(2)}) collective-permute-start(bf16[4,1,72,224]{3,2,1,0:T(8,128)(2,1)S(1)} %get-tuple-element.41), channel_id=1, source_target_pairs={{0,1},{1,0},{2,3},{3,2},{4,5},{5,4},{6,7},{7,6},{8,9},{9,8},{10,11... | collective-permute-start | bytes 387080 | tf_op jit(solution)/shard_map/ppermute | solution.py:381
  92.6 12.4 %collective-permute-start.17 = (bf16[4,2,36,224]{3,2,1,0:T(8,128)(2,1)S(1)}, bf16[4,2,36,224]{3,2,1,0:T(8,128)(2,1)S(1)}, u32[]{:S(2)}, u32[]{:S(2)}) collective-permute-start(bf16[4,2,36,224]{3,2,1,0:T(8,128)(2,1)S(1)} %get-tuple-element.33), channel_id=1, source_target_pairs={{0,16},{16,0},{1,17},{17,1},{2,18},{18,2},{3,19},{19,3},{4,20},{20... | collective-permute-start | bytes 387080 | tf_op jit(solution)/shard_map/ppermute | solution.py:453
  94.2 7.2 %collective-permute-start.26 = (bf16[4,1,36,224]{3,2,1,0:T(8,128)(2,1)S(1)}, bf16[4,1,36,224]{3,2,1,0:T(8,128)(2,1)S(1)}, u32[]{:S(2)}, u32[]{:S(2)}) collective-permute-start(bf16[4,1,36,224]{3,2,1,0:T(8,128)(2,1)S(1)} %get-tuple-element.39), channel_id=1, source_target_pairs={{0,16},{16,0},{1,17},{17,1},{2,18},{18,2},{3,19},{19,3},{4,20},{20... | collective-permute-start | bytes 193544 | tf_op jit(solution)/shard_map/ppermute | solution.py:453
  94.9 7.4 %collective-permute-start.29 = (bf16[4,1,36,224]{3,2,1,0:T(8,128)(2,1)S(1)}, bf16[4,1,36,224]{3,2,1,0:T(8,128)(2,1)S(1)}, u32[]{:S(2)}, u32[]{:S(2)}) collective-permute-start(bf16[4,1,36,224]{3,2,1,0:T(8,128)(2,1)S(1)} %get-tuple-element.43), channel_id=1, source_target_pairs={{0,16},{16,0},{1,17},{17,1},{2,18},{18,2},{3,19},{19,3},{4,20},{20... | collective-permute-start | bytes 193544 | tf_op jit(solution)/shard_map/ppermute | solution.py:453
  101.5 7.9 %collective-permute-start.27 = (bf16[4,36,224]{2,1,0:T(8,128)(2,1)S(1)}, bf16[4,36,224]{2,1,0:T(8,128)(2,1)S(1)}, u32[]{:S(2)}, u32[]{:S(2)}) collective-permute-start(bf16[4,36,224]{2,1,0:T(8,128)(2,1)S(1)} %join.4), channel_id=1, source_target_pairs={{0,8},{1,9},{2,10},{3,11},{4,12},{5,13},{6,14},{7,15},{8,0},{9,1},... | collective-permute-start | bytes 193544 | tf_op jit(solution)/shard_map/ppermute | solution.py:381
  102.3 7.0 %collective-permute-start.30 = (bf16[4,36,224]{2,1,0:T(8,128)(2,1)S(1)}, bf16[4,36,224]{2,1,0:T(8,128)(2,1)S(1)}, u32[]{:S(2)}, u32[]{:S(2)}) collective-permute-start(bf16[4,36,224]{2,1,0:T(8,128)(2,1)S(1)} %join.5), channel_id=1, source_target_pairs={{0,12},{1,13},{2,14},{3,15},{4,8},{5,9},{6,10},{7,11},{8,4},{9,5},... | collective-permute-start | bytes 193544 | tf_op jit(solution)/shard_map/ppermute | solution.py:381
  105.0 5.7 %collective-permute-start.18 = (bf16[4,36,224]{2,1,0:T(8,128)(2,1)S(1)}, bf16[4,36,224]{2,1,0:T(8,128)(2,1)S(1)}, u32[]{:S(2)}, u32[]{:S(2)}) collective-permute-start(bf16[4,36,224]{2,1,0:T(8,128)(2,1)S(1)} %get-tuple-element.35), channel_id=1, source_target_pairs={{0,4},{1,5},{2,6},{3,7},{4,0},{5,1},{6,2},{7,3},{8,12},{9,13},{10,... | collective-permute-start | bytes 193544 | tf_op jit(solution)/shard_map/ppermute | solution.py:381

commit v3 on v2

--- a/solution.py
+++ b/solution.py
@@ -41,6 +41,9 @@
 
 
 def attend_kernel(
+    first,
+    steps,
+    heads,
     me_ref,
     table_ref,
     nope0_ref,
@@ -51,10 +54,10 @@
 ):
     parts = refs[:4]
     wk_ref, wv_ref, out_ref, kv_ref, bias_ref, q_ref, s_ref, p_ref, total_ref, sem = refs[4:]
-    heads, tok, _ = nope0_ref.shape
+    tok = nope0_ref.shape[1]
     rows, keys = bias_ref.shape
     width = wk_ref.shape[2]
-    rope = rope0_ref.shape[0] // heads
+    rope = rope0_ref.shape[0] // nope0_ref.shape[0]
     span_len = keys // table_ref.shape[0]
     per = tok // span_len
 
@@ -64,8 +67,7 @@
         for n, part in enumerate(parts)
     ]
 
-    @pl.when(pl.program_id(0) == 0)
-    def _():
+    def prepare():
         for copy in copies:
             copy.start()
         me = me_ref[0]
@@ -88,64 +90,73 @@
         bias_ref[...] = jnp.where(kpos <= qpos, jnp.float32(0.0), jnp.float32(-1e30))
 
     f32, bf16 = jnp.float32, jnp.bfloat16
-    for h in range(heads):
-        nope = jnp.concatenate([nope0_ref[h].astype(f32), nope1_ref[h].astype(f32)], axis=0)
-        q_lat = jnp.dot(nope.astype(bf16), wk_ref[h], preferred_element_type=f32)
-        q_ref[h * rows : (h + 1) * rows, :width] = q_lat.astype(bf16)
-    lane = lax.broadcasted_iota(jnp.int32, (rows, 2 * rope), 1)
-    for h in range(0, heads, 2):
-        pick = slice(h * rope, (h + 2) * rope)
-        pair = jnp.concatenate(
-            [rope0_ref[pick, :].astype(f32).T, rope1_ref[pick, :].astype(f32).T], axis=0
-        )
-        q_ref[h * rows : (h + 1) * rows, width:] = jnp.where(lane < rope, pair, 0.0).astype(bf16)
-        q_ref[(h + 1) * rows : (h + 2) * rows, width:] = jnp.where(lane < rope, 0.0, pair).astype(
-            bf16
-        )
-
-    @pl.when(pl.program_id(0) == 0)
-    def _():
-        for copy in copies:
-            copy.wait()
-
-    units, step = 2, 16
-    count = heads * rows // units
-
-    def scores(u):
-        s_ref[pl.ds(u * count, count), :] = lax.dot_general(
-            q_ref[pl.ds(u * count, count), :],
-            kv_ref[...],
-            (((1,), (1,)), ((), ())),
-            preferred_element_type=f32,
-        )
-
-    def weights(u):
-        for r in range(u * count, (u + 1) * count, step):
-            block = s_ref[r : r + step, :] * (score_scale * LOG2E)
-            block = block + bias_ref[r % rows : r % rows + step, :]
-            weight = jnp.exp2(block - jnp.max(block, axis=1, keepdims=True))
-            total_ref[r : r + step, :] = 1.0 / jnp.sum(weight, axis=1, keepdims=True)
-            p_ref[r : r + step, :] = weight.astype(bf16)
-
-    def outputs(u):
-        context = jnp.dot(
-            p_ref[pl.ds(u * count, count), :], kv_ref[:, :width], preferred_element_type=f32
-        )
-        context = (context * total_ref[pl.ds(u * count, count), :]).astype(bf16)
-        for n in range(count // rows):
-            h = u * (count // rows) + n
-            part = jnp.dot(
-                context[n * rows : (n + 1) * rows], wv_ref[h], preferred_element_type=f32
+
+    def queries(base):
+        for h in range(heads):
+            g = base + h
+            nope = jnp.concatenate([nope0_ref[g].astype(f32), nope1_ref[g].astype(f32)], axis=0)
+            q_lat = jnp.dot(nope.astype(bf16), wk_ref[g], preferred_element_type=f32)
+            q_ref[h * rows : (h + 1) * rows, :width] = q_lat.astype(bf16)
+        lane = lax.broadcasted_iota(jnp.int32, (rows, 2 * rope), 1)
+        for h in range(0, heads, 2):
+            pick = slice((base + h) * rope, (base + h + 2) * rope)
+            pair = jnp.concatenate(
+                [rope0_ref[pick, :].astype(f32).T, rope1_ref[pick, :].astype(f32).T], axis=0
             )
-            out_ref[:, h * part.shape[1] : (h + 1) * part.shape[1]] = part.astype(out_ref.dtype)
-
-    for u in range(units + 2):
-        if u < units:
-            scores(u)
-        if 1 <= u <= units:
-            weights(u - 1)
-        if u >= 2:
-            outputs(u - 2)
+            q_ref[h * rows : (h + 1) * rows, width:] = jnp.where(lane < rope, pair, 0.0).astype(bf16)
+            q_ref[(h + 1) * rows : (h + 2) * rows, width:] = jnp.where(lane < rope, 0.0, pair).astype(
+                bf16
+            )
+
+    def attention(base, at):
+        units, step = 2, 16
+        count = heads * rows // units
+
+        def scores(u):
+            s_ref[pl.ds(u * count, count), :] = lax.dot_general(
+                q_ref[pl.ds(u * count, count), :],
+                kv_ref[...],
+                (((1,), (1,)), ((), ())),
+                preferred_element_type=f32,
+            )
+
+        def weights(u):
+            for r in range(u * count, (u + 1) * count, step):
+                block = s_ref[r : r + step, :] * (score_scale * LOG2E)
+                block = block + bias_ref[r % rows : r % rows + step, :]
+                weight = jnp.exp2(block - jnp.max(block, axis=1, keepdims=True))
+                total_ref[r : r + step, :] = 1.0 / jnp.sum(weight, axis=1, keepdims=True)
+                p_ref[r : r + step, :] = weight.astype(bf16)
+
+        def outputs(u):
+            context = jnp.dot(
+                p_ref[pl.ds(u * count, count), :], kv_ref[:, :width], preferred_element_type=f32
+            )
+            context = (context * total_ref[pl.ds(u * count, count), :]).astype(bf16)
+            for n in range(count // rows):
+                h = u * (count // rows) + n
+                part = jnp.dot(
+                    context[n * rows : (n + 1) * rows], wv_ref[base + h], preferred_element_type=f32
+                )
+                c = (at + h) * part.shape[1]
+                out_ref[:, c : c + part.shape[1]] = part.astype(out_ref.dtype)
+
+        for u in range(units + 2):
+            if u < units:
+                scores(u)
+            if 1 <= u <= units:
+                weights(u - 1)
+            if u >= 2:
+                outputs(u - 2)
+
+    prepare()
+    for n in range(steps):
+        base = first + n * heads
+        queries(base)
+        if n == 0:
+            for copy in copies:
+                copy.wait()
+        attention(base, n * heads)
 
 
 def attend(me, table, nope, rope, parts, wk, wv, group, groups, heads):
@@ -154,40 +165,20 @@
     rows = 2 * tok
     keys, depth = 4 * parts[0].shape[0], parts[0].shape[1]
     width = wk.shape[2]
-    rope_rows = rope[0].shape[0] // half * heads
-    first = group * steps
-
-    def mine(i, me_ref, table_ref):
-        return (first + i, 0, 0)
-
-    def mine_flat(i, me_ref, table_ref):
-        return (first + i, 0)
-
-    return pl.pallas_call(
-        attend_kernel,
-        grid_spec=pltpu.PrefetchScalarGridSpec(
-            num_scalar_prefetch=2,
-            grid=(steps,),
-            in_specs=[
-                pl.BlockSpec((heads, tok, size), mine),
-                pl.BlockSpec((heads, tok, size), mine),
-                pl.BlockSpec((rope_rows, tok), mine_flat),
-                pl.BlockSpec((rope_rows, tok), mine_flat),
-                *[pl.BlockSpec(memory_space=pl.ANY)] * 4,
-                pl.BlockSpec((heads, size, width), mine),
-                pl.BlockSpec((heads, width, size), mine),
-            ],
-            out_specs=pl.BlockSpec((rows, heads * size), lambda i, me_ref, table_ref: (0, i)),
-            scratch_shapes=[
-                pltpu.VMEM((keys, depth), jnp.bfloat16),
-                pltpu.VMEM((rows, keys), jnp.float32),
-                pltpu.VMEM((heads * rows, depth), jnp.bfloat16),
-                pltpu.VMEM((heads * rows, keys), jnp.float32),
-                pltpu.VMEM((heads * rows, keys), jnp.bfloat16),
-                pltpu.VMEM((heads * rows, 1), jnp.float32),
-                pltpu.SemaphoreType.DMA((4,)),
-            ],
-        ),
+    smem, vmem = pl.BlockSpec(memory_space=pltpu.SMEM), pl.BlockSpec(memory_space=pltpu.VMEM)
+    return pl.pallas_call(
+        functools.partial(attend_kernel, group * steps * heads, steps, heads),
+        in_specs=[smem] * 2 + [vmem] * 10,
+        out_specs=vmem,
+        scratch_shapes=[
+            pltpu.VMEM((keys, depth), jnp.bfloat16),
+            pltpu.VMEM((rows, keys), jnp.float32),
+            pltpu.VMEM((heads * rows, depth), jnp.bfloat16),
+            pltpu.VMEM((heads * rows, keys), jnp.float32),
+            pltpu.VMEM((heads * rows, keys), jnp.bfloat16),
+            pltpu.VMEM((heads * rows, 1), jnp.float32),
+            pltpu.SemaphoreType.DMA((4,)),
+        ],
         out_shape=jax.ShapeDtypeStruct((rows, half // groups * size), jnp.bfloat16),
         compiler_params=pltpu.CompilerParams(vmem_limit_bytes=24 * 1024 * 1024),
         cost_estimate=pl.CostEstimate(

time: 112 us -> 111 us (level)
  transfers between devices with their start and end apart: 31 -> 31, of which waited for: 13 -> 13; matrix products, arithmetic and copies ran while one was open for 7% -> 7% of each run, Pallas kernels for 18% -> 17%
where the time goes in v3:
time: 111 us
  waiting for transfers between devices  48.1 us (43%)
  starting transfers between devices  32.1 us (29%)
  Pallas kernels  20 us (18%)
  local copies, waits for them, and re-layouts  8.68 us (8%)
    ppermute x24, waiting for transfers between devices, swap(): return lax.ppermute(x, 'seq', [(i, i ^ bit) for i in range(n_seq)])  28.2 us
    ppermute x24, starting transfers between devices, swap(): return lax.ppermute(x, 'seq', [(i, i ^ bit) for i in range(n_seq)])  24.5 us
    ppermute x4, waiting for transfers between devices, move(): lax.ppermute(x, 'seq', [(4 * a + r, 4 * b + r) for a, b in pairs for r in...  14.8 us
    pallas_call x2, Pallas kernels, attend(): pl.pallas_call(functools.partial(attend_kernel, group * steps * heads, st...  13.8 us
    ppermute x3, waiting for transfers between devices, reduce(): got = lax.ppermute(send, 'heads', [(0, 1), (1, 0)])  5.12 us
    pallas_call x4, Pallas kernels, project(): pl.pallas_call(functools.partial(project_kernel, len(fixed), len(options)...  4.37 us
    ppermute x4, starting transfers between devices, move(): lax.ppermute(x, 'seq', [(4 * a + r, 4 * b + r) for a, b in pairs for r in...  3.91 us
    ppermute x3, starting transfers between devices, reduce(): got = lax.ppermute(send, 'heads', [(0, 1), (1, 0)])  3.69 us
  transfers between devices with their start and end apart: 31, of which 13 were waited for; matrix products, arithmetic and copies ran while one was open for 7% of the time, Pallas kernels for 17%

profile of v3, /device:TPU:0, one launch (start us, length us, event | category | flops | bytes accessed | tf_op | source)
XLA Modules:
  0.0 110.8 jit_solution(18154170233746859218)
XLA Ops:
  0.6 0.9 copy-done.1
  1.5 0.7 copy-done.2
  2.4 5.1 %collective-permute-start.2 = (bf16[72,640]{1,0:T(8,128)(2,1)S(1)}, bf16[72,640]{1,0:T(8,128)(2,1)S(1)}, u32[]{:S(2)}, u32[]{:S(2)}) collective-permute-start(bf16[72,640]{1,0:T(8,128)(2,1)S(1)} %pack.1), channel_id=1, source_target_pairs={{0,12},{1,13},{2,14},{3,15},{4,8},{5,9},{6,10},{7,11},{8,4},{9,5},... | collective-permute-start | bytes 276488 | tf_op jit(solution)/shard_map/ppermute | solution.py:372
  7.6 0.6 collective-permute-start
  8.2 1.7 %collective-permute-start.5 = (bf16[72,640]{1,0:T(8,128)(2,1)S(1)}, bf16[72,640]{1,0:T(8,128)(2,1)}, u32[]{:S(2)}, u32[]{:S(2)}) collective-permute-start(bf16[72,640]{1,0:T(8,128)(2,1)S(1)} %pack.1), channel_id=1, source_target_pairs={{0,2},{1,3},{2,0},{3,1},{4,6},{5,7},{6,4},{7,5},{8,10},{9,11},{10,... | collective-permute-start | bytes 276488 | tf_op jit(solution)/shard_map/ppermute | solution.py:372
  9.9 1.6 %dynamic-slice_bitcast_fusion = (bf16[224,2048]{1,0:T(8,128)(2,1)S(1)}, bf16[224,2048]{1,0:T(8,128)(2,1)S(1)}) fusion(bf16[4096,224]{0,1:T(8,128)(2,1)} %param.16, s32[]{:T(128)S(6)} %select_n.25, s32[]{:T(128)S(6)} %select_n.24), kind=kLoop, calls=%fused_computation | loop fusion | bytes 3670024 | tf_op jit(solution)/shard_map/dynamic_slice | solution.py:409
  11.6 1.2 %constant_dynamic-slice_fusion.3 = (bf16[72,16,128]{2,1,0:T(8,128)(2,1)S(1)}, bf16[72,16,128]{2,1,0:T(8,128)(2,1)S(1)}) fusion(bf16[72,32,128]{2,1,0:T(8,128)(2,1)} %param.10, s32[]{:T(128)S(6)} %select_n.22, s32[]{:T(128)S(6)} %select_n.20), kind=kLoop, calls=%fused_computation.12 | loop fusion | bytes 1179656 | tf_op jit(solution)/shard_map/dynamic-slice.1
  12.9 1.1 constant_dynamic-slice_fusion.2
  14.0 1.5 %collective-permute-done.1 = bf16[72,640]{1,0:T(8,128)(2,1)} collective-permute-done((bf16[72,640]{1,0:T(8,128)(2,1)S(1)}, bf16[72,640]{1,0:T(8,128)(2,1)}, u32[]{:S(2)}, u32[]{:S(2)}) %collective-permute-start.1) | collective-permute-done | bytes 92192 | tf_op jit(solution)/shard_map/ppermute | solution.py:372
  15.4 1.0 pad_maximum_fusion.refs_0_
  16.5 1.6 %collective-permute-start.6 = (bf16[72,640]{1,0:T(8,128)(2,1)}, bf16[72,640]{1,0:T(8,128)(2,1)S(1)}, u32[]{:S(2)}, u32[]{:S(2)}) collective-permute-start(bf16[72,640]{1,0:T(8,128)(2,1)} %collective-permute-done), channel_id=1, source_target_pairs={{0,2},{1,3},{2,0},{3,1},{4,6},{5,7},{6,4},{7,5},{8,10},{9,11},{10,... | collective-permute-start | bytes 276488 | tf_op jit(solution)/shard_map/ppermute | solution.py:372
  18.6 1.5 %collective-permute-start.8 = (bf16[72,640]{1,0:T(8,128)(2,1)S(1)}, bf16[72,640]{1,0:T(8,128)(2,1)S(1)}, u32[]{:S(2)}, u32[]{:S(2)}) collective-permute-start(bf16[72,640]{1,0:T(8,128)(2,1)S(1)} %collective-permute-done.2), channel_id=1, source_target_pairs={{0,2},{1,3},{2,0},{3,1},{4,6},{5,7},{6,4},{7,5},{8,10},{9,11},{10,... | collective-permute-start | bytes 276488 | tf_op jit(solution)/shard_map/ppermute | solution.py:372
  20.1 0.9 constant_dynamic-update-slice_fusion.3
  21.0 1.3 %collective-permute-done.6 = bf16[72,640]{1,0:T(8,128)(2,1)S(1)} collective-permute-done((bf16[72,640]{1,0:T(8,128)(2,1)}, bf16[72,640]{1,0:T(8,128)(2,1)S(1)}, u32[]{:S(2)}, u32[]{:S(2)}) %collective-permute-start.6) | collective-permute-done | bytes 92192 | tf_op jit(solution)/shard_map/ppermute | solution.py:372
  22.3 2.0 %collective-permute-done.7 = bf16[72,640]{1,0:T(8,128)(2,1)S(1)} collective-permute-done((bf16[72,640]{1,0:T(8,128)(2,1)}, bf16[72,640]{1,0:T(8,128)(2,1)S(1)}, u32[]{:S(2)}, u32[]{:S(2)}) %collective-permute-start.7) | collective-permute-done | bytes 92192 | tf_op jit(solution)/shard_map/ppermute | solution.py:372
  24.3 1.4 %collective-permute-done.8 = bf16[72,640]{1,0:T(8,128)(2,1)S(1)} collective-permute-done((bf16[72,640]{1,0:T(8,128)(2,1)S(1)}, bf16[72,640]{1,0:T(8,128)(2,1)S(1)}, u32[]{:S(2)}, u32[]{:S(2)}) %collective-permute-start.8) | collective-permute-done | bytes 92192 | tf_op jit(solution)/shard_map/ppermute | solution.py:372
  26.5 1.9 %constant_dynamic-slice_fusion.1.refs_4_ = bf16[16,128,512]{2,1,0:T(8,128)(2,1)S(1)} fusion(bf16[32,128,512]{2,1,0:T(8,128)(2,1)} %param.14, s32[]{:T(128)S(6)} %select_n.20), kind=kLoop, calls=%fused_computation.10 | loop fusion | bytes 4194308 | tf_op jit(solution)/shard_map/dynamic_slice | solution.py:395
  28.5 1.6 %collective-permute-start.14 = (bf16[224,2048]{1,0:T(8,128)(2,1)S(1)}, bf16[224,2048]{1,0:T(8,128)(2,1)S(1)}, u32[]{:S(2)}, u32[]{:S(2)}) collective-permute-start(bf16[224,2048]{1,0:T(8,128)(2,1)S(1)} %get-tuple-element.45.refs_4_.refs_2_), channel_id=1, source_target_pairs={{0,2},{1,3},{2,0},{3,1},{4,6},{5,7},{6,4},{7,5},{8,10},{9,11},{10,... | collective-permute-start | bytes 2752520 | tf_op jit(solution)/shard_map/ppermute | solution.py:372
  30.3 0.8 collective-permute-start.15
  31.1 6.8 %attend.2.refs_0_ = bf16[144,1024]{1,0:T(8,128)(2,1)S(1)} custom-call(s32[1]{0:T(128)} %bitcast.me_ref, s32[32]{0:T(128)S(1)} %copy-done.3, bf16[16,72,128]{2,1,0:T(8,128)(2,1)S(1)} %bitcast.16, bf16[16,72,128]{2,1,0:T(8,128)(2,1)S(1)} %collective-permute-done.3.nope1_ref, bf16[1024,72]{1,0:T(8,128)(2,1)S(1)} %get-tuple-element.26.rope0_ref, ...), custom_call_target="tpu_custom_call" | custom-call | flops 3057647616 | bytes 2392064 | tf_op jit(solution)/shard_map/attend/pallas_call | solution.py:169
  37.9 0.7 collective-permute-start.11
  38.6 7.0 %attend.3.refs_1_ = bf16[144,1024]{1,0:T(8,128)(2,1)S(1)} custom-call(s32[1]{0:T(128)} %bitcast.me_ref, s32[32]{0:T(128)S(1)} %copy-done.3, bf16[16,72,128]{2,1,0:T(8,128)(2,1)S(1)} %bitcast.17, bf16[16,72,128]{2,1,0:T(8,128)(2,1)S(1)} %collective-permute-done.3.nope1_ref, bf16[1024,72]{1,0:T(8,128)(2,1)S(1)} %get-tuple-element.26.rope0_ref, ...), custom_call_target="tpu_custom_call" | custom-call | flops 3057647616 | bytes 2392064 | tf_op jit(solution)/shard_map/attend/pallas_call | solution.py:169
  45.6 1.4 %collective-permute-start.12 = (bf16[144,1024]{1,0:T(8,128)(2,1)S(1)}, bf16[144,1024]{1,0:T(8,128)(2,1)S(1)}, u32[]{:S(2)}, u32[]{:S(2)}) collective-permute-start(bf16[144,1024]{1,0:T(8,128)(2,1)S(1)} %attend.3.refs_1_), channel_id=1, source_target_pairs={{0,4},{1,5},{2,6},{3,7},{4,0},{5,1},{6,2},{7,3},{8,12},{9,13},{10,... | collective-permute-start | bytes 884744 | tf_op jit(solution)/shard_map/ppermute | solution.py:372
  47.0 2.6 %collective-permute-start.21 = (bf16[144,1024]{1,0:T(8,128)(2,1)S(1)}, bf16[144,1024]{1,0:T(8,128)(2,1)S(1)}, u32[]{:S(2)}, u32[]{:S(2)}) collective-permute-start(bf16[144,1024]{1,0:T(8,128)(2,1)S(1)} %attend.2.refs_0_), channel_id=1, source_target_pairs={{0,12},{1,13},{2,14},{3,15},{4,8},{5,9},{6,10},{7,11},{8,4},{9,5},... | collective-permute-start | bytes 884744 | tf_op jit(solution)/shard_map/ppermute | solution.py:372
  49.6 1.2 %collective-permute-start.23 = (bf16[144,1024]{1,0:T(8,128)(2,1)S(1)}, bf16[144,1024]{1,0:T(8,128)(2,1)S(1)}, u32[]{:S(2)}, u32[]{:S(2)}) collective-permute-start(bf16[144,1024]{1,0:T(8,128)(2,1)S(1)} %attend.3.refs_1_), channel_id=1, source_target_pairs={{0,12},{1,13},{2,14},{3,15},{4,8},{5,9},{6,10},{7,11},{8,4},{9,5},... | collective-permute-start | bytes 884744 | tf_op jit(solution)/shard_map/ppermute | solution.py:372
  50.8 3.6 %collective-permute-done.12.refs_3_ = bf16[144,1024]{1,0:T(8,128)(2,1)S(1)} collective-permute-done((bf16[144,1024]{1,0:T(8,128)(2,1)S(1)}, bf16[144,1024]{1,0:T(8,128)(2,1)S(1)}, u32[]{:S(2)}, u32[]{:S(2)}) %collective-permute-start.12) | collective-permute-done | bytes 294944 | tf_op jit(solution)/shard_map/ppermute | solution.py:372
  54.4 0.7 collective-permute-start.19
  55.1 8.8 %collective-permute-done.21.refs_0_ = bf16[144,1024]{1,0:T(8,128)(2,1)S(1)} collective-permute-done((bf16[144,1024]{1,0:T(8,128)(2,1)S(1)}, bf16[144,1024]{1,0:T(8,128)(2,1)S(1)}, u32[]{:S(2)}, u32[]{:S(2)}) %collective-permute-start.21) | collective-permute-done | bytes 294944 | tf_op jit(solution)/shard_map/ppermute | solution.py:372
  63.9 0.7 collective-permute-start.20
  64.5 4.2 %collective-permute-done.23.refs_1_ = bf16[144,1024]{1,0:T(8,128)(2,1)S(1)} collective-permute-done((bf16[144,1024]{1,0:T(8,128)(2,1)S(1)}, bf16[144,1024]{1,0:T(8,128)(2,1)S(1)}, u32[]{:S(2)}, u32[]{:S(2)}) %collective-permute-start.23) | collective-permute-done | bytes 294944 | tf_op jit(solution)/shard_map/ppermute | solution.py:372
  68.7 1.3 %collective-permute-start.22 = (bf16[144,1024]{1,0:T(8,128)(2,1)S(1)}, bf16[144,1024]{1,0:T(8,128)(2,1)S(1)}, u32[]{:S(2)}, u32[]{:S(2)}) collective-permute-start(bf16[144,1024]{1,0:T(8,128)(2,1)S(1)} %collective-permute-done.21.refs_0_), channel_id=1, source_target_pairs={{4,0},{5,1},{6,2},{7,3},{8,12},{9,13},{10,14},{11,15},{20,16},{21,... | collective-permute-start | bytes 884744 | tf_op jit(solution)/shard_map/ppermute | solution.py:375
  70.0 1.3 %collective-permute-start.24 = (bf16[144,1024]{1,0:T(8,128)(2,1)S(1)}, bf16[144,1024]{1,0:T(8,128)(2,1)S(1)}, u32[]{:S(2)}, u32[]{:S(2)}) collective-permute-start(bf16[144,1024]{1,0:T(8,128)(2,1)S(1)} %collective-permute-done.23.refs_1_), channel_id=1, source_target_pairs={{4,0},{5,1},{6,2},{7,3},{8,12},{9,13},{10,14},{11,15},{20,16},{21,... | collective-permute-start | bytes 884744 | tf_op jit(solution)/shard_map/ppermute | solution.py:375
  71.3 0.8 project.4
  72.1 0.8 project.5
  73.0 11.7 %collective-permute-done.22.refs_2_ = bf16[144,1024]{1,0:T(8,128)(2,1)S(1)} collective-permute-done((bf16[144,1024]{1,0:T(8,128)(2,1)S(1)}, bf16[144,1024]{1,0:T(8,128)(2,1)S(1)}, u32[]{:S(2)}, u32[]{:S(2)}) %collective-permute-start.22) | collective-permute-done | bytes 294944 | tf_op jit(solution)/shard_map/ppermute | solution.py:375
  84.7 3.2 %collective-permute-done.24.refs_3_ = bf16[144,1024]{1,0:T(8,128)(2,1)S(1)} collective-permute-done((bf16[144,1024]{1,0:T(8,128)(2,1)S(1)}, bf16[144,1024]{1,0:T(8,128)(2,1)S(1)}, u32[]{:S(2)}, u32[]{:S(2)}) %collective-permute-start.24) | collective-permute-done | bytes 294944 | tf_op jit(solution)/shard_map/ppermute | solution.py:375
  87.8 1.4 %project.6 = (f32[4,1,72,224]{3,2,1,0:T(8,128)S(1)}, bf16[4,1,72,224]{3,2,1,0:T(8,128)(2,1)S(1)}) custom-call(s32[1]{0:T(128)} %bitcast.me_ref, bf16[144,1024]{1,0:T(8,128)(2,1)S(1)} %collective-permute-done.19.refs_0_, bf16[144,1024]{1,0:T(8,128)(2,1)S(1)} %collective-permute-done.20.refs_1_, bf16[144,1024]{1,0:T(8,128)(2,1)S(1)} %collective-permute-done.22.refs_2_, ...), custom_call_target="tpu_custom_call" | custom-call | flops 528482304 | tf_op jit(solution)/shard_map/project/pallas_call | solution.py:249
  89.3 1.4 %project.7 = (f32[4,1,72,224]{3,2,1,0:T(8,128)S(1)}, bf16[4,1,72,224]{3,2,1,0:T(8,128)(2,1)S(1)}) custom-call(s32[1]{0:T(128)} %bitcast.me_ref, bf16[144,1024]{1,0:T(8,128)(2,1)S(1)} %collective-permute-done.21.refs_0_, bf16[144,1024]{1,0:T(8,128)(2,1)S(1)} %collective-permute-done.23.refs_1_, bf16[224,2048]{1,0:T(8,128)(2,1)S(1)} %get-tuple-element.45.refs_4_.refs_2_, ...), custom_call_target="tpu_custom_call" | custom-call | flops 528482304 | tf_op jit(solution)/shard_map/project/pallas_call | solution.py:249
  90.7 0.6 collective-permute-start.28
  91.4 1.5 %collective-permute-start.17 = (bf16[4,2,36,224]{3,2,1,0:T(8,128)(2,1)S(1)}, bf16[4,2,36,224]{3,2,1,0:T(8,128)(2,1)S(1)}, u32[]{:S(2)}, u32[]{:S(2)}) collective-permute-start(bf16[4,2,36,224]{3,2,1,0:T(8,128)(2,1)S(1)} %get-tuple-element.33), channel_id=1, source_target_pairs={{0,16},{16,0},{1,17},{17,1},{2,18},{18,2},{3,19},{19,3},{4,20},{20... | collective-permute-start | bytes 387080 | tf_op jit(solution)/shard_map/ppermute | solution.py:444
  93.1 0.6 collective-permute-start.26
  93.7 1.5 %collective-permute-start.29 = (bf16[4,1,36,224]{3,2,1,0:T(8,128)(2,1)S(1)}, bf16[4,1,36,224]{3,2,1,0:T(8,128)(2,1)S(1)}, u32[]{:S(2)}, u32[]{:S(2)}) collective-permute-start(bf16[4,1,36,224]{3,2,1,0:T(8,128)(2,1)S(1)} %get-tuple-element.43), channel_id=1, source_target_pairs={{0,16},{16,0},{1,17},{17,1},{2,18},{18,2},{3,19},{19,3},{4,20},{20... | collective-permute-start | bytes 193544 | tf_op jit(solution)/shard_map/ppermute | solution.py:444
  95.3 5.0 %collective-permute-done.26.got_ref = bf16[4,1,36,224]{3,2,1,0:T(8,128)(2,1)S(1)} collective-permute-done((bf16[4,1,36,224]{3,2,1,0:T(8,128)(2,1)S(1)}, bf16[4,1,36,224]{3,2,1,0:T(8,128)(2,1)S(1)}, u32[]{:S(2)}, u32[]{:S(2)}) %collective-permute-start.26) | collective-permute-done | bytes 64544 | tf_op jit(solution)/shard_map/ppermute | solution.py:444
  100.3 0.7 collective-permute-start.27
  101.2 2.6 %collective-permute-start.30 = (bf16[4,36,224]{2,1,0:T(8,128)(2,1)S(1)}, bf16[4,36,224]{2,1,0:T(8,128)(2,1)S(1)}, u32[]{:S(2)}, u32[]{:S(2)}) collective-permute-start(bf16[4,36,224]{2,1,0:T(8,128)(2,1)S(1)} %join.5), channel_id=1, source_target_pairs={{0,12},{1,13},{2,14},{3,15},{4,8},{5,9},{6,10},{7,11},{8,4},{9,5},... | collective-permute-start | bytes 193544 | tf_op jit(solution)/shard_map/ppermute | solution.py:372
  104.0 4.2 %collective-permute-done.27.refs_2_ = bf16[4,36,224]{2,1,0:T(8,128)(2,1)S(1)} collective-permute-done((bf16[4,36,224]{2,1,0:T(8,128)(2,1)S(1)}, bf16[4,36,224]{2,1,0:T(8,128)(2,1)S(1)}, u32[]{:S(2)}, u32[]{:S(2)}) %collective-permute-start.27) | collective-permute-done | bytes 64544 | tf_op jit(solution)/shard_map/ppermute | solution.py:372
  108.2 1.3 %collective-permute-done.18.refs_1_ = bf16[4,36,224]{2,1,0:T(8,128)(2,1)S(1)} collective-permute-done((bf16[4,36,224]{2,1,0:T(8,128)(2,1)S(1)}, bf16[4,36,224]{2,1,0:T(8,128)(2,1)S(1)}, u32[]{:S(2)}, u32[]{:S(2)}) %collective-permute-start.18) | collective-permute-done | bytes 64544 | tf_op jit(solution)/shard_map/ppermute | solution.py:372
  109.5 1.3 %finish.1 = (bf16[36,3584]{1,0:T(8,128)(2,1)}, bf16[36,3584]{1,0:T(8,128)(2,1)}) custom-call(s32[1]{0:T(128)} %bitcast.me_ref, bf16[36,3584]{1,0:T(8,128)(2,1)S(1)} %copy-done, f32[1,3584]{1,0:T(1,128)S(1)} %broadcast_in_dim.3.gain_ref, bf16[4,36,224]{2,1,0:T(8,128)(2,1)S(1)} %get-tuple-element.34.refs_0_, ...), custom_call_target="tpu_custom_call" | custom-call | tf_op jit(solution)/shard_map/finish/pallas_call | solution.py:346
  (53 shorter events, 2.9 us)
Async XLA Ops:
  0.6 0.9 copy-start.1
  1.5 0.7 copy-start.2
  2.2 9.4 %copy-start.5 = (f32[3584]{0:T(1024)S(1)}, f32[3584]{0:T(1024)}, u32[]{:S(2)}) copy-start(f32[3584]{0:T(1024)} %param.18) | copy-start | bytes 43012
  2.4 11.5 %collective-permute-start.2 = (bf16[72,640]{1,0:T(8,128)(2,1)S(1)}, bf16[72,640]{1,0:T(8,128)(2,1)S(1)}, u32[]{:S(2)}, u32[]{:S(2)}) collective-permute-start(bf16[72,640]{1,0:T(8,128)(2,1)S(1)} %pack.1), channel_id=1, source_target_pairs={{0,12},{1,13},{2,14},{3,15},{4,8},{5,9},{6,10},{7,11},{8,4},{9,5},... | collective-permute-start | bytes 276488 | tf_op jit(solution)/shard_map/ppermute | solution.py:372
  7.6 7.8 %collective-permute-start.1 = (bf16[72,640]{1,0:T(8,128)(2,1)S(1)}, bf16[72,640]{1,0:T(8,128)(2,1)}, u32[]{:S(2)}, u32[]{:S(2)}) collective-permute-start(bf16[72,640]{1,0:T(8,128)(2,1)S(1)} %pack.1), channel_id=1, source_target_pairs={{0,8},{1,9},{2,10},{3,11},{4,12},{5,13},{6,14},{7,15},{8,0},{9,1},... | collective-permute-start | bytes 276488 | tf_op jit(solution)/shard_map/ppermute | solution.py:372
  7.6 7.8 %collective-permute-start = (bf16[72,640]{1,0:T(8,128)(2,1)S(1)}, bf16[72,640]{1,0:T(8,128)(2,1)}, u32[]{:S(2)}, u32[]{:S(2)}) collective-permute-start(bf16[72,640]{1,0:T(8,128)(2,1)S(1)} %pack.1), channel_id=1, source_target_pairs={{0,4},{1,5},{2,6},{3,7},{4,0},{5,1},{6,2},{7,3},{8,12},{9,13},{10,... | collective-permute-start | bytes 276488 | tf_op jit(solution)/shard_map/ppermute | solution.py:372
  8.2 10.3 %collective-permute-start.5 = (bf16[72,640]{1,0:T(8,128)(2,1)S(1)}, bf16[72,640]{1,0:T(8,128)(2,1)}, u32[]{:S(2)}, u32[]{:S(2)}) collective-permute-start(bf16[72,640]{1,0:T(8,128)(2,1)S(1)} %pack.1), channel_id=1, source_target_pairs={{0,2},{1,3},{2,0},{3,1},{4,6},{5,7},{6,4},{7,5},{8,10},{9,11},{10,... | collective-permute-start | bytes 276488 | tf_op jit(solution)/shard_map/ppermute | solution.py:372
  11.5 18.8 %collective-permute-start.13 = (bf16[224,2048]{1,0:T(8,128)(2,1)S(1)}, bf16[224,2048]{1,0:T(8,128)(2,1)S(1)}, u32[]{:S(2)}, u32[]{:S(2)}) collective-permute-start(bf16[224,2048]{1,0:T(8,128)(2,1)S(1)} %get-tuple-element.44), channel_id=1, source_target_pairs={{0,1},{1,0},{2,3},{3,2},{4,5},{5,4},{6,7},{7,6},{8,9},{9,8},{10,11... | collective-permute-start | bytes 2752520 | tf_op jit(solution)/shard_map/ppermute | solution.py:372
  16.4 14.7 %collective-permute-start.9 = (bf16[288,640]{1,0:T(8,128)(2,1)S(1)}, bf16[288,640]{1,0:T(8,128)(2,1)S(1)}, u32[]{:S(2)}, u32[]{:S(2)}) collective-permute-start(bf16[288,640]{1,0:T(8,128)(2,1)S(1)} %pad_maximum_fusion.refs_0_), channel_id=1, source_target_pairs={{0,1},{1,0},{2,3},{3,2},{4,5},{5,4},{6,7},{7,6},{8,9},{9,8},{10,11... | collective-permute-start | bytes 1105928 | tf_op jit(solution)/shard_map/ppermute | solution.py:372
  16.5 5.8 %collective-permute-start.6 = (bf16[72,640]{1,0:T(8,128)(2,1)}, bf16[72,640]{1,0:T(8,128)(2,1)S(1)}, u32[]{:S(2)}, u32[]{:S(2)}) collective-permute-start(bf16[72,640]{1,0:T(8,128)(2,1)} %collective-permute-done), channel_id=1, source_target_pairs={{0,2},{1,3},{2,0},{3,1},{4,6},{5,7},{6,4},{7,5},{8,10},{9,11},{10,... | collective-permute-start | bytes 276488 | tf_op jit(solution)/shard_map/ppermute | solution.py:372
  18.1 6.2 %collective-permute-start.7 = (bf16[72,640]{1,0:T(8,128)(2,1)}, bf16[72,640]{1,0:T(8,128)(2,1)S(1)}, u32[]{:S(2)}, u32[]{:S(2)}) collective-permute-start(bf16[72,640]{1,0:T(8,128)(2,1)} %collective-permute-done.1), channel_id=1, source_target_pairs={{0,2},{1,3},{2,0},{3,1},{4,6},{5,7},{6,4},{7,5},{8,10},{9,11},{10,... | collective-permute-start | bytes 276488 | tf_op jit(solution)/shard_map/ppermute | solution.py:372
  18.6 7.1 %collective-permute-start.8 = (bf16[72,640]{1,0:T(8,128)(2,1)S(1)}, bf16[72,640]{1,0:T(8,128)(2,1)S(1)}, u32[]{:S(2)}, u32[]{:S(2)}) collective-permute-start(bf16[72,640]{1,0:T(8,128)(2,1)S(1)} %collective-permute-done.2), channel_id=1, source_target_pairs={{0,2},{1,3},{2,0},{3,1},{4,6},{5,7},{6,4},{7,5},{8,10},{9,11},{10,... | collective-permute-start | bytes 276488 | tf_op jit(solution)/shard_map/ppermute | solution.py:372
  25.7 5.3 %collective-permute-start.10 = (bf16[288,640]{1,0:T(8,128)(2,1)S(1)}, bf16[288,640]{1,0:T(8,128)(2,1)S(1)}, u32[]{:S(2)}, u32[]{:S(2)}) collective-permute-start(bf16[288,640]{1,0:T(8,128)(2,1)S(1)} %constant_dynamic-update-slice_fusion.refs_1_), channel_id=1, source_target_pairs={{0,1},{1,0},{2,3},{3,2},{4,5},{5,4},{6,7},{7,6},{8,9},{9,8},{10,11... | collective-permute-start | bytes 1105928 | tf_op jit(solution)/shard_map/ppermute | solution.py:372
  25.9 5.2 %collective-permute-start.3 = (bf16[16,72,128]{2,1,0:T(8,128)(2,1)S(1)}, bf16[16,72,128]{2,1,0:T(8,128)(2,1)S(1)}, u32[]{:S(2)}, u32[]{:S(2)}) collective-permute-start(bf16[16,72,128]{2,1,0:T(8,128)(2,1)S(1)} %bitcast.20), channel_id=1, source_target_pairs={{0,1},{1,0},{2,3},{3,2},{4,5},{5,4},{6,7},{7,6},{8,9},{9,8},{10,11... | collective-permute-start | bytes 884744 | tf_op jit(solution)/shard_map/ppermute | solution.py:372
  26.4 3.6 %copy-start.4 = (bf16[32,512,128]{2,1,0:T(8,128)(2,1)S(1)}, bf16[32,512,128]{2,1,0:T(8,128)(2,1)}, u32[]{:S(2)}) copy-start(bf16[32,512,128]{2,1,0:T(8,128)(2,1)} %param.15) | copy-start | bytes 12582916
  26.5 2.0 %collective-permute-start.4 = (bf16[1024,72]{1,0:T(8,128)(2,1)S(1)}, bf16[1024,72]{1,0:T(8,128)(2,1)S(1)}, u32[]{:S(2)}, u32[]{:S(2)}) collective-permute-start(bf16[1024,72]{1,0:T(8,128)(2,1)S(1)} %get-tuple-element.48), channel_id=1, source_target_pairs={{0,1},{1,0},{2,3},{3,2},{4,5},{5,4},{6,7},{7,6},{8,9},{9,8},{10,11... | collective-permute-start | bytes 442376 | tf_op jit(solution)/shard_map/ppermute | solution.py:372
  28.5 2.6 %copy-start.3 = (s32[32]{0:T(128)S(1)}, s32[32]{0:T(128)}, u32[]{:S(2)}) copy-start(s32[32]{0:T(128)} %table_ref.3) | copy-start | bytes 388
  28.5 41.5 %collective-permute-start.14 = (bf16[224,2048]{1,0:T(8,128)(2,1)S(1)}, bf16[224,2048]{1,0:T(8,128)(2,1)S(1)}, u32[]{:S(2)}, u32[]{:S(2)}) collective-permute-start(bf16[224,2048]{1,0:T(8,128)(2,1)S(1)} %get-tuple-element.45.refs_4_.refs_2_), channel_id=1, source_target_pairs={{0,2},{1,3},{2,0},{3,1},{4,6},{5,7},{6,4},{7,5},{8,10},{9,11},{10,... | collective-permute-start | bytes 2752520 | tf_op jit(solution)/shard_map/ppermute | solution.py:372
  30.3 41.8 %collective-permute-start.15 = (bf16[224,2048]{1,0:T(8,128)(2,1)S(1)}, bf16[224,2048]{1,0:T(8,128)(2,1)S(1)}, u32[]{:S(2)}, u32[]{:S(2)}) collective-permute-start(bf16[224,2048]{1,0:T(8,128)(2,1)S(1)} %collective-permute-done.13.refs_5_.refs_3_), channel_id=1, source_target_pairs={{0,2},{1,3},{2,0},{3,1},{4,6},{5,7},{6,4},{7,5},{8,10},{9,11},{10,... | collective-permute-start | bytes 2752520 | tf_op jit(solution)/shard_map/ppermute | solution.py:372
  37.9 11.7 %collective-permute-start.11 = (bf16[144,1024]{1,0:T(8,128)(2,1)S(1)}, bf16[144,1024]{1,0:T(8,128)(2,1)S(1)}, u32[]{:S(2)}, u32[]{:S(2)}) collective-permute-start(bf16[144,1024]{1,0:T(8,128)(2,1)S(1)} %attend.2.refs_0_), channel_id=1, source_target_pairs={{0,4},{1,5},{2,6},{3,7},{4,0},{5,1},{6,2},{7,3},{8,12},{9,13},{10,... | collective-permute-start | bytes 884744 | tf_op jit(solution)/shard_map/ppermute | solution.py:372
  45.6 8.8 %collective-permute-start.12 = (bf16[144,1024]{1,0:T(8,128)(2,1)S(1)}, bf16[144,1024]{1,0:T(8,128)(2,1)S(1)}, u32[]{:S(2)}, u32[]{:S(2)}) collective-permute-start(bf16[144,1024]{1,0:T(8,128)(2,1)S(1)} %attend.3.refs_1_), channel_id=1, source_target_pairs={{0,4},{1,5},{2,6},{3,7},{4,0},{5,1},{6,2},{7,3},{8,12},{9,13},{10,... | collective-permute-start | bytes 884744 | tf_op jit(solution)/shard_map/ppermute | solution.py:372
  47.0 16.9 %collective-permute-start.21 = (bf16[144,1024]{1,0:T(8,128)(2,1)S(1)}, bf16[144,1024]{1,0:T(8,128)(2,1)S(1)}, u32[]{:S(2)}, u32[]{:S(2)}) collective-permute-start(bf16[144,1024]{1,0:T(8,128)(2,1)S(1)} %attend.2.refs_0_), channel_id=1, source_target_pairs={{0,12},{1,13},{2,14},{3,15},{4,8},{5,9},{6,10},{7,11},{8,4},{9,5},... | collective-permute-start | bytes 884744 | tf_op jit(solution)/shard_map/ppermute | solution.py:372
  49.6 19.1 %collective-permute-start.23 = (bf16[144,1024]{1,0:T(8,128)(2,1)S(1)}, bf16[144,1024]{1,0:T(8,128)(2,1)S(1)}, u32[]{:S(2)}, u32[]{:S(2)}) collective-permute-start(bf16[144,1024]{1,0:T(8,128)(2,1)S(1)} %attend.3.refs_1_), channel_id=1, source_target_pairs={{0,12},{1,13},{2,14},{3,15},{4,8},{5,9},{6,10},{7,11},{8,4},{9,5},... | collective-permute-start | bytes 884744 | tf_op jit(solution)/shard_map/ppermute | solution.py:372
  54.4 18.6 %collective-permute-start.19 = (bf16[144,1024]{1,0:T(8,128)(2,1)S(1)}, bf16[144,1024]{1,0:T(8,128)(2,1)S(1)}, u32[]{:S(2)}, u32[]{:S(2)}) collective-permute-start(bf16[144,1024]{1,0:T(8,128)(2,1)S(1)} %collective-permute-done.11.refs_2_), channel_id=1, source_target_pairs={{4,8},{5,9},{6,10},{7,11},{8,4},{9,5},{10,6},{11,7},{20,24},{21,25... | collective-permute-start | bytes 884744 | tf_op jit(solution)/shard_map/ppermute | solution.py:375
  63.9 9.1 %collective-permute-start.20 = (bf16[144,1024]{1,0:T(8,128)(2,1)S(1)}, bf16[144,1024]{1,0:T(8,128)(2,1)S(1)}, u32[]{:S(2)}, u32[]{:S(2)}) collective-permute-start(bf16[144,1024]{1,0:T(8,128)(2,1)S(1)} %collective-permute-done.12.refs_3_), channel_id=1, source_target_pairs={{4,8},{5,9},{6,10},{7,11},{8,4},{9,5},{10,6},{11,7},{20,24},{21,25... | collective-permute-start | bytes 884744 | tf_op jit(solution)/shard_map/ppermute | solution.py:375
  68.7 16.0 %collective-permute-start.22 = (bf16[144,1024]{1,0:T(8,128)(2,1)S(1)}, bf16[144,1024]{1,0:T(8,128)(2,1)S(1)}, u32[]{:S(2)}, u32[]{:S(2)}) collective-permute-start(bf16[144,1024]{1,0:T(8,128)(2,1)S(1)} %collective-permute-done.21.refs_0_), channel_id=1, source_target_pairs={{4,0},{5,1},{6,2},{7,3},{8,12},{9,13},{10,14},{11,15},{20,16},{21,... | collective-permute-start | bytes 884744 | tf_op jit(solution)/shard_map/ppermute | solution.py:375
  70.0 17.8 %collective-permute-start.24 = (bf16[144,1024]{1,0:T(8,128)(2,1)S(1)}, bf16[144,1024]{1,0:T(8,128)(2,1)S(1)}, u32[]{:S(2)}, u32[]{:S(2)}) collective-permute-start(bf16[144,1024]{1,0:T(8,128)(2,1)S(1)} %collective-permute-done.23.refs_1_), channel_id=1, source_target_pairs={{4,0},{5,1},{6,2},{7,3},{8,12},{9,13},{10,14},{11,15},{20,16},{21,... | collective-permute-start | bytes 884744 | tf_op jit(solution)/shard_map/ppermute | solution.py:375
  72.9 18.3 %collective-permute-start.16 = (bf16[4,2,72,224]{3,2,1,0:T(8,128)(2,1)S(1)}, bf16[4,2,72,224]{3,2,1,0:T(8,128)(2,1)S(1)}, u32[]{:S(2)}, u32[]{:S(2)}) collective-permute-start(bf16[4,2,72,224]{3,2,1,0:T(8,128)(2,1)S(1)} %get-tuple-element.31), channel_id=1, source_target_pairs={{0,1},{1,0},{2,3},{3,2},{4,5},{5,4},{6,7},{7,6},{8,9},{9,8},{10,11... | collective-permute-start | bytes 774152 | tf_op jit(solution)/shard_map/ppermute | solution.py:372
  89.2 3.8 %collective-permute-start.25 = (bf16[4,1,72,224]{3,2,1,0:T(8,128)(2,1)S(1)}, bf16[4,1,72,224]{3,2,1,0:T(8,128)(2,1)S(1)}, u32[]{:S(2)}, u32[]{:S(2)}) collective-permute-start(bf16[4,1,72,224]{3,2,1,0:T(8,128)(2,1)S(1)} %get-tuple-element.37), channel_id=1, source_target_pairs={{0,1},{1,0},{2,3},{3,2},{4,5},{5,4},{6,7},{7,6},{8,9},{9,8},{10,11... | collective-permute-start | bytes 387080 | tf_op jit(solution)/shard_map/ppermute | solution.py:372
  90.7 18.8 %copy-start = (bf16[36,3584]{1,0:T(8,128)(2,1)S(1)}, bf16[36,3584]{1,0:T(8,128)(2,1)}, u32[]{:S(2)}) copy-start(bf16[36,3584]{1,0:T(8,128)(2,1)} %res_ref.1) | copy-start | bytes 774148
  90.7 3.0 %collective-permute-start.28 = (bf16[4,1,72,224]{3,2,1,0:T(8,128)(2,1)S(1)}, bf16[4,1,72,224]{3,2,1,0:T(8,128)(2,1)S(1)}, u32[]{:S(2)}, u32[]{:S(2)}) collective-permute-start(bf16[4,1,72,224]{3,2,1,0:T(8,128)(2,1)S(1)} %get-tuple-element.41), channel_id=1, source_target_pairs={{0,1},{1,0},{2,3},{3,2},{4,5},{5,4},{6,7},{7,6},{8,9},{9,8},{10,11... | collective-permute-start | bytes 387080 | tf_op jit(solution)/shard_map/ppermute | solution.py:372
  91.4 12.3 %collective-permute-start.17 = (bf16[4,2,36,224]{3,2,1,0:T(8,128)(2,1)S(1)}, bf16[4,2,36,224]{3,2,1,0:T(8,128)(2,1)S(1)}, u32[]{:S(2)}, u32[]{:S(2)}) collective-permute-start(bf16[4,2,36,224]{3,2,1,0:T(8,128)(2,1)S(1)} %get-tuple-element.33), channel_id=1, source_target_pairs={{0,16},{16,0},{1,17},{17,1},{2,18},{18,2},{3,19},{19,3},{4,20},{20... | collective-permute-start | bytes 387080 | tf_op jit(solution)/shard_map/ppermute | solution.py:444
  93.1 7.2 %collective-permute-start.26 = (bf16[4,1,36,224]{3,2,1,0:T(8,128)(2,1)S(1)}, bf16[4,1,36,224]{3,2,1,0:T(8,128)(2,1)S(1)}, u32[]{:S(2)}, u32[]{:S(2)}) collective-permute-start(bf16[4,1,36,224]{3,2,1,0:T(8,128)(2,1)S(1)} %get-tuple-element.39), channel_id=1, source_target_pairs={{0,16},{16,0},{1,17},{17,1},{2,18},{18,2},{3,19},{19,3},{4,20},{20... | collective-permute-start | bytes 193544 | tf_op jit(solution)/shard_map/ppermute | solution.py:444
  93.7 7.4 %collective-permute-start.29 = (bf16[4,1,36,224]{3,2,1,0:T(8,128)(2,1)S(1)}, bf16[4,1,36,224]{3,2,1,0:T(8,128)(2,1)S(1)}, u32[]{:S(2)}, u32[]{:S(2)}) collective-permute-start(bf16[4,1,36,224]{3,2,1,0:T(8,128)(2,1)S(1)} %get-tuple-element.43), channel_id=1, source_target_pairs={{0,16},{16,0},{1,17},{17,1},{2,18},{18,2},{3,19},{19,3},{4,20},{20... | collective-permute-start | bytes 193544 | tf_op jit(solution)/shard_map/ppermute | solution.py:444
  100.3 7.9 %collective-permute-start.27 = (bf16[4,36,224]{2,1,0:T(8,128)(2,1)S(1)}, bf16[4,36,224]{2,1,0:T(8,128)(2,1)S(1)}, u32[]{:S(2)}, u32[]{:S(2)}) collective-permute-start(bf16[4,36,224]{2,1,0:T(8,128)(2,1)S(1)} %join.4), channel_id=1, source_target_pairs={{0,8},{1,9},{2,10},{3,11},{4,12},{5,13},{6,14},{7,15},{8,0},{9,1},... | collective-permute-start | bytes 193544 | tf_op jit(solution)/shard_map/ppermute | solution.py:372
  101.2 7.0 %collective-permute-start.30 = (bf16[4,36,224]{2,1,0:T(8,128)(2,1)S(1)}, bf16[4,36,224]{2,1,0:T(8,128)(2,1)S(1)}, u32[]{:S(2)}, u32[]{:S(2)}) collective-permute-start(bf16[4,36,224]{2,1,0:T(8,128)(2,1)S(1)} %join.5), channel_id=1, source_target_pairs={{0,12},{1,13},{2,14},{3,15},{4,8},{5,9},{6,10},{7,11},{8,4},{9,5},... | collective-permute-start | bytes 193544 | tf_op jit(solution)/shard_map/ppermute | solution.py:372
  103.8 5.7 %collective-permute-start.18 = (bf16[4,36,224]{2,1,0:T(8,128)(2,1)S(1)}, bf16[4,36,224]{2,1,0:T(8,128)(2,1)S(1)}, u32[]{:S(2)}, u32[]{:S(2)}) collective-permute-start(bf16[4,36,224]{2,1,0:T(8,128)(2,1)S(1)} %get-tuple-element.35), channel_id=1, source_target_pairs={{0,4},{1,5},{2,6},{3,7},{4,0},{5,1},{6,2},{7,3},{8,12},{9,13},{10,... | collective-permute-start | bytes 193544 | tf_op jit(solution)/shard_map/ppermute | solution.py:372
